TPU v7x, 256 devices: a whole 4x4x8 slice. The times are simulated.
256 devices in a mesh: krow: 32 (over x, z_lo, y), col: 8 (over z_hi, core).
Axes of the slice: x: 4, y: 4, z: 8 (z_hi: 4, z_lo: 2; z = z_hi * 2 + z_lo), core: 2. Of those that a mesh axis runs over, the one named last changes fastest.
Arguments:
- features: bfloat16 [16384, 6144], P('krow', 'col'), may hold values from -9 to 9
- slab: bfloat16 [16384, 2048], P('krow', 'col'), may hold values from -9 to 9
- pack_order: int32 [32, 512], P('krow'), may hold values from 0 to 511, each once within a row
- place_order: int32 [32, 512], P('krow'), may hold values from 0 to 511, each once within a row
- start: int32 [1], replicated, may hold values from 512 to 2048
Outputs:
- factored: float32 [16384, 1024], P(('krow', 'col'))
Inputs may be any that keep to these rules, and one draw needn't show every extreme that they name: Row k of krow device s's sending order is its local row pack_order[s, k]. `place_order`: each krow device's elimination rows are a rearrangement of the rows it receives. Slab columns from start[0] on are not yet computed and are ignored.
All inputs are finite; a program needn't handle non-finite values.
Results may differ from a plain program's by a relative error of at most 0.0003.
Values may be sent and summed in bfloat16 or wider, within the bound.
No kernel may reach another device: no remote copies, remote signals or barrier semaphores. Data moves between devices by JAX's collectives and lax.ppermute only.
A program may use at most 64 MiB of HBM per device.

v0:
```python
import jax
import jax.numpy as jnp
from jax import lax
from jax.sharding import PartitionSpec as P

F = 6144
PW = 512


RIDGE = 0.5


def spread(value, axis, source):
    kept = jnp.where(lax.axis_index(axis) == source, value, 0).astype(value.dtype)
    return lax.psum(kept, axis)


def in_one_piece(arrays, axis, dim, along):
    ends, at = ([], 0)
    for a in arrays[:-1]:
        at += a.shape[along]
        ends.append(at)
    both = jnp.concatenate(arrays, axis=along)
    return tuple(
        jnp.split(lax.psum_scatter(both, axis, scatter_dimension=dim, tiled=True), ends, axis=along)
    )


def from_everyone(value, axis):
    copies = jnp.broadcast_to(value, (lax.axis_size(axis), *value.shape))
    return lax.all_to_all(copies, axis, split_axis=0, concat_axis=0, tiled=True)


def laid_out(tiles, dim):
    shape = list(tiles.shape[1:])
    shape[dim] *= tiles.shape[0]
    return jnp.moveaxis(tiles, 0, dim).reshape(shape)


def collect(value, axis, dim):
    tiles = from_everyone(value, axis)
    return laid_out(tiles, dim)


def shards(features, slab, pack_order, place_order, start):
    rows_dev = features.shape[0]
    prior_dev = slab.shape[1]
    column_ranks = lax.axis_size("col")
    krow_index = lax.axis_index("krow")
    col_index = lax.axis_index("col")
    packed = jnp.take(features, pack_order[0], axis=0)
    arrived = lax.all_to_all(packed, "krow", split_axis=0, concat_axis=0, tiled=True)
    ordered = jnp.take(arrived, place_order[0], axis=0)
    own_norms = jnp.sum(jnp.square(ordered.astype(jnp.float32)), axis=1)
    positions = krow_index * rows_dev + jnp.arange(rows_dev)
    kept = (col_index * prior_dev + jnp.arange(prior_dev) < start[0])[None, :]
    identity = jnp.eye(PW, dtype=jnp.float32)
    highest = lax.Precision.HIGHEST
    earlier = None
    pieces = []
    for panel in range(2):
        lower = panel * PW
        root = lower // rows_dev
        is_root = krow_index == root
        panel_feats, panel_slab = (spread(ordered, "krow", root), spread(slab, "krow", root))
        panel_slab = jnp.where(kept, panel_slab, jnp.zeros((), jnp.bfloat16))
        panel_norms = jnp.sum(jnp.square(panel_feats.astype(jnp.float32)), axis=1)
        gram = jnp.dot(ordered, panel_feats.T, preferred_element_type=jnp.float32)
        dist_part = own_norms[:, None] + panel_norms[None, :] - 2.0 * gram
        update_part = jnp.dot(slab, panel_slab.T, preferred_element_type=jnp.float32)
        dist, update = in_one_piece((dist_part, update_part), "col", 1, 0)
        width = dist.shape[1]
        targets = lower + col_index * width + jnp.arange(width)
        shift = (positions[:, None] == targets[None, :]).astype(jnp.float32)
        share = jnp.exp(-dist / (2.0 * F)) + RIDGE * shift - update
        matrix = collect(share, "col", 1)
        if panel == 0:
            block = matrix
            factor = spread(jnp.linalg.cholesky(jnp.where(is_root, block, identity)), "krow", root)
        else:
            block = matrix
            block = block - jnp.dot(earlier, earlier.T, precision=highest)
            local_factor = jnp.linalg.cholesky(jnp.where(is_root, block, identity))
            factor, remote = (spread(local_factor, "krow", root), spread(earlier, "krow", root))
            matrix = matrix - jnp.dot(earlier, remote.T, precision=highest)
        solved = jax.scipy.linalg.solve_triangular(factor, matrix.T, lower=True).T
        solved = jnp.where((positions >= lower)[:, None], solved, jnp.zeros((), jnp.float32))
        earlier = solved
        pieces.append(solved)
    whole = jnp.concatenate(pieces, axis=1)
    part_rows = rows_dev // column_ranks
    return lax.dynamic_slice_in_dim(whole, col_index * part_rows, part_rows, 0)


def solution(mesh):
    in_specs = (P("krow", "col"), P("krow", "col"), P("krow", None), P("krow", None), P())
    out_specs = P(("krow", "col"), None)
    return jax.shard_map(shards, mesh=mesh, in_specs=in_specs, out_specs=out_specs, check_vma=False)
```

profile of v0, /device:TPU:2, one launch (start us, length us, event | category | flops | bytes accessed | tf_op | source)
XLA Modules:
  0.0 1435.3 jit_solution(6125507964438926998)
XLA Ops:
  8.0 2.0 gather_fusion
  11.1 9.0 all-to-all-start
  21.0 11.6 all-to-all-done
  32.6 2.0 gather_fusion.1
  37.2 309.6 %all-reduce.11.cloned.1.call-done = (bf16[512,256]{1,0:T(8,128)(2,1)}, bf16[512,768]{1,0:T(8,128)(2,1)}, bf16[512,256]{1,0:T(8,128)(2,1)}, bf16[512,768]{1,0:T(8,128)(2,1)}) async-done(((bf16[512,256]{1,0:T(8,128)(2,1)}, bf16[512,768]{1,0:T(8,128)(2,1)}, bf16[512,256]{1,0:T(8,128)(2,1)}, bf16[512,768]{1,0:T(8,128)(2,1)}), (bf16[512,256]{1,0:T(8,128)(2,1)}, bf16[512,768]{1,0:T(8,128)(2,1)}, ...) | async-done | bytes 2097168 | tf_op jit(solution)/shard_map/psum | solution.py:15
  346.7 1.4 multiply_reduce_fusion.1
  348.2 1.8 fusion.1
  350.5 1.9 copy.62
  354.9 1.8 copy.64
  356.8 47.5 %reduce-scatter.7.cloned.1.call-done = f32[64,1024]{1,0:T(8,128)} async-done(((f32[512,1024]{1,0:T(8,128)}), f32[64,1024]{1,0:T(8,128)}) %reduce-scatter.7.cloned.1.call-update) | async-done | bytes 262160
  405.5 45.2 %reduce-scatter.9.cloned.1.call-done = f32[64,1024]{1,0:T(8,128)} async-done(((f32[512,1024]{1,0:T(8,128)}), f32[64,1024]{1,0:T(8,128)}) %reduce-scatter.9.cloned.1.call-update) | async-done | bytes 262160
  453.4 3.6 all-to-all-start.1
  457.2 29.4 %all-to-all-done.1 = f32[8,512,64]{1,2,0:T(8,128)S(1)} async-done(((f32[8,512,64]{1,2,0:T(8,128)}), f32[8,512,64]{1,2,0:T(8,128)S(1)}, u32[]{:S(2)}, u32[]{:S(2)}) %all-to-all-start.1) | async-done | bytes 1048608 | tf_op jit(solution)/shard_map/all_to_all | solution.py:31
  489.4 11.7 cholesky.286
  501.7 9.8 custom-call.27
  512.9 11.7 cholesky.305
  527.0 11.0 custom-call.28
  540.3 1.5 convolution_subtract_fusion.11
  541.8 11.7 cholesky.326
  553.7 9.8 custom-call.29
  565.1 11.8 cholesky.343
  584.7 4.2 all-to-all-start.2
  589.0 301.2 %all-reduce.7.cloned.1.call-done = f32[512,512]{0,1:T(8,128)} async-done(((f32[512,512]{0,1:T(8,128)}), f32[512,512]{0,1:T(8,128)}) %all-reduce.7.cloned.1.call-update) | async-done | bytes 1048592 | tf_op jit(solution)/shard_map/psum | solution.py:15
  891.6 8.3 while.4
  900.6 40.2 %custom-call.30 = f32[4,128,128]{1,2,0:T(8,128)S(1)} custom-call(f32[4,128,128]{2,1,0:T(8,128)} %copy-done.12), custom_call_target="InvertDiagBlocksLowerTriangular" | custom-call | tf_op jit(solution)/shard_map/jit(_solve_triangular)/triangular_solve | solution.py:86
  946.6 1.6 convolution_subtract_fusion.7
  948.2 1.4 fusion.61
  949.7 3.3 convert_select_fusion
  954.3 1.4 fusion.4
  956.8 11.7 cholesky.358
  968.7 9.8 custom-call.31
  979.7 1.5 convolution_subtract_fusion.8
  981.2 11.7 cholesky.377
  994.3 9.8 custom-call.32
  1005.6 11.7 cholesky.398
  1018.1 10.2 custom-call.33
  1029.7 11.7 cholesky.415
  1044.7 1.5 fusion.8
  1047.5 317.1 %all-reduce.9.cloned.1.call-done = (f32[512,512]{1,0:T(8,128)}, f32[512,512]{1,0:T(8,128)}) async-done(((f32[512,512]{1,0:T(8,128)}, f32[512,512]{1,0:T(8,128)}), (f32[512,512]{1,0:T(8,128)}, f32[512,512]{1,0:T(8,128)})) %all-reduce.9.cloned.1.call-update) | async-done | bytes 2097168 | tf_op jit(solution)/shard_map/psum | solution.py:15
  1364.6 2.4 fusion.7
  1367.0 11.5 while.5
  1367.6 2.3 bitcast_dynamic-update-slice_fusion.5
  1370.5 2.3 bitcast_dynamic-update-slice_fusion.5
  1373.4 2.3 bitcast_dynamic-update-slice_fusion.5
  1376.3 2.2 bitcast_dynamic-update-slice_fusion.5
  1378.5 39.5 %custom-call.34 = f32[4,128,128]{1,2,0:T(8,128)S(1)} custom-call(f32[4,128,128]{2,1,0:T(8,128)S(1)} %get-tuple-element.23), custom_call_target="InvertDiagBlocksLowerTriangular" | custom-call | tf_op jit(solution)/shard_map/jit(_solve_triangular)/triangular_solve | solution.py:86
  1418.0 3.2 fusion
  1425.1 1.6 convolution_subtract_fusion.6
  (179 shorter events, 63.5 us)
Async XLA Ops:
  6.5 1.5 copy-start
  10.0 10.1 copy-start.16
  10.0 10.1 copy-start.7
  11.1 21.6 %all-to-all-start = ((bf16[32,16,768]{2,1,0:T(8,128)(2,1)}), bf16[32,16,768]{2,1,0:T(8,128)(2,1)S(1)}, u32[]{:S(2)}, u32[]{:S(2)}) async-start(bf16[32,16,768]{2,1,0:T(8,128)(2,1)} %bitcast.2), calls=%async_computation | async-start | bytes 1572864 | tf_op jit(solution)/shard_map/all_to_all | solution.py:52
  20.1 326.7 %all-reduce.11.cloned.1.call-start = ((), (), s32[]{:S(2)}) async-start(), calls=%async_computation.9 | async-start | bytes 4194304 | tf_op jit(solution)/shard_map/psum | solution.py:15
  34.7 313.5 %copy-start.1 = (bf16[512,768]{1,0:T(8,128)(2,1)}, bf16[512,768]{1,0:T(8,128)(2,1)S(1)}, u32[]{:S(2)}) copy-start(bf16[512,768]{1,0:T(8,128)(2,1)S(1)} %gather_fusion.1) | copy-start | bytes 2359300
  36.1 368.2 %reduce-scatter.7.cloned.1.call-start = ((), (), s32[]{:S(2)}) async-start(), calls=%async_computation.6 | async-start | bytes 2359296
  346.7 3.2 copy-start.15
  352.3 1.1 copy-start.9
  352.3 1.4 copy-start.14
  352.3 1.7 copy-start.2
  352.4 98.3 %reduce-scatter.9.cloned.1.call-start = ((), (), s32[]{:S(2)}) async-start(), calls=%async_computation.7 | async-start | bytes 2359296
  453.4 33.2 %all-to-all-start.1 = ((f32[8,512,64]{1,2,0:T(8,128)}), f32[8,512,64]{1,2,0:T(8,128)S(1)}, u32[]{:S(2)}, u32[]{:S(2)}) async-start(f32[8,512,64]{1,2,0:T(8,128)} %broadcast_in_dim.77), calls=%async_computation.1 | async-start | bytes 2097152 | tf_op jit(solution)/shard_map/all_to_all | solution.py:31
  457.0 433.2 %all-reduce.7.cloned.1.call-start = ((), (), s32[]{:S(2)}) async-start(), calls=%async_computation.5 | async-start | bytes 2097152 | tf_op jit(solution)/shard_map/psum | solution.py:15
  489.4 37.6 %copy-start.6 = (f32[512,512]{1,0:T(8,128)}, f32[512,512]{1,0:T(8,128)S(1)}, u32[]{:S(2)}) copy-start(f32[512,512]{1,0:T(8,128)S(1)} %fusion.5) | copy-start | bytes 3145732
  501.1 0.6 copy-start.13
  512.2 0.7 copy-start.10
  584.7 364.9 %all-to-all-start.2 = ((f32[8,512,64]{1,2,0:T(8,128)}), f32[8,512,64]{1,2,0:T(8,128)}, u32[]{:S(2)}, u32[]{:S(2)}) async-start(f32[8,512,64]{1,2,0:T(8,128)} %broadcast_in_dim.80), calls=%async_computation.2 | async-start | bytes 2097152 | tf_op jit(solution)/shard_map/all_to_all | solution.py:31
  589.0 775.6 %all-reduce.9.cloned.1.call-start = ((), (), s32[]{:S(2)}) async-start(), calls=%async_computation.8 | async-start | bytes 4194304 | tf_op jit(solution)/shard_map/psum | solution.py:15
  899.9 0.7 copy-start.12
  900.6 41.4 %copy-start.4 = (f32[512,512]{0,1:T(8,128)}, f32[512,512]{0,1:T(8,128)S(1)}, u32[]{:S(2)}) copy-start(f32[512,512]{0,1:T(8,128)S(1)} %get-tuple-element.205) | copy-start | bytes 3145732
  940.7 0.7 copy-start.11
  955.7 1.0 copy-start.5
  1364.6 53.4 %copy-start.8 = (f32[512,512]{1,0:T(8,128)S(1)}, f32[512,512]{1,0:T(8,128)}, u32[]{:S(2)}) copy-start(f32[512,512]{1,0:T(8,128)} %get-tuple-element.48) | copy-start | bytes 3145732
  1426.6 1.2 copy-start.3
Sparse Core Ops, SparseCore 0:
  36.2 310.4 all-reduce.10
  352.5 51.7 reduce-scatter.6
  406.8 43.8 reduce-scatter.8
  583.6 306.5 all-reduce.6
  1046.4 318.1 all-reduce.8
where the time goes:
time: 1450 us; the launch traced here: 1440 us
  waiting for transfers between devices  1060 us (73%)
  other arithmetic  259 us (18%)
  local copies, waits for them, and re-layouts  43.7 us (3%)
  matrix products  33.9 us (2%)
  between operations  20 us (1%)
  starting transfers between devices  17.2 us (1%)
    psum x3, waiting for transfers between devices, spread(): return lax.psum(kept, axis)  928 us
    unnamed x7, waiting for transfers between devices  92.8 us
    another operation x5, other arithmetic, shards(): solved = jax.scipy.linalg.solve_triangular(factor, matrix.T, lower=True).T  83.4 us
    another operation x15, other arithmetic, shards(): jnp.linalg.cholesky(jnp.where(is_root, block, identity))  81 us
    another operation x15, other arithmetic, shards(): local_factor = jnp.linalg.cholesky(jnp.where(is_root, block, identity))  79.5 us
    all_to_all x2, waiting for transfers between devices, from_everyone(): return lax.all_to_all(copies, axis, split_axis=0, concat_axis=0, tiled=True)  29.4 us
  transfers between devices with their start and end apart: 8, of which 7 were waited for; matrix products, arithmetic and copies ran while one was open for 5% of the time, Pallas kernels for 0%

commit v1 on v0

v1 whole, which is shorter than its diff:
```python
import jax
import jax.numpy as jnp
from jax import lax
from jax.sharding import PartitionSpec as P

F = 6144
PW = 512
TOP = 2 * PW
BK = 128
RIDGE = 0.5


def swap(value, axis):
    return lax.all_to_all(value, axis, split_axis=0, concat_axis=0, tiled=True)


def from_everyone(value, axis):
    return swap(jnp.broadcast_to(value, (lax.axis_size(axis), *value.shape)), axis)


def sq_norms(rows):
    return jnp.sum(jnp.square(rows.astype(jnp.float32)), axis=1)


def inner(a, b):
    return lax.dot_general(a, b, (((1,), (1,)), ((), ())), preferred_element_type=jnp.float32)


def fold(upper, lower, pair):
    blocks = []
    for slot in range(9):
        hi = upper[:, slot * BK:(slot + 1) * BK] if slot < 8 else None
        at = 8 - slot
        lo = lower[:, at * BK:(at + 1) * BK] if slot > 4 else None
        if lo is None:
            blocks.append(hi)
        elif hi is None:
            blocks.append(lo)
        else:
            blocks.append(jnp.where(slot + pair <= 7, hi, lo))
    return jnp.concatenate(blocks, axis=1)


def unfold(folded):
    rows = []
    for r in range(8):
        if r >= 4:
            b = 7 - r
            part = folded[b * BK:(b + 1) * BK, :(r + 1) * BK]
        else:
            part = jnp.concatenate(
                [folded[r * BK:(r + 1) * BK, (8 - j) * BK:(9 - j) * BK] for j in range(r + 1)], axis=1)
        rows.append(jnp.pad(part, ((0, 0), (0, TOP - part.shape[1]))))
    return jnp.concatenate(rows, axis=0)


def factor_and_solve(folded, matrix):
    top = unfold(folded)
    factor = lax.linalg.cholesky(top, symmetrize_input=False)
    return jax.scipy.linalg.solve_triangular(factor, matrix.T, lower=True).T


def shards(features, slab, pack_order, place_order, start):
    n_krow, n_col = lax.axis_size("krow"), lax.axis_size("col")
    rows_dev = features.shape[0]
    group = rows_dev // n_krow
    prior_dev = slab.shape[1]
    krow, col = lax.axis_index("krow"), lax.axis_index("col")

    kept = (col * prior_dev + jnp.arange(prior_dev) < start[0])[None, :]
    slab_part = swap(slab, "krow")[:2 * group]
    places = from_everyone(place_order, "krow")[:2, 0]
    packed = jnp.take(features, pack_order[0], axis=0)
    top_arrived = from_everyone(packed[:2 * group], "krow")
    top_slab = from_everyone(slab_part, "krow")
    arrived = swap(packed, "krow")

    def by_panel(tiles):
        width = tiles.shape[-1]
        tiles = tiles.reshape(n_krow, 2, group, width)
        return jnp.moveaxis(tiles, 1, 0).reshape(TOP, width)

    top_feats = by_panel(top_arrived)
    wanted = (places + jnp.arange(2)[:, None] * rows_dev).reshape(TOP)
    top_feats = jnp.take(top_feats, wanted, axis=0)
    top_slab = jnp.where(kept, by_panel(top_slab), jnp.zeros((), jnp.bfloat16))
    top_norms = sq_norms(top_feats)

    share = PW // n_krow
    at = krow * share
    pair = at // BK
    row_lo = at
    row_hi = (7 - pair) * BK + (at - pair * BK)

    def rows_of(array, first):
        return lax.dynamic_slice_in_dim(array, first, share, 0)

    def both(array):
        return jnp.concatenate([rows_of(array, row_hi), rows_of(array, row_lo)], axis=0)

    gram = inner(both(top_feats), top_feats)
    dist = both(top_norms)[:, None] + top_norms[None, :] - 2.0 * gram
    update = inner(both(top_slab), top_slab)
    dist = fold(dist[:share], dist[share:], pair)
    update = fold(update[:share], update[share:], pair)
    parts = jnp.concatenate([dist, update], axis=1)
    summed = jnp.sum(swap(parts, "col").reshape(n_col, share // n_col, 2 * 9 * BK), axis=0)
    dist, update = summed[:, :9 * BK], summed[:, 9 * BK:]
    mine = share // n_col
    col_ids = jnp.arange(TOP)[None, :]
    ids = jnp.arange(mine)[:, None] + col * mine
    shift = fold((row_hi + ids == col_ids).astype(jnp.float32),
                 (row_lo + ids == col_ids).astype(jnp.float32), pair)
    entries = jnp.exp(-dist / (2.0 * F)) + RIDGE * shift - update
    entries = from_everyone(entries, "col").reshape(share, 9 * BK)
    folded = from_everyone(entries, "krow").reshape(PW, 9 * BK)

    ordered = jnp.take(arrived, place_order[0], axis=0)
    dist = sq_norms(ordered)[:, None] + top_norms[None, :] - 2.0 * inner(ordered, top_feats)
    update = inner(slab, top_slab)
    parts = lax.psum_scatter(jnp.concatenate([dist, update], axis=1), "col", scatter_dimension=0, tiled=True)
    dist, update = parts[:, :TOP], parts[:, TOP:]
    own = rows_dev // n_col
    positions = krow * rows_dev + col * own + jnp.arange(own)
    shift = (positions[:, None] == col_ids).astype(jnp.float32)
    matrix = jnp.exp(-dist / (2.0 * F)) + RIDGE * shift - update

    solved = factor_and_solve(folded, matrix)
    return jnp.where((positions[:, None] >= PW) | (col_ids < PW), solved, 0.0)


def solution(mesh):
    in_specs = (P("krow", "col"), P("krow", "col"), P("krow", None), P("krow", None), P())
    out_specs = P(("krow", "col"), None)
    return jax.shard_map(shards, mesh=mesh, in_specs=in_specs, out_specs=out_specs, check_vma=False)
```

time: 1450 us -> 531 us (0.37)
  waiting for transfers between devices: 1060 us -> 82.7 us
  starting transfers between devices: 17.2 us -> 44.5 us
    psum x3 -> x0, waiting for transfers between devices: 928 us -> none  [spread(): return lax.psum(kept, axis)]
    unnamed x7 -> x1, waiting for transfers between devices: 92.8 us -> 0.02 us
    all_to_all x3 -> x7, waiting for transfers between devices: 41 us -> 82.6 us  [swap(): return lax.all_to_all(value, axis, split_axis=0, concat_axis=0, tiled=True)]
    all_to_all x3 -> x7, starting transfers between devices: 16.8 us -> 44.4 us  [swap(): return lax.all_to_all(value, axis, split_axis=0, concat_axis=0, tiled=True)]
    another operation x35 -> x34, other arithmetic: 244 us -> 258 us  [the longest x31 173 us: factor_and_solve(): factor = lax.linalg.cholesky(top, symmetrize_input=False)]
    another operation x26 -> x29, matrix products: 24.4 us -> 32.7 us  [the longest x14 21.6 us: factor_and_solve(): factor = lax.linalg.cholesky(top, symmetrize_input=False)]
    another operation x58 -> x32, local copies, waits for them, and re-layouts: 23.4 us -> 30.1 us  [the longest x41 20.3 us: shards(): solved = jax.scipy.linalg.solve_triangular(factor, matrix.T, lower=True).T]
  transfers between devices with their start and end apart: 8 -> 8, of which waited for: 7 -> 7; matrix products, arithmetic and copies ran while one was open for 5% -> 64% of each run, Pallas kernels for 0% -> 0%
where the time goes in v1:
time: 531 us; the launch traced here: 523 us
  other arithmetic  268 us (50%)
  waiting for transfers between devices  82.7 us (16%)
  local copies, waits for them, and re-layouts  58.1 us (11%)
  starting transfers between devices  44.5 us (8%)
  matrix products  38.6 us (7%)
  between operations  20.2 us (4%)
  blocking collectives  10.9 us (2%)
    another operation x31, other arithmetic, factor_and_solve(): factor = lax.linalg.cholesky(top, symmetrize_input=False)  173 us
    another operation x3, other arithmetic, factor_and_solve(): return jax.scipy.linalg.solve_triangular(factor, matrix.T, lower=True).T  84.5 us
    all_to_all x7, waiting for transfers between devices, swap(): return lax.all_to_all(value, axis, split_axis=0, concat_axis=0, tiled=True)  82.6 us
    all_to_all x7, starting transfers between devices, swap(): return lax.all_to_all(value, axis, split_axis=0, concat_axis=0, tiled=True)  44.4 us
    another operation x24, local copies, waits for them, and re-layouts  27.4 us
    another operation x14, matrix products, factor_and_solve(): factor = lax.linalg.cholesky(top, symmetrize_input=False)  21.6 us
    another operation x15, matrix products, factor_and_solve(): return jax.scipy.linalg.solve_triangular(factor, matrix.T, lower=True).T  11.1 us
    all_to_all x1, blocking collectives, swap(): return lax.all_to_all(value, axis, split_axis=0, concat_axis=0, tiled=True)  10.9 us
  transfers between devices with their start and end apart: 8, of which 7 were waited for; matrix products, arithmetic and copies ran while one was open for 64% of the time, Pallas kernels for 0%

profile of v1, /device:TPU:2, one launch (start us, length us, event | category | flops | bytes accessed | tf_op | source)
XLA Modules:
  0.0 522.7 jit_solution(8429848087670894854)
XLA Ops:
  6.5 9.1 %all-to-all-start.2 = ((bf16[32,16,256]{2,1,0:T(8,128)(2,1)}), bf16[32,16,256]{2,1,0:T(8,128)(2,1)S(1)}, u32[]{:S(2)}, u32[]{:S(2)}) async-start(bf16[32,16,256]{2,1,0:T(8,128)(2,1)} %bitcast.142), calls=%async_computation.2 | async-start | bytes 524288 | tf_op jit(solution)/shard_map/all_to_all | solution.py:14
  15.7 8.0 %all-to-all-done.2 = bf16[32,16,256]{2,1,0:T(8,128)(2,1)S(1)} async-done(((bf16[32,16,256]{2,1,0:T(8,128)(2,1)}), bf16[32,16,256]{2,1,0:T(8,128)(2,1)S(1)}, u32[]{:S(2)}, u32[]{:S(2)}) %all-to-all-start.2) | async-done | bytes 262176 | tf_op jit(solution)/shard_map/all_to_all | solution.py:14
  25.0 5.0 all-to-all-start
  30.0 7.3 %all-to-all-done = s32[32,1,512]{2,1,0:T(1,128)S(1)} async-done(((s32[32,1,512]{2,1,0:T(1,128)}), s32[32,1,512]{2,1,0:T(1,128)S(1)}, u32[]{:S(2)}, u32[]{:S(2)}) %all-to-all-start) | async-done | bytes 65568 | tf_op jit(solution)/shard_map/all_to_all | solution.py:14
  38.2 5.0 all-to-all-start.3
  46.8 5.3 %all-to-all-done.3 = bf16[32,32,256]{2,1,0:T(8,128)(2,1)S(1)} async-done(((bf16[32,32,256]{2,1,0:T(8,128)(2,1)}), bf16[32,32,256]{2,1,0:T(8,128)(2,1)S(1)}, u32[]{:S(2)}, u32[]{:S(2)}) %all-to-all-start.3) | async-done | bytes 524320 | tf_op jit(solution)/shard_map/all_to_all | solution.py:14
  53.4 5.3 %all-to-all-start.1 = ((bf16[32,32,768]{2,1,0:T(8,128)(2,1)}), bf16[32,32,768]{2,1,0:T(8,128)(2,1)S(1)}, u32[]{:S(2)}, u32[]{:S(2)}) async-start(bf16[32,32,768]{2,1,0:T(8,128)(2,1)} %broadcast_in_dim.61), calls=%async_computation.1 | async-start | bytes 3145728 | tf_op jit(solution)/shard_map/all_to_all | solution.py:14
  61.9 14.4 %all-to-all-done.1 = bf16[32,32,768]{2,1,0:T(8,128)(2,1)S(1)} async-done(((bf16[32,32,768]{2,1,0:T(8,128)(2,1)}), bf16[32,32,768]{2,1,0:T(8,128)(2,1)S(1)}, u32[]{:S(2)}, u32[]{:S(2)}) %all-to-all-start.1) | async-done | bytes 1572896 | tf_op jit(solution)/shard_map/all_to_all | solution.py:14
  79.0 5.2 %gather_fusion = bf16[1024,768]{1,0:T(8,128)(2,1)} fusion(bf16[1024,768]{1,0:T(8,128)(2,1)S(1)} %bitcast.137, s32[1024]{0:T(1024)S(1)} %get-tuple-element.119), kind=kCustom, calls=%fused_computation.2 | custom fusion | bytes 3149824 | tf_op jit(solution)/shard_map/jit(_take)/gather | solution.py:85
  88.4 7.6 %all-to-all-start.4 = ((f32[8,2,2304]{2,1,0:T(2,128)}), f32[8,2,2304]{2,1,0:T(2,128)S(1)}, u32[]{:S(2)}, u32[]{:S(2)}) async-start(f32[8,2,2304]{2,1,0:T(2,128)} %all_to_all.40), calls=%async_computation.4 | async-start | bytes 294912 | tf_op jit(solution)/shard_map/all_to_all | solution.py:14
  96.0 9.9 %all-to-all-done.4 = f32[8,2,2304]{2,1,0:T(2,128)S(1)} async-done(((f32[8,2,2304]{2,1,0:T(2,128)}), f32[8,2,2304]{2,1,0:T(2,128)S(1)}, u32[]{:S(2)}, u32[]{:S(2)}) %all-to-all-start.4) | async-done | bytes 147488 | tf_op jit(solution)/shard_map/all_to_all | solution.py:14
  106.1 10.9 %all_to_all.55 = f32[8,2,1152]{2,1,0:T(2,128)S(1)} all-to-all(f32[8,2,1152]{2,1,0:T(2,128)S(1)} %broadcast_in_dim.66), channel_id=1, replica_groups=mesh['krow'=32,'col'=8] {'col'}, dimensions={0} | all-to-all | bytes 147456 | tf_op jit(solution)/shard_map/all_to_all | solution.py:14
  116.9 6.4 %all-to-all-start.7 = ((bf16[32,16,768]{2,1,0:T(8,128)(2,1)}), bf16[32,16,768]{2,1,0:T(8,128)(2,1)S(1)}, u32[]{:S(2)}, u32[]{:S(2)}) async-start(bf16[32,16,768]{2,1,0:T(8,128)(2,1)} %bitcast.140), calls=%async_computation.7 | async-start | bytes 1572864 | tf_op jit(solution)/shard_map/all_to_all | solution.py:14
  123.4 12.2 %all-to-all-done.7 = bf16[32,16,768]{2,1,0:T(8,128)(2,1)S(1)} async-done(((bf16[32,16,768]{2,1,0:T(8,128)(2,1)}), bf16[32,16,768]{2,1,0:T(8,128)(2,1)S(1)}, u32[]{:S(2)}, u32[]{:S(2)}) %all-to-all-start.7) | async-done | bytes 786464 | tf_op jit(solution)/shard_map/all_to_all | solution.py:14
  137.3 6.0 %all-to-all-start.6 = ((f32[32,16,1152]{2,1,0:T(8,128)}), f32[32,16,1152]{2,1,0:T(8,128)}, u32[]{:S(2)}, u32[]{:S(2)}) async-start(f32[32,16,1152]{2,1,0:T(8,128)} %broadcast_in_dim.67), calls=%async_computation.6 | async-start | bytes 4718592 | tf_op jit(solution)/shard_map/all_to_all | solution.py:14
  143.5 2.8 convolution_bitcast_fusion
  146.3 3.0 gather_fusion.2
  150.8 2.3 multiply_subtract_fusion
  153.1 2.5 pad_maximum_fusion
  155.6 25.5 %all-to-all-done.6 = f32[32,16,1152]{2,1,0:T(8,128)} async-done(((f32[32,16,1152]{2,1,0:T(8,128)}), f32[32,16,1152]{2,1,0:T(8,128)}, u32[]{:S(2)}, u32[]{:S(2)}) %all-to-all-start.6) | async-done | bytes 2359328 | tf_op jit(solution)/shard_map/all_to_all | solution.py:14
  185.4 11.7 %cholesky.221 = f32[128,128]{1,0:T(8,128)S(1)} custom-call(f32[128,128]{1,0:T(8,128)S(1)} %get-tuple-element.39), custom_call_target="Cholesky" | custom-call | tf_op jit(solution)/shard_map/cholesky | solution.py:59
  197.1 2.6 cholesky.253
  199.8 9.8 %custom-call.48 = f32[1,128,128]{1,2,0:T(8,128)S(1)} custom-call(f32[1,128,128]{2,1,0:T(8,128)S(1)} %get-tuple-element.82), custom_call_target="InvertDiagBlocksLowerTriangular" | custom-call | tf_op jit(solution)/shard_map/cholesky | solution.py:59
  214.5 12.2 %cholesky.242 = f32[128,128]{1,0:T(8,128)S(1)} custom-call(f32[128,128]{1,0:T(8,128)S(1)} %cholesky.580), custom_call_target="Cholesky" | custom-call | tf_op jit(solution)/shard_map/cholesky | solution.py:59
  227.4 9.8 %custom-call.49 = f32[1,128,128]{1,2,0:T(8,128)S(1)} custom-call(f32[1,128,128]{2,1,0:T(8,128)S(1)} %get-tuple-element.79), custom_call_target="InvertDiagBlocksLowerTriangular" | custom-call | tf_op jit(solution)/shard_map/cholesky | solution.py:59
  240.6 11.7 %cholesky.465 = f32[128,128]{1,0:T(8,128)S(1)} custom-call(f32[128,128]{1,0:T(8,128)S(1)} %cholesky.585), custom_call_target="Cholesky" | custom-call | tf_op jit(solution)/shard_map/cholesky | solution.py:59
  253.0 9.8 %custom-call.50 = f32[1,128,128]{1,2,0:T(8,128)S(1)} custom-call(f32[1,128,128]{2,1,0:T(8,128)S(1)} %get-tuple-element.76), custom_call_target="InvertDiagBlocksLowerTriangular" | custom-call | tf_op jit(solution)/shard_map/cholesky | solution.py:59
  263.9 2.5 convolution_subtract_fusion.2
  266.5 11.7 %cholesky.484 = f32[128,128]{1,0:T(8,128)S(1)} custom-call(f32[128,128]{1,0:T(8,128)S(1)} %cholesky.590), custom_call_target="Cholesky" | custom-call | tf_op jit(solution)/shard_map/cholesky | solution.py:59
  278.8 9.8 %custom-call.51 = f32[1,128,128]{1,2,0:T(8,128)S(1)} custom-call(f32[1,128,128]{2,1,0:T(8,128)S(1)} %get-tuple-element.73), custom_call_target="InvertDiagBlocksLowerTriangular" | custom-call | tf_op jit(solution)/shard_map/cholesky | solution.py:59
  292.0 11.7 %cholesky.503 = f32[128,128]{1,0:T(8,128)S(1)} custom-call(f32[128,128]{1,0:T(8,128)S(1)} %cholesky.594), custom_call_target="Cholesky" | custom-call | tf_op jit(solution)/shard_map/cholesky | solution.py:59
  304.4 10.0 %custom-call.52 = f32[1,128,128]{1,2,0:T(8,128)S(1)} custom-call(f32[1,128,128]{2,1,0:T(8,128)S(1)} %get-tuple-element.70), custom_call_target="InvertDiagBlocksLowerTriangular" | custom-call | tf_op jit(solution)/shard_map/cholesky | solution.py:59
  317.7 11.7 %cholesky.523 = f32[128,128]{1,0:T(8,128)S(1)} custom-call(f32[128,128]{1,0:T(8,128)S(1)} %cholesky.598), custom_call_target="Cholesky" | custom-call | tf_op jit(solution)/shard_map/cholesky | solution.py:59
  330.0 9.8 %custom-call.53 = f32[1,128,128]{1,2,0:T(8,128)S(1)} custom-call(f32[1,128,128]{2,1,0:T(8,128)S(1)} %get-tuple-element.67), custom_call_target="InvertDiagBlocksLowerTriangular" | custom-call | tf_op jit(solution)/shard_map/cholesky | solution.py:59
  342.8 12.1 %cholesky.543 = f32[128,128]{1,0:T(8,128)S(1)} custom-call(f32[128,128]{1,0:T(8,128)S(1)} %cholesky.602), custom_call_target="Cholesky" | custom-call | tf_op jit(solution)/shard_map/cholesky | solution.py:59
  355.5 9.8 %custom-call.54 = f32[1,128,128]{1,2,0:T(8,128)S(1)} custom-call(f32[1,128,128]{2,1,0:T(8,128)S(1)} %get-tuple-element.64), custom_call_target="InvertDiagBlocksLowerTriangular" | custom-call | tf_op jit(solution)/shard_map/cholesky | solution.py:59
  368.0 11.7 %cholesky.561 = f32[128,128]{1,0:T(8,128)S(1)} custom-call(f32[128,128]{1,0:T(8,128)S(1)} %convolution_subtract_fusion.6), custom_call_target="Cholesky" | custom-call | tf_op jit(solution)/shard_map/cholesky | solution.py:59
  390.6 4.9 select_select_fusion
  395.5 27.4 %while.1 = (s32[]{:T(128)}, f32[1024,1024]{1,0:T(8,128)}, s32[8,2]{0,1:T(2,128)S(1)}, f32[8,128,128]{2,1,0:T(8,128)}, s32[]{:T(128)}) while((s32[]{:T(128)}, f32[1024,1024]{1,0:T(8,128)}, s32[8,2]{0,1:T(2,128)S(1)}, f32[8,128,128]{2,1,0:T(8,128)}, s32[]{:T(128)}) %tuple.88), condition=%wide.while_cond, body=%wide.while_body.sunk | while | flops 2 | bytes 132705 | solution.py:60
  396.1 2.8 bitcast_dynamic-update-slice_fusion.2
  399.5 2.8 bitcast_dynamic-update-slice_fusion.2
  402.9 2.8 bitcast_dynamic-update-slice_fusion.2
  406.4 2.8 bitcast_dynamic-update-slice_fusion.2
  409.8 2.9 bitcast_dynamic-update-slice_fusion.2
  413.3 2.8 bitcast_dynamic-update-slice_fusion.2
  416.7 2.8 bitcast_dynamic-update-slice_fusion.2
  420.1 2.8 bitcast_dynamic-update-slice_fusion.2
  422.9 79.6 %custom-call.55 = f32[8,128,128]{1,2,0:T(8,128)S(1)} custom-call(f32[8,128,128]{2,1,0:T(8,128)} %get-tuple-element.13), custom_call_target="InvertDiagBlocksLowerTriangular" | custom-call | tf_op jit(solution)/shard_map/jit(_solve_triangular)/triangular_solve | solution.py:60
  (168 shorter events, 73.1 us)
Async XLA Ops:
  6.5 38.1 %copy-start = (bf16[512,768]{1,0:T(8,128)(2,1)S(1)}, bf16[512,768]{1,0:T(8,128)(2,1)}, u32[]{:S(2)}) copy-start(bf16[512,768]{1,0:T(8,128)(2,1)} %param.7) | copy-start | bytes 2359300
  6.5 17.1 %all-to-all-start.2 = ((bf16[32,16,256]{2,1,0:T(8,128)(2,1)}), bf16[32,16,256]{2,1,0:T(8,128)(2,1)S(1)}, u32[]{:S(2)}, u32[]{:S(2)}) async-start(bf16[32,16,256]{2,1,0:T(8,128)(2,1)} %bitcast.142), calls=%async_computation.2 | async-start | bytes 524288 | tf_op jit(solution)/shard_map/all_to_all | solution.py:14
  25.0 12.3 %all-to-all-start = ((s32[32,1,512]{2,1,0:T(1,128)}), s32[32,1,512]{2,1,0:T(1,128)S(1)}, u32[]{:S(2)}, u32[]{:S(2)}) async-start(s32[32,1,512]{2,1,0:T(1,128)} %broadcast_in_dim.59), calls=%async_computation | async-start | bytes 131072 | tf_op jit(solution)/shard_map/all_to_all | solution.py:14
  38.2 13.9 %all-to-all-start.3 = ((bf16[32,32,256]{2,1,0:T(8,128)(2,1)}), bf16[32,32,256]{2,1,0:T(8,128)(2,1)S(1)}, u32[]{:S(2)}, u32[]{:S(2)}) async-start(bf16[32,32,256]{2,1,0:T(8,128)(2,1)} %broadcast_in_dim.64), calls=%async_computation.3 | async-start | bytes 1048576 | tf_op jit(solution)/shard_map/all_to_all | solution.py:14
  46.8 15.1 %copy-start.4 = (bf16[512,768]{1,0:T(8,128)(2,1)}, bf16[512,768]{1,0:T(8,128)(2,1)S(1)}, u32[]{:S(2)}) copy-start(bf16[512,768]{1,0:T(8,128)(2,1)S(1)} %broadcast_select_fusion.2) | copy-start | bytes 2359300
  52.1 1.3 copy-start.5
  53.4 22.9 %all-to-all-start.1 = ((bf16[32,32,768]{2,1,0:T(8,128)(2,1)}), bf16[32,32,768]{2,1,0:T(8,128)(2,1)S(1)}, u32[]{:S(2)}, u32[]{:S(2)}) async-start(bf16[32,32,768]{2,1,0:T(8,128)(2,1)} %broadcast_in_dim.61), calls=%async_computation.1 | async-start | bytes 3145728 | tf_op jit(solution)/shard_map/all_to_all | solution.py:14
  60.9 0.8 copy-start.3
  76.4 1.2 copy-start.2
  86.4 0.6 copy-start.9
  88.4 17.5 %all-to-all-start.4 = ((f32[8,2,2304]{2,1,0:T(2,128)}), f32[8,2,2304]{2,1,0:T(2,128)S(1)}, u32[]{:S(2)}, u32[]{:S(2)}) async-start(f32[8,2,2304]{2,1,0:T(2,128)} %all_to_all.40), calls=%async_computation.4 | async-start | bytes 294912 | tf_op jit(solution)/shard_map/all_to_all | solution.py:14
  116.9 18.7 %all-to-all-start.7 = ((bf16[32,16,768]{2,1,0:T(8,128)(2,1)}), bf16[32,16,768]{2,1,0:T(8,128)(2,1)S(1)}, u32[]{:S(2)}, u32[]{:S(2)}) async-start(bf16[32,16,768]{2,1,0:T(8,128)(2,1)} %bitcast.140), calls=%async_computation.7 | async-start | bytes 1572864 | tf_op jit(solution)/shard_map/all_to_all | solution.py:14
  123.3 20.1 %copy-start.6 = (bf16[512,256]{1,0:T(8,128)(2,1)S(1)}, bf16[512,256]{1,0:T(8,128)(2,1)}, u32[]{:S(2)}) copy-start(bf16[512,256]{1,0:T(8,128)(2,1)} %param.8) | copy-start | bytes 786436
  123.4 20.0 %copy-start.11 = (s32[1,512]{1,0:T(1,128)S(1)}, s32[1,512]{1,0:T(1,128)}, u32[]{:S(2)}) copy-start(s32[1,512]{1,0:T(1,128)} %param.10) | copy-start | bytes 6148
  137.3 43.9 %all-to-all-start.6 = ((f32[32,16,1152]{2,1,0:T(8,128)}), f32[32,16,1152]{2,1,0:T(8,128)}, u32[]{:S(2)}, u32[]{:S(2)}) async-start(f32[32,16,1152]{2,1,0:T(8,128)} %broadcast_in_dim.67), calls=%async_computation.6 | async-start | bytes 4718592 | tf_op jit(solution)/shard_map/all_to_all | solution.py:14
  143.3 359.2 %reduce-scatter.2.cloned.1.call-start = ((), (), s32[]{:S(2)}) async-start(), calls=%async_computation.9 | async-start | bytes 4718592 | tf_op jit(solution)/shard_map/reduce_scatter | solution.py:121
  146.3 4.5 copy-start.10
  150.8 2.3 copy-start.1
  211.9 2.3 copy-start.7
  211.9 2.6 copy-start.8
Sparse Core Ops, SparseCore 0:
  155.7 57.8 reduce-scatter.1

commit v2 on v1

--- a/solution.py
+++ b/solution.py
@@ -1,14 +1,18 @@
 import jax
 import jax.numpy as jnp
 from jax import lax
+from jax.experimental import pallas as pl
+from jax.experimental.pallas import tpu as pltpu
 from jax.sharding import PartitionSpec as P
 
 F = 6144
 PW = 512
 TOP = 2 * PW
 BK = 128
+OWN = 64
+CODE = 32
 RIDGE = 0.5
-
+HI = lax.Precision.HIGHEST
 
 def swap(value, axis):
     return lax.all_to_all(value, axis, split_axis=0, concat_axis=0, tiled=True)
@@ -41,23 +45,84 @@
     return jnp.concatenate(blocks, axis=1)
 
 
-def unfold(folded):
-    rows = []
-    for r in range(8):
-        if r >= 4:
-            b = 7 - r
-            part = folded[b * BK:(b + 1) * BK, :(r + 1) * BK]
+def dot_t(a, b):
+    return lax.dot_general(a, b, (((1,), (1,)), ((), ())), precision=HI, preferred_element_type=jnp.float32)
+
+def over_rows(v, k):
+    return jnp.broadcast_to(v[k:k + 1, :], v.shape)
+
+def over_lanes(v, c):
+    return jnp.broadcast_to(v[:, c:c + 1], v.shape)
+
+def invert_factor(tiles, w_ref):
+    n = len(tiles)
+    lane = lax.broadcasted_iota(jnp.int32, (8, BK), 1)
+    sub = lax.broadcasted_iota(jnp.int32, (8, BK), 0)
+    for g in range(n):
+        c0 = 8 * g
+        top = tiles[g]
+        cols = [over_lanes(top, c0 + k) for k in range(8)]
+        cross, inv, rows = {}, [], []
+        pivots = jnp.ones((8, BK), jnp.float32)
+        for k in range(8):
+            p = over_rows(cols[k], k)
+            r = 1.0 / p
+            row = jnp.where(lane == c0 + k, p + 1.0, over_rows(top, k))
+            m = jnp.where(sub > k, cols[k] * r, 0.0)
+            for k2 in range(k + 1, 8):
+                cross[k, k2] = over_rows(cols[k2], k)
+                cols[k2] = cols[k2] - m * cross[k, k2]
+            top = top - m * row
+            pivots = jnp.where(sub == k, p, pivots)
+            inv.append(r)
+            rows.append(row)
+        unit = jnp.where(lane < c0 + sub, top, jnp.where(lane == c0 + sub, 1.0, 0.0))
+        w_ref[c0:c0 + 8, :] = unit * lax.rsqrt(pivots)
+        for i in range(g + 1, n):
+            tile = tiles[i]
+            cols = [over_lanes(tile, c0 + k) for k in range(8)]
+            for k in range(8):
+                m = cols[k] * inv[k]
+                for k2 in range(k + 1, 8):
+                    cols[k2] = cols[k2] - m * cross[k, k2]
+                tile = tile - m * rows[k]
+            tiles[i] = tile
+
+def chol_kernel(f_ref, m_ref, o_ref, a_ref, w_ref):
+    nb = TOP // BK
+    for r in range(nb):
+        if r >= nb // 2:
+            b = nb - 1 - r
+            a_ref[r * BK:(r + 1) * BK, :(r + 1) * BK] = f_ref[b * BK:(b + 1) * BK, :(r + 1) * BK]
         else:
-            part = jnp.concatenate(
-                [folded[r * BK:(r + 1) * BK, (8 - j) * BK:(9 - j) * BK] for j in range(r + 1)], axis=1)
-        rows.append(jnp.pad(part, ((0, 0), (0, TOP - part.shape[1]))))
-    return jnp.concatenate(rows, axis=0)
-
+            for j in range(r + 1):
+                a_ref[r * BK:(r + 1) * BK, j * BK:(j + 1) * BK] = f_ref[r * BK:(r + 1) * BK, (nb - j) * BK:(nb + 1 - j) * BK]
+    a_ref[TOP:, :] = m_ref[...]
+
+    def step(j, carry):
+        o = pl.multiple_of(j * BK, BK)
+        tiles = [a_ref[pl.ds(pl.multiple_of(o + 8 * i, 8), 8), pl.ds(o, BK)] for i in range(BK // 8)]
+        invert_factor(tiles, w_ref)
+        for b in range(nb):
+            @pl.when(j == b)
+            def _():
+                lo, hi = b * BK, (b + 1) * BK
+                panel = dot_t(a_ref[hi:, lo:hi], w_ref[...])
+                o_ref[:, lo:hi] = panel[TOP - hi:, :]
+                for c in range(b + 1, nb):
+                    at = c * BK
+                    a_ref[at:, at:at + BK] -= dot_t(panel[at - hi:, :], panel[at - hi:at - hi + BK, :])
+        return carry
+    lax.fori_loop(0, nb, step, 0)
 
 def factor_and_solve(folded, matrix):
-    top = unfold(folded)
-    factor = lax.linalg.cholesky(top, symmetrize_input=False)
-    return jax.scipy.linalg.solve_triangular(factor, matrix.T, lower=True).T
+    return pl.pallas_call(
+        chol_kernel,
+        out_shape=jax.ShapeDtypeStruct(matrix.shape, jnp.float32),
+        in_specs=[pl.BlockSpec(memory_space=pltpu.VMEM)] * 2,
+        out_specs=pl.BlockSpec(memory_space=pltpu.VMEM),
+        scratch_shapes=[pltpu.VMEM((TOP + OWN, TOP), jnp.float32), pltpu.VMEM((BK, BK), jnp.float32)],
+    )(folded, matrix)
 
 
 def shards(features, slab, pack_order, place_order, start):
@@ -68,22 +133,22 @@
     krow, col = lax.axis_index("krow"), lax.axis_index("col")
 
     kept = (col * prior_dev + jnp.arange(prior_dev) < start[0])[None, :]
-    slab_part = swap(slab, "krow")[:2 * group]
-    places = from_everyone(place_order, "krow")[:2, 0]
+    order = place_order[0]
+    coded = jnp.stack([order // CODE, order % CODE], axis=1).astype(jnp.bfloat16)
+    coded = jnp.pad(coded, ((0, 0), (0, BK - 2)))
+    slab_part = swap(jnp.concatenate([slab, coded], axis=1), "krow")[:2 * group]
     packed = jnp.take(features, pack_order[0], axis=0)
-    top_arrived = from_everyone(packed[:2 * group], "krow")
-    top_slab = from_everyone(slab_part, "krow")
+    feat_dev = packed.shape[1]
+    tiles = from_everyone(jnp.concatenate([packed[:2 * group], slab_part], axis=1), "krow")
+    packed, tiles = lax.optimization_barrier((packed, tiles))
     arrived = swap(packed, "krow")
 
-    def by_panel(tiles):
-        width = tiles.shape[-1]
-        tiles = tiles.reshape(n_krow, 2, group, width)
-        return jnp.moveaxis(tiles, 1, 0).reshape(TOP, width)
-
-    top_feats = by_panel(top_arrived)
-    wanted = (places + jnp.arange(2)[:, None] * rows_dev).reshape(TOP)
-    top_feats = jnp.take(top_feats, wanted, axis=0)
-    top_slab = jnp.where(kept, by_panel(top_slab), jnp.zeros((), jnp.bfloat16))
+    tiles = tiles.reshape(n_krow, 2, group, tiles.shape[-1])
+    top = jnp.moveaxis(tiles, 1, 0).reshape(TOP, tiles.shape[-1])
+    places = top[:, feat_dev + prior_dev:feat_dev + prior_dev + 2].astype(jnp.float32).astype(jnp.int32)
+    wanted = places[:, 0] * CODE + places[:, 1] + jnp.arange(TOP) // rows_dev * rows_dev
+    top_feats = jnp.take(top[:, :feat_dev], wanted, axis=0)
+    top_slab = jnp.where(kept, top[:, feat_dev:feat_dev + prior_dev], jnp.zeros((), jnp.bfloat16))
     top_norms = sq_norms(top_feats)
 
     share = PW // n_krow
@@ -104,6 +169,7 @@
     dist = fold(dist[:share], dist[share:], pair)
     update = fold(update[:share], update[share:], pair)
     parts = jnp.concatenate([dist, update], axis=1)
+    parts, arrived = lax.optimization_barrier((parts, arrived))
     summed = jnp.sum(swap(parts, "col").reshape(n_col, share // n_col, 2 * 9 * BK), axis=0)
     dist, update = summed[:, :9 * BK], summed[:, 9 * BK:]
     mine = share // n_col

time: 531 us -> 242 us (0.46)
  other arithmetic: 268 us -> 20.6 us
  Pallas kernels: 0 us -> 45.3 us
  local copies, waits for them, and re-layouts: 58.1 us -> 17.6 us
  matrix products: 38.6 us -> 4.92 us
  starting transfers between devices: 44.5 us -> 37.8 us
  between operations: 20.2 us -> 14.5 us
    another operation x34 -> x3, other arithmetic: 258 us -> 0.79 us  [the longest x31 173 us: factor_and_solve(): factor = lax.linalg.cholesky(top, symmetrize_input=False)]
    pallas_call x0 -> x1, Pallas kernels: none -> 45.3 us  [factor_and_solve(): pl.pallas_call(chol_kernel, out_shape=jax.ShapeDtypeStruct(matrix.shape,...]
    reduce_scatter x1, waiting for transfers between devices: 0.02 us -> 39.1 us  [shards(): lax.psum_scatter(jnp.concatenate([dist, update], axis=1), 'col', scatter_...]
    all_to_all x7 -> x5, waiting for transfers between devices: 82.6 us -> 47.3 us  [swap(): return lax.all_to_all(value, axis, split_axis=0, concat_axis=0, tiled=True)]
    another operation x29 -> x0, matrix products: 32.7 us -> none  [the longest x14 21.6 us: factor_and_solve(): factor = lax.linalg.cholesky(top, symmetrize_input=False)]
    another operation x32 -> x0, local copies, waits for them, and re-layouts: 30.1 us -> none
    all_to_all x7 -> x5, starting transfers between devices: 44.4 us -> 37.7 us  [swap(): return lax.all_to_all(value, axis, split_axis=0, concat_axis=0, tiled=True)]
    slice x8 -> x3, local copies, waits for them, and re-layouts: 5.57 us -> 0.11 us  [the longest x1 0.1 us: shards(): top_feats = jnp.take(top[:, :feat_dev], wanted, axis=0)]
  transfers between devices with their start and end apart: 8 -> 6, of which waited for: 7 -> 5; matrix products, arithmetic and copies ran while one was open for 64% -> 10% of each run, Pallas kernels for 0% -> 0%
where the time goes in v2:
time: 242 us; the launch traced here: 238 us
  waiting for transfers between devices  86.5 us (36%)
  Pallas kernels  45.3 us (19%)
  starting transfers between devices  37.8 us (16%)
  other arithmetic  20.6 us (9%)
  local copies, waits for them, and re-layouts  17.6 us (7%)
  between operations  14.5 us (6%)
  blocking collectives  11.3 us (5%)
  matrix products  4.92 us (2%)
    all_to_all x5, waiting for transfers between devices, swap(): return lax.all_to_all(value, axis, split_axis=0, concat_axis=0, tiled=True)  47.3 us
    pallas_call x1, Pallas kernels, factor_and_solve(): pl.pallas_call(chol_kernel, out_shape=jax.ShapeDtypeStruct(matrix.shape,...  45.3 us
    reduce_scatter x1, waiting for transfers between devices, shards(): lax.psum_scatter(jnp.concatenate([dist, update], axis=1), 'col', scatter_...  39.1 us
    all_to_all x5, starting transfers between devices, swap(): return lax.all_to_all(value, axis, split_axis=0, concat_axis=0, tiled=True)  37.7 us
    all_to_all x1, blocking collectives, swap(): return lax.all_to_all(value, axis, split_axis=0, concat_axis=0, tiled=True)  11.3 us
    gather x1, local copies, waits for them, and re-layouts, shards(): top_feats = jnp.take(top[:, :feat_dev], wanted, axis=0)  5.22 us
    dot_general x4, matrix products, inner(): lax.dot_general(a, b, (((1,), (1,)), ((), ())), preferred_element_type=jn...  4.92 us
  transfers between devices with their start and end apart: 6, of which 5 were waited for; matrix products, arithmetic and copies ran while one was open for 10% of the time, Pallas kernels for 0%

profile of v2, /device:TPU:2, one launch (start us, length us, event | category | flops | bytes accessed | tf_op | source)
XLA Modules:
  0.0 238.4 jit_solution(14735420794351867722)
XLA Ops:
  6.5 0.8 fusion.22
  7.3 0.2 copy.11
  7.5 1.7 fusion.7
  9.3 9.0 %all-to-all-start = ((bf16[32,16,384]{2,1,0:T(8,128)(2,1)}), bf16[32,16,384]{2,1,0:T(8,128)(2,1)S(1)}, u32[]{:S(2)}, u32[]{:S(2)}) async-start(bf16[32,16,384]{2,1,0:T(8,128)(2,1)} %bitcast.2), calls=%async_computation | async-start | bytes 786432 | tf_op jit(solution)/shard_map/all_to_all | solution.py:18
  18.2 0.7 compare_select_fusion.2
  18.9 0.7 compare_select_fusion.1
  19.6 2.0 gather_fusion.1
  21.7 0.1 broadcast_select_fusion.2
  21.9 0.9 copy-done.5
  22.7 4.7 %all-to-all-done = bf16[32,16,384]{2,1,0:T(8,128)(2,1)S(1)} async-done(((bf16[32,16,384]{2,1,0:T(8,128)(2,1)}), bf16[32,16,384]{2,1,0:T(8,128)(2,1)S(1)}, u32[]{:S(2)}, u32[]{:S(2)}) %all-to-all-start) | async-done | bytes 393248 | tf_op jit(solution)/shard_map/all_to_all | solution.py:18
  27.5 1.6 broadcast_in_dim.51
  29.1 5.2 %all-to-all-start.1 = ((bf16[32,32,1152]{2,1,0:T(8,128)(2,1)}), bf16[32,32,1152]{2,1,0:T(8,128)(2,1)S(1)}, u32[]{:S(2)}, u32[]{:S(2)}) async-start(bf16[32,32,1152]{2,1,0:T(8,128)(2,1)} %broadcast_in_dim.51), calls=%async_computation.1 | async-start | bytes 4718592 | tf_op jit(solution)/shard_map/all_to_all | solution.py:18
  35.0 28.3 %all-to-all-done.1 = bf16[32,32,1152]{2,1,0:T(8,128)(2,1)S(1)} async-done(((bf16[32,32,1152]{2,1,0:T(8,128)(2,1)}), bf16[32,32,1152]{2,1,0:T(8,128)(2,1)S(1)}, u32[]{:S(2)}, u32[]{:S(2)}) %all-to-all-start.1) | async-done | bytes 2359328 | tf_op jit(solution)/shard_map/all_to_all | solution.py:18
  63.3 0.2 copy.8
  63.5 0.9 convert_convert_fusion
  64.4 0.7 copy-done.2
  65.1 0.1 slice.198
  65.2 7.5 %all-to-all-start.2 = ((bf16[32,16,768]{2,1,0:T(8,128)(2,1)}), bf16[32,16,768]{2,1,0:T(8,128)(2,1)S(1)}, u32[]{:S(2)}, u32[]{:S(2)}) async-start(bf16[32,16,768]{2,1,0:T(8,128)(2,1)} %bitcast.40), calls=%async_computation.2 | async-start | bytes 1572864 | tf_op jit(solution)/shard_map/all_to_all | solution.py:18
  72.7 1.9 slice_select_fusion
  74.6 2.4 and_reduce_fusion
  77.0 1.2 reduce.2
  78.2 5.2 %gather_fusion = bf16[1024,768]{1,0:T(8,128)(2,1)} fusion(bf16[1024,768]{1,0:T(8,128)(2,1)S(1)} %slice.198, s32[1024]{0:T(1024)S(1)} %broadcast_clamp_fusion), kind=kCustom, calls=%fused_computation.2 | custom fusion | bytes 3149824 | tf_op jit(solution)/shard_map/jit(_take)/gather | solution.py:150
  83.5 2.2 multiply_reduce_fusion
  85.7 0.1 fusion.28
  85.8 0.1 pad_maximum_fusion.3
  85.9 0.6 fusion
  86.4 0.2 fusion.14
  86.8 1.8 convolution_bitcast_fusion
  88.6 2.7 %gather_fusion.2 = bf16[512,768]{1,0:T(8,128)(2,1)} fusion(bf16[512,768]{1,0:T(8,128)(2,1)S(1)} %bitcast.34, s32[1024]{0:T(1024)S(1)} %get-tuple-element.26), kind=kCustom, calls=%fused_computation.1.clone | custom fusion | bytes 1574912 | tf_op jit(solution)/shard_map/jit(_take)/gather | solution.py:184
  91.4 1.5 multiply_reduce_fusion.1
  92.9 2.3 multiply_subtract_fusion
  95.2 2.5 %pad_maximum_fusion = f32[512,2048]{1,0:T(8,128)} fusion(f32[512,1024]{1,0:T(8,128)S(1)} %copy-done.3, f32[512,1024]{1,0:T(8,128)S(1)} %multiply_subtract_fusion), kind=kLoop, calls=%fused_computation.3 | loop fusion | flops 1048576 | bytes 8388608 | tf_op jit(solution)/shard_map/concatenate | solution.py:187
  97.7 0.1 compare_convert_fusion
  97.8 0.1 compare_convert_fusion.1
  97.9 0.7 all_to_all.35
  98.6 7.6 %all-to-all-start.3 = ((f32[8,2,2304]{2,1,0:T(2,128)}), f32[8,2,2304]{2,1,0:T(2,128)S(1)}, u32[]{:S(2)}, u32[]{:S(2)}) async-start(f32[8,2,2304]{2,1,0:T(2,128)} %all_to_all.35), calls=%async_computation.3 | async-start | bytes 294912 | tf_op jit(solution)/shard_map/all_to_all | solution.py:18
  106.2 10.3 %all-to-all-done.3 = f32[8,2,2304]{2,1,0:T(2,128)S(1)} async-done(((f32[8,2,2304]{2,1,0:T(2,128)}), f32[8,2,2304]{2,1,0:T(2,128)S(1)}, u32[]{:S(2)}, u32[]{:S(2)}) %all-to-all-start.3) | async-done | bytes 147488 | tf_op jit(solution)/shard_map/all_to_all | solution.py:18
  116.5 0.1 reduce_sum.28
  116.6 11.3 %all_to_all.45 = f32[8,2,1152]{2,1,0:T(2,128)S(1)} all-to-all(f32[8,2,1152]{2,1,0:T(2,128)S(1)} %broadcast_in_dim.56), channel_id=1, replica_groups=mesh['krow'=32,'col'=8] {'col'}, dimensions={0} | all-to-all | bytes 147456 | tf_op jit(solution)/shard_map/all_to_all | solution.py:18
  127.9 0.1 reshape.203
  127.9 1.6 broadcast_in_dim.57
  129.5 8.5 %all-to-all-start.5 = ((f32[32,16,1152]{2,1,0:T(8,128)}), f32[32,16,1152]{2,1,0:T(8,128)S(1)}, u32[]{:S(2)}, u32[]{:S(2)}) async-start(f32[32,16,1152]{2,1,0:T(8,128)} %broadcast_in_dim.57), calls=%async_computation.5 | async-start | bytes 4718592 | tf_op jit(solution)/shard_map/all_to_all | solution.py:18
  138.1 39.1 %reduce-scatter.2.cloned.1.call-done = f32[64,2048]{1,0:T(8,128)} async-done(((f32[512,2048]{1,0:T(8,128)}), f32[64,2048]{1,0:T(8,128)}) %reduce-scatter.2.cloned.1.call-update) | async-done | bytes 524304 | tf_op jit(solution)/shard_map/reduce_scatter | solution.py:187
  177.2 1.8 slice_subtract_fusion.m_ref
  179.1 4.0 %all-to-all-done.5 = f32[32,16,1152]{2,1,0:T(8,128)S(1)} async-done(((f32[32,16,1152]{2,1,0:T(8,128)}), f32[32,16,1152]{2,1,0:T(8,128)S(1)}, u32[]{:S(2)}, u32[]{:S(2)}) %all-to-all-start.5) | async-done | bytes 2359328 | tf_op jit(solution)/shard_map/all_to_all | solution.py:18
  183.1 1.4 copy-done.1
  184.5 45.3 %shard_map.55 = f32[64,1024]{1,0:T(8,128)} custom-call(f32[512,1152]{1,0:T(8,128)} %bitcast.36, f32[64,1024]{1,0:T(8,128)} %slice_subtract_fusion.m_ref), custom_call_target="tpu_custom_call" | custom-call | tf_op jit(solution)/shard_map/pallas_call | solution.py:119
  229.8 1.7 or_select_fusion
  (51 shorter events, 0.3 us)
Async XLA Ops:
  6.5 13.1 %copy-start = (bf16[512,768]{1,0:T(8,128)(2,1)S(1)}, bf16[512,768]{1,0:T(8,128)(2,1)}, u32[]{:S(2)}) copy-start(bf16[512,768]{1,0:T(8,128)(2,1)} %param.7) | copy-start | bytes 2359300
  9.3 18.2 %all-to-all-start = ((bf16[32,16,384]{2,1,0:T(8,128)(2,1)}), bf16[32,16,384]{2,1,0:T(8,128)(2,1)S(1)}, u32[]{:S(2)}, u32[]{:S(2)}) async-start(bf16[32,16,384]{2,1,0:T(8,128)(2,1)} %bitcast.2), calls=%async_computation | async-start | bytes 786432 | tf_op jit(solution)/shard_map/all_to_all | solution.py:18
  19.6 2.0 copy-start.8
  21.9 0.9 copy-start.5
  29.1 5.9 %copy-start.7 = (s32[1,512]{1,0:T(1,128)S(1)}, s32[1,512]{1,0:T(1,128)}, u32[]{:S(2)}) copy-start(s32[1,512]{1,0:T(1,128)} %param.10) | copy-start | bytes 6148
  29.1 34.2 %all-to-all-start.1 = ((bf16[32,32,1152]{2,1,0:T(8,128)(2,1)}), bf16[32,32,1152]{2,1,0:T(8,128)(2,1)S(1)}, u32[]{:S(2)}, u32[]{:S(2)}) async-start(bf16[32,32,1152]{2,1,0:T(8,128)(2,1)} %broadcast_in_dim.51), calls=%async_computation.1 | async-start | bytes 4718592 | tf_op jit(solution)/shard_map/all_to_all | solution.py:18
  63.5 1.6 copy-start.2
  65.2 23.4 %all-to-all-start.2 = ((bf16[32,16,768]{2,1,0:T(8,128)(2,1)}), bf16[32,16,768]{2,1,0:T(8,128)(2,1)S(1)}, u32[]{:S(2)}, u32[]{:S(2)}) async-start(bf16[32,16,768]{2,1,0:T(8,128)(2,1)} %bitcast.40), calls=%async_computation.2 | async-start | bytes 1572864 | tf_op jit(solution)/shard_map/all_to_all | solution.py:18
  72.7 104.6 %reduce-scatter.2.cloned.1.call-start = ((), (), s32[]{:S(2)}) async-start(), calls=%async_computation.7 | async-start | bytes 4718592 | tf_op jit(solution)/shard_map/reduce_scatter | solution.py:187
  83.5 2.2 copy-start.4
  85.7 1.1 copy-start.6
  92.9 2.3 copy-start.3
  98.6 17.8 %all-to-all-start.3 = ((f32[8,2,2304]{2,1,0:T(2,128)}), f32[8,2,2304]{2,1,0:T(2,128)S(1)}, u32[]{:S(2)}, u32[]{:S(2)}) async-start(f32[8,2,2304]{2,1,0:T(2,128)} %all_to_all.35), calls=%async_computation.3 | async-start | bytes 294912 | tf_op jit(solution)/shard_map/all_to_all | solution.py:18
  129.5 53.6 %all-to-all-start.5 = ((f32[32,16,1152]{2,1,0:T(8,128)}), f32[32,16,1152]{2,1,0:T(8,128)S(1)}, u32[]{:S(2)}, u32[]{:S(2)}) async-start(f32[32,16,1152]{2,1,0:T(8,128)} %broadcast_in_dim.57), calls=%async_computation.5 | async-start | bytes 4718592 | tf_op jit(solution)/shard_map/all_to_all | solution.py:18
  183.1 1.4 copy-start.1
Sparse Core Ops, SparseCore 0:
  97.8 79.3 reduce-scatter.1

commit v3 on v2

--- a/solution.py
+++ b/solution.py
@@ -9,10 +9,14 @@
 PW = 512
 TOP = 2 * PW
 BK = 128
-OWN = 64
 CODE = 32
 RIDGE = 0.5
 HI = lax.Precision.HIGHEST
+
+
+def rows_at(array, where):
+    return array.at[where].get(mode="promise_in_bounds", unique_indices=True)
+
 
 def swap(value, axis):
     return lax.all_to_all(value, axis, split_axis=0, concat_axis=0, tiled=True)
@@ -48,13 +52,16 @@
 def dot_t(a, b):
     return lax.dot_general(a, b, (((1,), (1,)), ((), ())), precision=HI, preferred_element_type=jnp.float32)
 
+
 def over_rows(v, k):
     return jnp.broadcast_to(v[k:k + 1, :], v.shape)
 
+
 def over_lanes(v, c):
     return jnp.broadcast_to(v[:, c:c + 1], v.shape)
 
-def invert_factor(tiles, w_ref):
+
+def invert_factor(tiles, w_ref, first):
     n = len(tiles)
     lane = lax.broadcasted_iota(jnp.int32, (8, BK), 1)
     sub = lax.broadcasted_iota(jnp.int32, (8, BK), 0)
@@ -77,7 +84,7 @@
             inv.append(r)
             rows.append(row)
         unit = jnp.where(lane < c0 + sub, top, jnp.where(lane == c0 + sub, 1.0, 0.0))
-        w_ref[c0:c0 + 8, :] = unit * lax.rsqrt(pivots)
+        w_ref[pl.ds(pl.multiple_of(first + c0, 8), 8), :] = unit * lax.rsqrt(pivots)
         for i in range(g + 1, n):
             tile = tiles[i]
             cols = [over_lanes(tile, c0 + k) for k in range(8)]
@@ -88,41 +95,86 @@
                 tile = tile - m * rows[k]
             tiles[i] = tile
 
-def chol_kernel(f_ref, m_ref, o_ref, a_ref, w_ref):
+
+def factor_kernel(core_ref, mine_ref, other_ref, a_ref, w_ref):
     nb = TOP // BK
-    for r in range(nb):
-        if r >= nb // 2:
-            b = nb - 1 - r
-            a_ref[r * BK:(r + 1) * BK, :(r + 1) * BK] = f_ref[b * BK:(b + 1) * BK, :(r + 1) * BK]
-        else:
-            for j in range(r + 1):
-                a_ref[r * BK:(r + 1) * BK, j * BK:(j + 1) * BK] = f_ref[r * BK:(r + 1) * BK, (nb - j) * BK:(nb + 1 - j) * BK]
-    a_ref[TOP:, :] = m_ref[...]
+    pieces = mine_ref.shape[0]
+    half = mine_ref.shape[1]
+    per = pieces // (nb // 2)
+
+    def place(first, second):
+        for b in range(nb // 2):
+            for i in range(per):
+                for h, ref in enumerate((first, second)):
+                    src = ref[b * per + i]
+                    at = i * 2 * half + h * half
+                    r = nb - 1 - b
+                    a_ref[r * BK + at:r * BK + at + half, :(r + 1) * BK] = src[:, :(r + 1) * BK]
+                    for j in range(b + 1):
+                        a_ref[b * BK + at:b * BK + at + half, j * BK:(j + 1) * BK] = (
+                            src[:, (nb - j) * BK:(nb + 1 - j) * BK])
+
+    @pl.when(core_ref[0] == 0)
+    def _():
+        place(mine_ref, other_ref)
+
+    @pl.when(core_ref[0] != 0)
+    def _():
+        place(other_ref, mine_ref)
 
     def step(j, carry):
         o = pl.multiple_of(j * BK, BK)
         tiles = [a_ref[pl.ds(pl.multiple_of(o + 8 * i, 8), 8), pl.ds(o, BK)] for i in range(BK // 8)]
-        invert_factor(tiles, w_ref)
-        for b in range(nb):
+        invert_factor(tiles, w_ref, o)
+        for b in range(nb - 1):
             @pl.when(j == b)
             def _():
                 lo, hi = b * BK, (b + 1) * BK
-                panel = dot_t(a_ref[hi:, lo:hi], w_ref[...])
-                o_ref[:, lo:hi] = panel[TOP - hi:, :]
+                panel = dot_t(a_ref[hi:, lo:hi], w_ref[lo:hi, :])
+                a_ref[hi:, lo:hi] = panel
                 for c in range(b + 1, nb):
                     at = c * BK
                     a_ref[at:, at:at + BK] -= dot_t(panel[at - hi:, :], panel[at - hi:at - hi + BK, :])
         return carry
+
     lax.fori_loop(0, nb, step, 0)
 
-def factor_and_solve(folded, matrix):
+
+def solve_kernel(first_ref, p0_ref, p1_ref, p2_ref, p3_ref, a_ref, w_ref, o_ref):
+    nb = TOP // BK
+    total = (p0_ref[...] + p1_ref[...]) + (p2_ref[...] + p3_ref[...])
+    rows = total.shape[0]
+    pos = first_ref[0] + lax.broadcasted_iota(jnp.int32, (rows, TOP), 0)
+    col = lax.broadcasted_iota(jnp.int32, (rows, TOP), 1)
+    shift = jnp.where(pos == col, RIDGE, 0.0)
+    m = jnp.exp(total[:, :TOP] * (-1.0 / (2.0 * F))) + shift - total[:, TOP:]
+    for b in range(nb):
+        lo, hi = b * BK, (b + 1) * BK
+        x = dot_t(m[:, :BK], w_ref[lo:hi, :])
+        keep = (pos[:, lo:hi] >= PW) | (lo < PW)
+        o_ref[:, lo:hi] = jnp.where(keep, x, 0.0)
+        if b + 1 < nb:
+            m = m[:, BK:] - dot_t(x, a_ref[hi:, lo:hi])
+
+
+def factor(core, mine, other):
+    vmem = pl.BlockSpec(memory_space=pltpu.VMEM)
     return pl.pallas_call(
-        chol_kernel,
-        out_shape=jax.ShapeDtypeStruct(matrix.shape, jnp.float32),
-        in_specs=[pl.BlockSpec(memory_space=pltpu.VMEM)] * 2,
-        out_specs=pl.BlockSpec(memory_space=pltpu.VMEM),
-        scratch_shapes=[pltpu.VMEM((TOP + OWN, TOP), jnp.float32), pltpu.VMEM((BK, BK), jnp.float32)],
-    )(folded, matrix)
+        factor_kernel,
+        out_shape=(jax.ShapeDtypeStruct((TOP, TOP), jnp.float32), jax.ShapeDtypeStruct((TOP, BK), jnp.float32)),
+        in_specs=[pl.BlockSpec(memory_space=pltpu.SMEM), vmem, vmem],
+        out_specs=(vmem, vmem),
+    )(core, mine, other)
+
+
+def solve(first, parts, low, inverses):
+    vmem = pl.BlockSpec(memory_space=pltpu.VMEM)
+    return pl.pallas_call(
+        solve_kernel,
+        out_shape=jax.ShapeDtypeStruct((parts[0].shape[0], TOP), jnp.float32),
+        in_specs=[pl.BlockSpec(memory_space=pltpu.SMEM)] + [vmem] * 6,
+        out_specs=vmem,
+    )(first, *parts, low, inverses)
 
 
 def shards(features, slab, pack_order, place_order, start):
@@ -137,7 +189,7 @@
     coded = jnp.stack([order // CODE, order % CODE], axis=1).astype(jnp.bfloat16)
     coded = jnp.pad(coded, ((0, 0), (0, BK - 2)))
     slab_part = swap(jnp.concatenate([slab, coded], axis=1), "krow")[:2 * group]
-    packed = jnp.take(features, pack_order[0], axis=0)
+    packed = rows_at(features, pack_order[0])
     feat_dev = packed.shape[1]
     tiles = from_everyone(jnp.concatenate([packed[:2 * group], slab_part], axis=1), "krow")
     packed, tiles = lax.optimization_barrier((packed, tiles))
@@ -147,7 +199,7 @@
     top = jnp.moveaxis(tiles, 1, 0).reshape(TOP, tiles.shape[-1])
     places = top[:, feat_dev + prior_dev:feat_dev + prior_dev + 2].astype(jnp.float32).astype(jnp.int32)
     wanted = places[:, 0] * CODE + places[:, 1] + jnp.arange(TOP) // rows_dev * rows_dev
-    top_feats = jnp.take(top[:, :feat_dev], wanted, axis=0)
+    top_feats = rows_at(top[:, :feat_dev], wanted)
     top_slab = jnp.where(kept, top[:, feat_dev:feat_dev + prior_dev], jnp.zeros((), jnp.bfloat16))
     top_norms = sq_norms(top_feats)
 
@@ -170,7 +222,8 @@
     update = fold(update[:share], update[share:], pair)
     parts = jnp.concatenate([dist, update], axis=1)
     parts, arrived = lax.optimization_barrier((parts, arrived))
-    summed = jnp.sum(swap(parts, "col").reshape(n_col, share // n_col, 2 * 9 * BK), axis=0)
+    parts = swap(parts, "col")
+    summed = jnp.sum(parts.reshape(n_col, share // n_col, 2 * 9 * BK), axis=0)
     dist, update = summed[:, :9 * BK], summed[:, 9 * BK:]
     mine = share // n_col
     col_ids = jnp.arange(TOP)[None, :]
@@ -179,20 +232,38 @@
                  (row_lo + ids == col_ids).astype(jnp.float32), pair)
     entries = jnp.exp(-dist / (2.0 * F)) + RIDGE * shift - update
     entries = from_everyone(entries, "col").reshape(share, 9 * BK)
-    folded = from_everyone(entries, "krow").reshape(PW, 9 * BK)
-
-    ordered = jnp.take(arrived, place_order[0], axis=0)
+
+    core, pair_at = col % 2, col // 2
+    pairs = n_col // 2
+    own = rows_dev // n_col
+
+    def split_rows(array):
+        array = array.reshape(pairs, 2, own, *array.shape[1:])
+        halves = [lax.dynamic_index_in_dim(array, which, 1, keepdims=False) for which in (1 - core, core)]
+        return jnp.concatenate([h.reshape(pairs * own, *h.shape[2:]) for h in halves], axis=0)
+
+    ordered = rows_at(arrived, split_rows(place_order[0]))
     dist = sq_norms(ordered)[:, None] + top_norms[None, :] - 2.0 * inner(ordered, top_feats)
-    update = inner(slab, top_slab)
-    parts = lax.psum_scatter(jnp.concatenate([dist, update], axis=1), "col", scatter_dimension=0, tiled=True)
-    dist, update = parts[:, :TOP], parts[:, TOP:]
-    own = rows_dev // n_col
-    positions = krow * rows_dev + col * own + jnp.arange(own)
-    shift = (positions[:, None] == col_ids).astype(jnp.float32)
-    matrix = jnp.exp(-dist / (2.0 * F)) + RIDGE * shift - update
-
-    solved = factor_and_solve(folded, matrix)
-    return jnp.where((positions[:, None] >= PW) | (col_ids < PW), solved, 0.0)
+    update = inner(split_rows(slab), top_slab)
+    parts = jnp.concatenate([dist, update], axis=1)
+    half = pairs * own
+    got = lax.ppermute(parts[:half], "col", [(c, c ^ 1) for c in range(n_col)])
+    both_cores = (parts[half:] + got).reshape(pairs, own, 2 * TOP)
+    both_cores, entries = lax.optimization_barrier((both_cores, entries))
+    sums = [lax.dynamic_index_in_dim(both_cores, pair_at, 0, keepdims=False)]
+    for away in range(1, pairs):
+        piece = lax.dynamic_index_in_dim(both_cores, (pair_at + away) % pairs, 0, keepdims=False)
+        to = [(c, (c // 2 + away) % pairs * 2 + c % 2) for c in range(n_col)]
+        sums.append(lax.ppermute(piece, "col", to))
+
+    half_share = share // 2
+    piece = lax.dynamic_slice_in_dim(entries, core * half_share, half_share, 0)
+    mine = from_everyone(piece, "krow")
+    mine = mine.reshape(n_krow, half_share, 9 * BK)
+    other = lax.ppermute(mine, "col", [(c, c ^ 1) for c in range(n_col)])
+    low, inverses = factor(core.reshape(1), mine, other)
+    first_row = krow * rows_dev + col * own
+    return solve(first_row.reshape(1), sums, low, inverses)
 
 
 def solution(mesh):

time: 242 us -> 215 us (0.89)
  waiting for transfers between devices: 86.5 us -> 51.1 us
  blocking collectives: 11.3 us -> 25.4 us
  between operations: 14.5 us -> 1.08 us
  Pallas kernels: 45.3 us -> 53.6 us
  other arithmetic: 20.6 us -> 16.5 us
    reduce_scatter x1 -> x0, waiting for transfers between devices: 39.1 us -> none  [shards(): lax.psum_scatter(jnp.concatenate([dist, update], axis=1), 'col', scatter_...]
    all_to_all x1, blocking collectives: 11.3 us -> 25.4 us  [swap(): return lax.all_to_all(value, axis, split_axis=0, concat_axis=0, tiled=True)]
    pallas_call x1 -> x2, Pallas kernels: 45.3 us -> 53.6 us  [the longest x1 45.2 us: factor(): pl.pallas_call(factor_kernel, out_shape=(jax.ShapeDtypeStruct((TOP, TOP),...]
    all_to_all x5, starting transfers between devices: 37.7 us -> 32.7 us  [swap(): return lax.all_to_all(value, axis, split_axis=0, concat_axis=0, tiled=True)]
    ppermute x0 -> x5, starting transfers between devices: none -> 4.28 us  [the longest x3 4.27 us: shards(): sums.append(lax.ppermute(piece, 'col', to))]
    add x1, other arithmetic: 0.01 us -> 3.45 us  [shards(): both_cores = (parts[half:] + got).reshape(pairs, own, 2 * TOP)]
    all_to_all x5, waiting for transfers between devices: 47.3 us -> 50.5 us  [swap(): return lax.all_to_all(value, axis, split_axis=0, concat_axis=0, tiled=True)]
  transfers between devices with their start and end apart: 6 -> 10, of which waited for: 5 -> 5; matrix products, arithmetic and copies ran while one was open for 10% -> 11% of each run, Pallas kernels for 0% -> 21%
where the time goes in v3:
time: 215 us; the launch traced here: 211 us
  Pallas kernels  53.6 us (25%)
  waiting for transfers between devices  51.1 us (24%)
  starting transfers between devices  36.9 us (17%)
  blocking collectives  25.4 us (12%)
  local copies, waits for them, and re-layouts  19.9 us (9%)
  other arithmetic  16.5 us (8%)
  matrix products  6.83 us (3%)
    all_to_all x5, waiting for transfers between devices, swap(): return lax.all_to_all(value, axis, split_axis=0, concat_axis=0, tiled=True)  50.5 us
    pallas_call x1, Pallas kernels, factor(): pl.pallas_call(factor_kernel, out_shape=(jax.ShapeDtypeStruct((TOP, TOP),...  45.2 us
    all_to_all x5, starting transfers between devices, swap(): return lax.all_to_all(value, axis, split_axis=0, concat_axis=0, tiled=True)  32.7 us
    all_to_all x1, blocking collectives, swap(): return lax.all_to_all(value, axis, split_axis=0, concat_axis=0, tiled=True)  25.4 us
    gather x3, local copies, waits for them, and re-layouts, rows_at(): return array.at[where].get(mode='promise_in_bounds', unique_indices=True)  9.25 us
    pallas_call x1, Pallas kernels, solve(): pl.pallas_call(solve_kernel, out_shape=jax.ShapeDtypeStruct((parts[0].sha...  8.46 us
    dot_general x4, matrix products, inner(): lax.dot_general(a, b, (((1,), (1,)), ((), ())), preferred_element_type=jn...  6.83 us
  transfers between devices with their start and end apart: 10, of which 5 were waited for; matrix products, arithmetic and copies ran while one was open for 11% of the time, Pallas kernels for 21%

profile of v3, /device:TPU:2, one launch (start us, length us, event | category | flops | bytes accessed | tf_op | source)
XLA Modules:
  0.0 211.4 jit_solution(15314226100506198212)
XLA Ops:
  0.0 0.8 fusion.26
  0.8 0.2 copy.12
  1.0 1.7 fusion.10
  2.7 9.0 %all-to-all-start = ((bf16[32,16,384]{2,1,0:T(8,128)(2,1)}), bf16[32,16,384]{2,1,0:T(8,128)(2,1)S(1)}, u32[]{:S(2)}, u32[]{:S(2)}) async-start(bf16[32,16,384]{2,1,0:T(8,128)(2,1)} %bitcast.4), calls=%async_computation | async-start | bytes 786432 | tf_op jit(solution)/shard_map/all_to_all | solution.py:22
  11.7 0.5 broadcast.248
  12.3 1.3 reduce.6
  13.9 0.7 compare_select_fusion.1
  14.6 2.0 gather_fusion
  16.6 4.3 %all-to-all-done = bf16[32,16,384]{2,1,0:T(8,128)(2,1)S(1)} async-done(((bf16[32,16,384]{2,1,0:T(8,128)(2,1)}), bf16[32,16,384]{2,1,0:T(8,128)(2,1)S(1)}, u32[]{:S(2)}, u32[]{:S(2)}) %all-to-all-start) | async-done | bytes 393248 | tf_op jit(solution)/shard_map/all_to_all | solution.py:22
  21.0 1.6 broadcast_in_dim.18
  22.6 5.2 %all-to-all-start.1 = ((bf16[32,32,1152]{2,1,0:T(8,128)(2,1)}), bf16[32,32,1152]{2,1,0:T(8,128)(2,1)S(1)}, u32[]{:S(2)}, u32[]{:S(2)}) async-start(bf16[32,32,1152]{2,1,0:T(8,128)(2,1)} %broadcast_in_dim.18), calls=%async_computation.1 | async-start | bytes 4718592 | tf_op jit(solution)/shard_map/all_to_all | solution.py:22
  28.5 0.7 constant_dynamic-slice_fusion.2
  29.2 27.6 %all-to-all-done.1 = bf16[32,32,1152]{2,1,0:T(8,128)(2,1)S(1)} async-done(((bf16[32,32,1152]{2,1,0:T(8,128)(2,1)}), bf16[32,32,1152]{2,1,0:T(8,128)(2,1)S(1)}, u32[]{:S(2)}, u32[]{:S(2)}) %all-to-all-start.1) | async-done | bytes 2359328 | tf_op jit(solution)/shard_map/all_to_all | solution.py:22
  56.8 0.2 copy.7
  57.0 1.0 convert_convert_fusion
  58.0 0.6 copy-done.2
  58.7 7.5 %all-to-all-start.2 = ((bf16[32,16,768]{2,1,0:T(8,128)(2,1)}), bf16[32,16,768]{2,1,0:T(8,128)(2,1)S(1)}, u32[]{:S(2)}, u32[]{:S(2)}) async-start(bf16[32,16,768]{2,1,0:T(8,128)(2,1)} %bitcast.59), calls=%async_computation.2 | async-start | bytes 1572864 | tf_op jit(solution)/shard_map/all_to_all | solution.py:22
  66.2 1.9 slice_select_fusion
  68.1 1.6 fusion.8
  69.7 5.2 %gather_fusion.1 = bf16[1024,768]{1,0:T(8,128)(2,1)} fusion(bf16[1024,768]{1,0:T(8,128)(2,1)S(1)} %slice.195, s32[1024]{0:T(1024)S(1)} %broadcast_clamp_fusion), kind=kCustom, calls=%fused_computation.1 | custom fusion | bytes 3149824 | tf_op jit(solution)/shard_map/gather | solution.py:18
  74.9 1.8 multiply_reduce_fusion
  76.8 0.8 constant_dynamic-slice_fusion.8
  77.5 0.7 constant_dynamic-slice_fusion.6
  78.4 2.0 fusion.2
  80.4 0.2 fusion.18
  80.8 1.8 fusion.11
  82.6 2.0 gather_fusion.2
  84.6 0.9 copy-done.7
  85.5 0.2 multiply_reduce_fusion.1
  85.8 2.8 %multiply_subtract_fusion = f32[512,1024]{1,0:T(8,128)S(1)} fusion(bf16[512,768]{1,0:T(8,128)(2,1)} %copy-done.7, bf16[1024,768]{1,0:T(8,128)(2,1)} %gather_fusion.1, f32[1024]{0:T(1024)S(1)} %multiply_reduce_fusion, f32[512]{0:T(512)S(1)} %multiply_reduce_fusion.1), kind=kOutput, calls=%fused_computation.9 | convolution fusion | flops 806879232 | bytes 4462592 | tf_op jit(solution)/shard_map/dot_general | solution.py:34
  88.6 1.6 pad_maximum_fusion
  90.1 0.4 copy-done.3
  90.7 0.7 all_to_all.35
  91.5 7.7 %all-to-all-start.3 = ((f32[8,2,2304]{2,1,0:T(2,128)}), f32[8,2,2304]{2,1,0:T(2,128)S(1)}, u32[]{:S(2)}, u32[]{:S(2)}) async-start(f32[8,2,2304]{2,1,0:T(2,128)} %all_to_all.35), calls=%async_computation.3 | async-start | bytes 294912 | tf_op jit(solution)/shard_map/all_to_all | solution.py:22
  99.2 10.2 %all-to-all-done.3 = f32[8,2,2304]{2,1,0:T(2,128)S(1)} async-done(((f32[8,2,2304]{2,1,0:T(2,128)}), f32[8,2,2304]{2,1,0:T(2,128)S(1)}, u32[]{:S(2)}, u32[]{:S(2)}) %all-to-all-start.3) | async-done | bytes 147488 | tf_op jit(solution)/shard_map/all_to_all | solution.py:22
  109.5 0.7 broadcast_in_dim.34
  110.2 3.4 %all-to-all-start.4 = ((f32[8,2,1152]{2,1,0:T(2,128)}), f32[8,2,1152]{2,1,0:T(2,128)S(1)}, u32[]{:S(2)}, u32[]{:S(2)}) async-start(f32[8,2,1152]{2,1,0:T(2,128)} %broadcast_in_dim.34), calls=%async_computation.4 | async-start | bytes 147456 | tf_op jit(solution)/shard_map/all_to_all | solution.py:22
  113.5 8.3 %all-to-all-done.4 = f32[8,2,1152]{2,1,0:T(2,128)S(1)} async-done(((f32[8,2,1152]{2,1,0:T(2,128)}), f32[8,2,1152]{2,1,0:T(2,128)S(1)}, u32[]{:S(2)}, u32[]{:S(2)}) %all-to-all-start.4) | async-done | bytes 73760 | tf_op jit(solution)/shard_map/all_to_all | solution.py:22
  121.9 3.4 %fusion.1 = f32[256,2048]{1,0:T(8,128)} fusion(f32[256,2048]{1,0:T(8,128)} %collective-permute-done, f32[512,1024]{1,0:T(8,128)} %copy-done.3, f32[512,1024]{1,0:T(8,128)S(1)} %copy-done.1), kind=kLoop, calls=%fused_computation.7 | loop fusion | flops 1048576 | bytes 8388608 | tf_op jit(solution)/shard_map/add | solution.py:251
  125.4 25.4 %all_to_all.45.mine_ref = f32[32,8,1152]{2,1,0:T(8,128)} all-to-all(f32[32,8,1152]{2,1,0:T(8,128)S(1)} %broadcast_in_dim.35), channel_id=1, replica_groups=mesh['krow'=32,'col'=8] {'krow'}, dimensions={0} | all-to-all | bytes 2359296 | tf_op jit(solution)/shard_map/all_to_all | solution.py:22
  150.9 1.2 dynamic-slice_bitcast_fusion
  152.1 0.5 collective-permute-start.3
  152.6 3.7 %collective-permute-start.2 = (f32[64,2048]{1,0:T(8,128)}, f32[64,2048]{1,0:T(8,128)S(1)}, u32[]{:S(2)}, u32[]{:S(2)}) collective-permute-start(f32[64,2048]{1,0:T(8,128)} %get-tuple-element.24), channel_id=1, source_target_pairs={{0,4},{1,5},{2,6},{3,7},{4,0},{5,1},{6,2},{7,3},{8,12},{9,13},{10,... | collective-permute-start | bytes 1572872 | tf_op jit(solution)/shard_map/ppermute | solution.py:257
  156.4 45.2 %shard_map.55 = (f32[1024,1024]{1,0:T(8,128)}, f32[1024,128]{1,0:T(8,128)}) custom-call(s32[1]{0:T(128)} %bitcast.21.core_ref, f32[32,8,1152]{2,1,0:T(8,128)} %all_to_all.45.mine_ref, f32[32,8,1152]{2,1,0:T(8,128)} %collective-permute-done.4.other_ref), custom_call_target="tpu_custom_call" | custom-call | tf_op jit(solution)/shard_map/pallas_call | solution.py:162
  201.5 0.6 collective-permute-done.1.p1_ref
  202.3 0.2 copy-done.10
  202.5 0.4 copy-done.11
  203.0 8.5 %shard_map.56 = f32[64,1024]{1,0:T(8,128)} custom-call(s32[1]{0:T(128)} %bitcast.first_ref, f32[64,2048]{1,0:T(8,128)} %get-tuple-element.26.p0_ref, f32[64,2048]{1,0:T(8,128)} %copy-done.11, f32[64,2048]{1,0:T(8,128)} %copy-done.10, f32[64,2048]{1,0:T(8,128)} %copy-done.9, f32[1024,1024]{1,0:T(8,128)} %get-tuple-element.19.a_ref, ...), custom_call_target="tpu_custom_call" | custom-call | tf_op jit(solution)/shard_map/pallas_call | solution.py:172
  (70 shorter events, 1.3 us)
Async XLA Ops:
  0.0 14.6 %copy-start = (bf16[512,768]{1,0:T(8,128)(2,1)S(1)}, bf16[512,768]{1,0:T(8,128)(2,1)}, u32[]{:S(2)}) copy-start(bf16[512,768]{1,0:T(8,128)(2,1)} %param.5) | copy-start | bytes 2359300
  2.7 18.2 %all-to-all-start = ((bf16[32,16,384]{2,1,0:T(8,128)(2,1)}), bf16[32,16,384]{2,1,0:T(8,128)(2,1)S(1)}, u32[]{:S(2)}, u32[]{:S(2)}) async-start(bf16[32,16,384]{2,1,0:T(8,128)(2,1)} %bitcast.4), calls=%async_computation | async-start | bytes 786432 | tf_op jit(solution)/shard_map/all_to_all | solution.py:22
  16.6 6.0 %copy-start.6 = (bf16[512,768]{1,0:T(8,128)(2,1)}, bf16[512,768]{1,0:T(8,128)(2,1)S(1)}, u32[]{:S(2)}) copy-start(bf16[512,768]{1,0:T(8,128)(2,1)S(1)} %gather_fusion) | copy-start | bytes 2359300
  22.6 5.9 %copy-start.8 = (bf16[512,256]{1,0:T(8,128)(2,1)S(1)}, bf16[512,256]{1,0:T(8,128)(2,1)}, u32[]{:S(2)}) copy-start(bf16[512,256]{1,0:T(8,128)(2,1)} %param.6) | copy-start | bytes 786436
  22.6 34.2 %all-to-all-start.1 = ((bf16[32,32,1152]{2,1,0:T(8,128)(2,1)}), bf16[32,32,1152]{2,1,0:T(8,128)(2,1)S(1)}, u32[]{:S(2)}, u32[]{:S(2)}) async-start(bf16[32,32,1152]{2,1,0:T(8,128)(2,1)} %broadcast_in_dim.18), calls=%async_computation.1 | async-start | bytes 4718592 | tf_op jit(solution)/shard_map/all_to_all | solution.py:22
  57.0 1.6 copy-start.2
  58.7 23.9 %all-to-all-start.2 = ((bf16[32,16,768]{2,1,0:T(8,128)(2,1)}), bf16[32,16,768]{2,1,0:T(8,128)(2,1)S(1)}, u32[]{:S(2)}, u32[]{:S(2)}) async-start(bf16[32,16,768]{2,1,0:T(8,128)(2,1)} %bitcast.59), calls=%async_computation.2 | async-start | bytes 1572864 | tf_op jit(solution)/shard_map/all_to_all | solution.py:22
  74.9 5.5 %copy-start.5 = (bf16[1024,256]{1,0:T(8,128)(2,1)S(1)}, bf16[1024,256]{1,0:T(8,128)(2,1)}, u32[]{:S(2)}) copy-start(bf16[1024,256]{1,0:T(8,128)(2,1)} %slice_select_fusion) | copy-start | bytes 1572868
  74.9 5.9 %copy-start.12 = (bf16[4,1,64,256]{3,2,1,0:T(8,128)(2,1)S(1)}, bf16[4,1,64,256]{3,2,1,0:T(8,128)(2,1)}, u32[]{:S(2)}) copy-start(bf16[4,1,64,256]{3,2,1,0:T(8,128)(2,1)} %get-tuple-element.32) | copy-start | bytes 393220
  84.6 0.9 copy-start.7
  85.7 2.8 %copy-start.1 = (f32[512,1024]{1,0:T(8,128)S(1)}, f32[512,1024]{1,0:T(8,128)}, u32[]{:S(2)}) copy-start(f32[512,1024]{1,0:T(8,128)} %fusion.11) | copy-start | bytes 6291460
  88.6 2.0 copy-start.3
  90.6 31.3 %collective-permute-start = (f32[256,2048]{1,0:T(8,128)}, f32[256,2048]{1,0:T(8,128)}, u32[]{:S(2)}, u32[]{:S(2)}) collective-permute-start(f32[256,2048]{1,0:T(8,128)} %pad_maximum_fusion), channel_id=1, source_target_pairs={{0,1},{1,0},{2,3},{3,2},{4,5},{5,4},{6,7},{7,6},{8,9},{9,8},{10,11... | collective-permute-start | bytes 6291464 | tf_op jit(solution)/shard_map/ppermute | solution.py:250
  91.5 17.9 %all-to-all-start.3 = ((f32[8,2,2304]{2,1,0:T(2,128)}), f32[8,2,2304]{2,1,0:T(2,128)S(1)}, u32[]{:S(2)}, u32[]{:S(2)}) async-start(f32[8,2,2304]{2,1,0:T(2,128)} %all_to_all.35), calls=%async_computation.3 | async-start | bytes 294912 | tf_op jit(solution)/shard_map/all_to_all | solution.py:22
  110.2 11.7 %all-to-all-start.4 = ((f32[8,2,1152]{2,1,0:T(2,128)}), f32[8,2,1152]{2,1,0:T(2,128)S(1)}, u32[]{:S(2)}, u32[]{:S(2)}) async-start(f32[8,2,1152]{2,1,0:T(2,128)} %broadcast_in_dim.34), calls=%async_computation.4 | async-start | bytes 147456 | tf_op jit(solution)/shard_map/all_to_all | solution.py:22
  125.4 25.5 %copy-start.4 = (f32[256,2048]{1,0:T(8,128)S(1)}, f32[256,2048]{1,0:T(8,128)}, u32[]{:S(2)}) copy-start(f32[256,2048]{1,0:T(8,128)} %fusion.1) | copy-start | bytes 6291460
  150.9 5.5 %collective-permute-start.4 = (f32[32,8,1152]{2,1,0:T(8,128)}, f32[32,8,1152]{2,1,0:T(8,128)}, u32[]{:S(2)}, u32[]{:S(2)}) collective-permute-start(f32[32,8,1152]{2,1,0:T(8,128)} %all_to_all.45.mine_ref), channel_id=1, source_target_pairs={{0,1},{1,0},{2,3},{3,2},{4,5},{5,4},{6,7},{7,6},{8,9},{9,8},{10,11... | collective-permute-start | bytes 3538952 | tf_op jit(solution)/shard_map/ppermute | solution.py:263
  152.1 49.4 %collective-permute-start.3 = (f32[64,2048]{1,0:T(8,128)}, f32[64,2048]{1,0:T(8,128)S(1)}, u32[]{:S(2)}, u32[]{:S(2)}) collective-permute-start(f32[64,2048]{1,0:T(8,128)} %get-tuple-element.23), channel_id=1, source_target_pairs={{0,6},{1,7},{2,0},{3,1},{4,2},{5,3},{6,4},{7,5},{8,14},{9,15},{10,... | collective-permute-start | bytes 1572872 | tf_op jit(solution)/shard_map/ppermute | solution.py:257
  152.6 48.9 %collective-permute-start.2 = (f32[64,2048]{1,0:T(8,128)}, f32[64,2048]{1,0:T(8,128)S(1)}, u32[]{:S(2)}, u32[]{:S(2)}) collective-permute-start(f32[64,2048]{1,0:T(8,128)} %get-tuple-element.24), channel_id=1, source_target_pairs={{0,4},{1,5},{2,6},{3,7},{4,0},{5,1},{6,2},{7,3},{8,12},{9,13},{10,... | collective-permute-start | bytes 1572872 | tf_op jit(solution)/shard_map/ppermute | solution.py:257
  156.3 45.8 %collective-permute-start.1 = (f32[64,2048]{1,0:T(8,128)S(1)}, f32[64,2048]{1,0:T(8,128)S(1)}, u32[]{:S(2)}, u32[]{:S(2)}) collective-permute-start(f32[64,2048]{1,0:T(8,128)S(1)} %get-tuple-element.25), channel_id=1, source_target_pairs={{0,2},{1,3},{2,4},{3,5},{4,6},{5,7},{6,0},{7,1},{8,10},{9,11},{10,... | collective-permute-start | bytes 1572872 | tf_op jit(solution)/shard_map/ppermute | solution.py:257
  201.5 0.8 copy-start.9
  201.5 1.0 copy-start.10
  202.2 0.8 copy-start.11

commit v4 on v3

--- a/solution.py
+++ b/solution.py
@@ -10,6 +10,7 @@
 TOP = 2 * PW
 BK = 128
 CODE = 32
+MB = 16
 RIDGE = 0.5
 HI = lax.Precision.HIGHEST
 
@@ -58,41 +59,49 @@
 
 
 def over_lanes(v, c):
-    return jnp.broadcast_to(v[:, c:c + 1], v.shape)
+    return jnp.take_along_axis(v, jnp.full(v.shape, c, jnp.int32), axis=1, mode="promise_in_bounds")
+
+
+def inverse_of(p):
+    return 1.0 / p
 
 
 def invert_factor(tiles, w_ref, first):
     n = len(tiles)
-    lane = lax.broadcasted_iota(jnp.int32, (8, BK), 1)
-    sub = lax.broadcasted_iota(jnp.int32, (8, BK), 0)
+    lane = lax.broadcasted_iota(jnp.int32, (MB, BK), 1)
+    sub = lax.broadcasted_iota(jnp.int32, (MB, BK), 0)
     for g in range(n):
-        c0 = 8 * g
-        top = tiles[g]
-        cols = [over_lanes(top, c0 + k) for k in range(8)]
-        cross, inv, rows = {}, [], []
-        pivots = jnp.ones((8, BK), jnp.float32)
-        for k in range(8):
-            p = over_rows(cols[k], k)
-            r = 1.0 / p
-            row = jnp.where(lane == c0 + k, p + 1.0, over_rows(top, k))
-            m = jnp.where(sub > k, cols[k] * r, 0.0)
-            for k2 in range(k + 1, 8):
-                cross[k, k2] = over_rows(cols[k2], k)
-                cols[k2] = cols[k2] - m * cross[k, k2]
-            top = top - m * row
+        c0 = MB * g
+        cols = [over_lanes(tiles[g], c0 + k) for k in range(MB)]
+        own = (lane >= c0) & (lane < c0 + MB)
+        both = jnp.where(own, jnp.where(lane == c0 + sub, 1.0, 0.0), tiles[g])
+        down = both
+        pivots = jnp.ones((MB, BK), jnp.float32)
+        scale = pivots
+        p = over_rows(cols[0], 0)
+        for k in range(MB):
+            r = inverse_of(p)
             pivots = jnp.where(sub == k, p, pivots)
-            inv.append(r)
-            rows.append(row)
-        unit = jnp.where(lane < c0 + sub, top, jnp.where(lane == c0 + sub, 1.0, 0.0))
-        w_ref[pl.ds(pl.multiple_of(first + c0, 8), 8), :] = unit * lax.rsqrt(pivots)
+            scale = jnp.where(sub == k, r, scale)
+            if k + 1 < MB and 1:
+                b = over_rows(cols[k], k + 1)
+                p = over_rows(cols[k + 1], k + 1) - (b * b) * r
+            m = jnp.where(sub == k, 0.0, cols[k] * r)
+            row = over_rows(both, k)
+            for k2 in range(k + 1, MB):
+                cols[k2] = cols[k2] - m * over_rows(cols[k2], k)
+            if k + 1 < MB and not 1:
+                p = over_rows(cols[k + 1], k + 1)
+            both = both - m * row
+            down = down - jnp.where(sub > k, m, 0.0) * row
+        w_ref[pl.ds(pl.multiple_of(first + c0, MB), MB), :] = (
+            jnp.where(lane < c0 + MB, down, 0.0) * lax.rsqrt(pivots))
+        both = both * scale
+        rows = [over_rows(both, k) for k in range(MB)]
         for i in range(g + 1, n):
-            tile = tiles[i]
-            cols = [over_lanes(tile, c0 + k) for k in range(8)]
-            for k in range(8):
-                m = cols[k] * inv[k]
-                for k2 in range(k + 1, 8):
-                    cols[k2] = cols[k2] - m * cross[k, k2]
-                tile = tile - m * rows[k]
+            tile = jnp.where(own, 0.0, tiles[i])
+            for k in range(MB):
+                tile = tile - over_lanes(tiles[i], c0 + k) * rows[k]
             tiles[i] = tile
 
 
@@ -124,7 +133,7 @@
 
     def step(j, carry):
         o = pl.multiple_of(j * BK, BK)
-        tiles = [a_ref[pl.ds(pl.multiple_of(o + 8 * i, 8), 8), pl.ds(o, BK)] for i in range(BK // 8)]
+        tiles = [a_ref[pl.ds(pl.multiple_of(o + MB * i, MB), MB), pl.ds(o, BK)] for i in range(BK // MB)]
         invert_factor(tiles, w_ref, o)
         for b in range(nb - 1):
             @pl.when(j == b)
@@ -140,14 +149,15 @@
     lax.fori_loop(0, nb, step, 0)
 
 
-def solve_kernel(first_ref, p0_ref, p1_ref, p2_ref, p3_ref, a_ref, w_ref, o_ref):
+def solve_kernel(first_ref, d0_ref, d1_ref, d2_ref, d3_ref, u0_ref, u1_ref, u2_ref, u3_ref, a_ref, w_ref, o_ref):
     nb = TOP // BK
-    total = (p0_ref[...] + p1_ref[...]) + (p2_ref[...] + p3_ref[...])
-    rows = total.shape[0]
+    dist = (d0_ref[...] + d1_ref[...]) + (d2_ref[...] + d3_ref[...])
+    update = (u0_ref[...] + u1_ref[...]) + (u2_ref[...] + u3_ref[...])
+    rows = dist.shape[0]
     pos = first_ref[0] + lax.broadcasted_iota(jnp.int32, (rows, TOP), 0)
     col = lax.broadcasted_iota(jnp.int32, (rows, TOP), 1)
     shift = jnp.where(pos == col, RIDGE, 0.0)
-    m = jnp.exp(total[:, :TOP] * (-1.0 / (2.0 * F))) + shift - total[:, TOP:]
+    m = jnp.exp(-dist / (2.0 * F)) + shift - update
     for b in range(nb):
         lo, hi = b * BK, (b + 1) * BK
         x = dot_t(m[:, :BK], w_ref[lo:hi, :])
@@ -172,7 +182,7 @@
     return pl.pallas_call(
         solve_kernel,
         out_shape=jax.ShapeDtypeStruct((parts[0].shape[0], TOP), jnp.float32),
-        in_specs=[pl.BlockSpec(memory_space=pltpu.SMEM)] + [vmem] * 6,
+        in_specs=[pl.BlockSpec(memory_space=pltpu.SMEM)] + [vmem] * (len(parts) + 2),
         out_specs=vmem,
     )(first, *parts, low, inverses)
 
@@ -198,8 +208,10 @@
     tiles = tiles.reshape(n_krow, 2, group, tiles.shape[-1])
     top = jnp.moveaxis(tiles, 1, 0).reshape(TOP, tiles.shape[-1])
     places = top[:, feat_dev + prior_dev:feat_dev + prior_dev + 2].astype(jnp.float32).astype(jnp.int32)
-    wanted = places[:, 0] * CODE + places[:, 1] + jnp.arange(TOP) // rows_dev * rows_dev
-    top_feats = rows_at(top[:, :feat_dev], wanted)
+    wanted = (places[:, :1] * CODE + places[:, 1:]).reshape(2, rows_dev, 1)
+    pick = (wanted == jnp.arange(rows_dev)).astype(jnp.bfloat16)
+    top_feats = jnp.einsum("bij,bjf->bif", pick, top[:, :feat_dev].reshape(2, rows_dev, feat_dev),
+                           preferred_element_type=jnp.float32).astype(jnp.bfloat16).reshape(TOP, feat_dev)
     top_slab = jnp.where(kept, top[:, feat_dev:feat_dev + prior_dev], jnp.zeros((), jnp.bfloat16))
     top_norms = sq_norms(top_feats)
 
@@ -242,19 +254,27 @@
         halves = [lax.dynamic_index_in_dim(array, which, 1, keepdims=False) for which in (1 - core, core)]
         return jnp.concatenate([h.reshape(pairs * own, *h.shape[2:]) for h in halves], axis=0)
 
+    def other_core(value):
+        return lax.ppermute(value, "col", [(c, c ^ 1) for c in range(n_col)])
+
+    def spread_over_pairs(value):
+        pieces = [lax.dynamic_index_in_dim(value, pair_at, 0, keepdims=False)]
+        for away in range(1, pairs):
+            piece = lax.dynamic_index_in_dim(value, (pair_at + away) % pairs, 0, keepdims=False)
+            to = [(c, (c // 2 + away) % pairs * 2 + c % 2) for c in range(n_col)]
+            pieces.append(lax.ppermute(piece, "col", to))
+        return pieces
+
+    half = pairs * own
+    update = inner(split_rows(slab), top_slab)
+    updates = (update[half:] + other_core(update[:half])).reshape(pairs, own, TOP)
+    updates = spread_over_pairs(updates)
+
     ordered = rows_at(arrived, split_rows(place_order[0]))
     dist = sq_norms(ordered)[:, None] + top_norms[None, :] - 2.0 * inner(ordered, top_feats)
-    update = inner(split_rows(slab), top_slab)
-    parts = jnp.concatenate([dist, update], axis=1)
-    half = pairs * own
-    got = lax.ppermute(parts[:half], "col", [(c, c ^ 1) for c in range(n_col)])
-    both_cores = (parts[half:] + got).reshape(pairs, own, 2 * TOP)
-    both_cores, entries = lax.optimization_barrier((both_cores, entries))
-    sums = [lax.dynamic_index_in_dim(both_cores, pair_at, 0, keepdims=False)]
-    for away in range(1, pairs):
-        piece = lax.dynamic_index_in_dim(both_cores, (pair_at + away) % pairs, 0, keepdims=False)
-        to = [(c, (c // 2 + away) % pairs * 2 + c % 2) for c in range(n_col)]
-        sums.append(lax.ppermute(piece, "col", to))
+    dists = (dist[half:] + other_core(dist[:half])).reshape(pairs, own, TOP)
+    dists, entries = lax.optimization_barrier((dists, entries))
+    dists = spread_over_pairs(dists)
 
     half_share = share // 2
     piece = lax.dynamic_slice_in_dim(entries, core * half_share, half_share, 0)
@@ -263,7 +283,7 @@
     other = lax.ppermute(mine, "col", [(c, c ^ 1) for c in range(n_col)])
     low, inverses = factor(core.reshape(1), mine, other)
     first_row = krow * rows_dev + col * own
-    return solve(first_row.reshape(1), sums, low, inverses)
+    return solve(first_row.reshape(1), dists + updates, low, inverses)
 
 
 def solution(mesh):

time: 215 us -> 238 us (1.11)
  the two profiles are of different devices: /device:TPU:2 before, /device:TPU:8 now
where the time goes in v4:
time: 238 us; the launch traced here: 237 us
  waiting for transfers between devices  98.3 us (41%)
  starting transfers between devices  51.9 us (22%)
  Pallas kernels  43.4 us (18%)
  local copies, waits for them, and re-layouts  20.8 us (9%)
  other arithmetic  14.9 us (6%)
  matrix products  6.24 us (3%)
    all_to_all x6, waiting for transfers between devices, swap(): return lax.all_to_all(value, axis, split_axis=0, concat_axis=0, tiled=True)  69.7 us
    all_to_all x6, starting transfers between devices, swap(): return lax.all_to_all(value, axis, split_axis=0, concat_axis=0, tiled=True)  37.2 us
    pallas_call x1, Pallas kernels, factor(): pl.pallas_call(factor_kernel, out_shape=(jax.ShapeDtypeStruct((TOP, TOP),...  34.9 us
    ppermute x6, waiting for transfers between devices, spread_over_pairs(): pieces.append(lax.ppermute(piece, 'col', to))  28.6 us
    ppermute x6, starting transfers between devices, spread_over_pairs(): pieces.append(lax.ppermute(piece, 'col', to))  14.6 us
    pallas_call x1, Pallas kernels, solve(): pl.pallas_call(solve_kernel, out_shape=jax.ShapeDtypeStruct((parts[0].sha...  8.46 us
    unnamed x36, local copies, waits for them, and re-layouts  5.14 us
    gather x2, local copies, waits for them, and re-layouts, rows_at(): return array.at[where].get(mode='promise_in_bounds', unique_indices=True)  4.76 us
  transfers between devices with their start and end apart: 15, of which 7 were waited for; matrix products, arithmetic and copies ran while one was open for 10% of the time, Pallas kernels for 15%

profile of v4, /device:TPU:8, one launch (start us, length us, event | category | flops | bytes accessed | tf_op | source)
XLA Modules:
  0.0 236.6 jit_solution(17152323639087182337)
XLA Ops:
  0.0 0.8 fusion.22
  1.0 1.8 fusion.6
  2.7 8.9 %all-to-all-start = ((bf16[32,16,384]{2,1,0:T(8,128)(2,1)}), bf16[32,16,384]{2,1,0:T(8,128)(2,1)S(1)}, u32[]{:S(2)}, u32[]{:S(2)}) async-start(bf16[32,16,384]{2,1,0:T(8,128)(2,1)} %bitcast.4), calls=%async_computation | async-start | bytes 786432 | tf_op jit(solution)/shard_map/all_to_all | solution.py:23
  12.2 1.3 reduce.7
  13.8 0.7 compare_select_fusion
  14.5 2.7 %gather_fusion = bf16[512,768]{1,0:T(8,128)(2,1)} fusion(bf16[512,768]{1,0:T(8,128)(2,1)S(1)} %copy-done, s32[1024]{0:T(1024)S(1)} %pad_clamp_fusion.1), kind=kCustom, calls=%fused_computation | custom fusion | bytes 1574912 | tf_op jit(solution)/shard_map/gather | solution.py:19
  17.2 0.8 slice.199
  18.0 3.0 %all-to-all-done = bf16[32,16,384]{2,1,0:T(8,128)(2,1)S(1)} async-done(((bf16[32,16,384]{2,1,0:T(8,128)(2,1)}), bf16[32,16,384]{2,1,0:T(8,128)(2,1)S(1)}, u32[]{:S(2)}, u32[]{:S(2)}) %all-to-all-start) | async-done | bytes 393248 | tf_op jit(solution)/shard_map/all_to_all | solution.py:23
  21.1 1.6 broadcast_in_dim.18
  22.7 5.3 %all-to-all-start.1 = ((bf16[32,32,1152]{2,1,0:T(8,128)(2,1)}), bf16[32,32,1152]{2,1,0:T(8,128)(2,1)S(1)}, u32[]{:S(2)}, u32[]{:S(2)}) async-start(bf16[32,32,1152]{2,1,0:T(8,128)(2,1)} %broadcast_in_dim.18), calls=%async_computation.1 | async-start | bytes 4718592 | tf_op jit(solution)/shard_map/all_to_all | solution.py:23
  30.0 28.8 %all-to-all-done.1 = bf16[32,32,1152]{2,1,0:T(8,128)(2,1)S(1)} async-done(((bf16[32,32,1152]{2,1,0:T(8,128)(2,1)}), bf16[32,32,1152]{2,1,0:T(8,128)(2,1)S(1)}, u32[]{:S(2)}, u32[]{:S(2)}) %all-to-all-start.1) | async-done | bytes 2359328 | tf_op jit(solution)/shard_map/all_to_all | solution.py:23
  59.1 1.3 copy-done.1
  60.5 1.3 slice.204
  61.7 6.7 %all-to-all-start.2 = ((bf16[32,16,768]{2,1,0:T(8,128)(2,1)}), bf16[32,16,768]{2,1,0:T(8,128)(2,1)S(1)}, u32[]{:S(2)}, u32[]{:S(2)}) async-start(bf16[32,16,768]{2,1,0:T(8,128)(2,1)} %bitcast.12), calls=%async_computation.2 | async-start | bytes 1572864 | tf_op jit(solution)/shard_map/all_to_all | solution.py:23
  68.4 1.1 slice_select_fusion
  69.9 2.6 %multiply_reduce_fusion = (f32[2,512]{1,0:T(2,128)S(1)}, bf16[2,512,768]{2,1,0:T(8,128)(2,1)S(1)}) fusion(bf16[2,512,768]{2,1,0:T(8,128)(2,1)} %bitcast.77, s32[2,512]{1,0:T(2,128)S(1)} %eq.51), kind=kOutput, calls=%fused_computation.2 | convolution fusion | flops 808975360 | bytes 3153920 | tf_op jit(solution)/shard_map/bij,bjf->bif/dot_general | solution.py:213
  73.6 6.5 %all-to-all-done.2 = bf16[32,16,768]{2,1,0:T(8,128)(2,1)S(1)} async-done(((bf16[32,16,768]{2,1,0:T(8,128)(2,1)}), bf16[32,16,768]{2,1,0:T(8,128)(2,1)S(1)}, u32[]{:S(2)}, u32[]{:S(2)}) %all-to-all-start.2) | async-done | bytes 786464 | tf_op jit(solution)/shard_map/all_to_all | solution.py:23
  80.1 2.0 gather_fusion.1
  82.4 2.4 %multiply_subtract_fusion = f32[512,1024]{1,0:T(8,128)S(1)} fusion(bf16[512,768]{1,0:T(8,128)(2,1)S(1)} %gather_fusion.1, bf16[1024,768]{1,0:T(8,128)(2,1)} %bitcast.76, f32[1024]{0:T(1024)S(1)} %bitcast.84, f32[512]{0:T(512)S(1)} %multiply_reduce_fusion.1), kind=kOutput, calls=%fused_computation.3 | convolution fusion | flops 806879232 | bytes 4462592 | tf_op jit(solution)/shard_map/dot_general | solution.py:35
  84.8 1.4 copy-done.3
  86.4 1.3 constant_dynamic-update-slice_fusion.12
  87.7 0.7 all_to_all.35
  88.4 7.7 %all-to-all-start.3 = ((f32[8,2,2304]{2,1,0:T(2,128)}), f32[8,2,2304]{2,1,0:T(2,128)S(1)}, u32[]{:S(2)}, u32[]{:S(2)}) async-start(f32[8,2,2304]{2,1,0:T(2,128)} %all_to_all.35), calls=%async_computation.3 | async-start | bytes 294912 | tf_op jit(solution)/shard_map/all_to_all | solution.py:23
  96.1 1.3 constant_dynamic-update-slice_fusion.11
  97.3 1.2 constant_dynamic-update-slice_fusion.10
  98.6 6.7 %all-to-all-done.3 = f32[8,2,2304]{2,1,0:T(2,128)S(1)} async-done(((f32[8,2,2304]{2,1,0:T(2,128)}), f32[8,2,2304]{2,1,0:T(2,128)S(1)}, u32[]{:S(2)}, u32[]{:S(2)}) %all-to-all-start.3) | async-done | bytes 147488 | tf_op jit(solution)/shard_map/all_to_all | solution.py:23
  105.3 0.7 reduce_sum.32
  106.0 0.7 slice_subtract_fusion
  106.7 0.7 broadcast_in_dim.34
  107.4 3.4 %all-to-all-start.4 = ((f32[8,2,1152]{2,1,0:T(2,128)}), f32[8,2,1152]{2,1,0:T(2,128)S(1)}, u32[]{:S(2)}, u32[]{:S(2)}) async-start(f32[8,2,1152]{2,1,0:T(2,128)} %broadcast_in_dim.34), calls=%async_computation.4 | async-start | bytes 147456 | tf_op jit(solution)/shard_map/all_to_all | solution.py:23
  110.8 8.6 %all-to-all-done.4 = f32[8,2,1152]{2,1,0:T(2,128)S(1)} async-done(((f32[8,2,1152]{2,1,0:T(2,128)}), f32[8,2,1152]{2,1,0:T(2,128)S(1)}, u32[]{:S(2)}, u32[]{:S(2)}) %all-to-all-start.4) | async-done | bytes 73760 | tf_op jit(solution)/shard_map/all_to_all | solution.py:23
  119.4 2.4 slice_add_fusion.1
  121.8 1.1 broadcast_in_dim.35
  122.9 5.4 %all-to-all-start.5 = ((f32[32,8,1152]{2,1,0:T(8,128)}), f32[32,8,1152]{2,1,0:T(8,128)}, u32[]{:S(2)}, u32[]{:S(2)}) async-start(f32[32,8,1152]{2,1,0:T(8,128)} %broadcast_in_dim.35), calls=%async_computation.5 | async-start | bytes 2359296 | tf_op jit(solution)/shard_map/all_to_all | solution.py:23
  128.8 1.0 slice.235
  129.9 15.9 %all-to-all-done.5.mine_ref = f32[32,8,1152]{2,1,0:T(8,128)} async-done(((f32[32,8,1152]{2,1,0:T(8,128)}), f32[32,8,1152]{2,1,0:T(8,128)}, u32[]{:S(2)}, u32[]{:S(2)}) %all-to-all-start.5) | async-done | bytes 1179680 | tf_op jit(solution)/shard_map/all_to_all | solution.py:23
  145.8 1.5 slice_add_fusion
  147.3 0.8 dynamic-slice_bitcast_fusion
  148.1 0.7 collective-permute-start.7
  148.8 4.0 %collective-permute-start.6 = (f32[64,1024]{1,0:T(8,128)S(1)}, f32[64,1024]{1,0:T(8,128)S(1)}, u32[]{:S(2)}, u32[]{:S(2)}) collective-permute-start(f32[64,1024]{1,0:T(8,128)S(1)} %get-tuple-element.26), channel_id=1, source_target_pairs={{0,4},{1,5},{2,6},{3,7},{4,0},{5,1},{6,2},{7,3},{8,12},{9,13},{10,... | collective-permute-start | bytes 786440 | tf_op jit(solution)/shard_map/ppermute | solution.py:265
  152.8 0.9 dynamic-slice_bitcast_fusion.4
  153.7 4.1 %collective-permute-start.3 = (f32[64,1024]{1,0:T(8,128)}, f32[64,1024]{1,0:T(8,128)S(1)}, u32[]{:S(2)}, u32[]{:S(2)}) collective-permute-start(f32[64,1024]{1,0:T(8,128)} %get-tuple-element.29), channel_id=1, source_target_pairs={{0,6},{1,7},{2,0},{3,1},{4,2},{5,3},{6,4},{7,5},{8,14},{9,15},{10,... | collective-permute-start | bytes 786440 | tf_op jit(solution)/shard_map/ppermute | solution.py:265
  157.8 28.6 %collective-permute-done.7.u3_ref = f32[64,1024]{1,0:T(8,128)S(1)} collective-permute-done((f32[64,1024]{1,0:T(8,128)S(1)}, f32[64,1024]{1,0:T(8,128)S(1)}, u32[]{:S(2)}, u32[]{:S(2)}) %collective-permute-start.7) | collective-permute-done | bytes 262176 | tf_op jit(solution)/shard_map/ppermute | solution.py:265
  186.4 2.4 %collective-permute-start.2 = (f32[64,1024]{1,0:T(8,128)S(1)}, f32[64,1024]{1,0:T(8,128)S(1)}, u32[]{:S(2)}, u32[]{:S(2)}) collective-permute-start(f32[64,1024]{1,0:T(8,128)S(1)} %get-tuple-element.30), channel_id=1, source_target_pairs={{0,4},{1,5},{2,6},{3,7},{4,0},{5,1},{6,2},{7,3},{8,12},{9,13},{10,... | collective-permute-start | bytes 786440 | tf_op jit(solution)/shard_map/ppermute | solution.py:265
  188.8 3.3 %collective-permute-start.1 = (f32[64,1024]{1,0:T(8,128)S(1)}, f32[64,1024]{1,0:T(8,128)S(1)}, u32[]{:S(2)}, u32[]{:S(2)}) collective-permute-start(f32[64,1024]{1,0:T(8,128)S(1)} %get-tuple-element.31), channel_id=1, source_target_pairs={{0,2},{1,3},{2,4},{3,5},{4,6},{5,7},{6,0},{7,1},{8,10},{9,11},{10,... | collective-permute-start | bytes 786440 | tf_op jit(solution)/shard_map/ppermute | solution.py:265
  192.1 34.9 %shard_map.55 = (f32[1024,1024]{1,0:T(8,128)}, f32[1024,128]{1,0:T(8,128)}) custom-call(s32[1]{0:T(128)} %bitcast.28.core_ref, f32[32,8,1152]{2,1,0:T(8,128)} %all-to-all-done.5.mine_ref, f32[32,8,1152]{2,1,0:T(8,128)} %collective-permute-done.8.other_ref), custom_call_target="tpu_custom_call" | custom-call | tf_op jit(solution)/shard_map/pallas_call | solution.py:172
  227.1 0.6 copy-done.7
  228.2 8.5 %shard_map.56 = f32[64,1024]{1,0:T(8,128)} custom-call(s32[1]{0:T(128)} %bitcast.first_ref, f32[64,1024]{1,0:T(8,128)} %get-tuple-element.32.d0_ref, f32[64,1024]{1,0:T(8,128)} %copy-done.11, f32[64,1024]{1,0:T(8,128)} %copy-done.10, f32[64,1024]{1,0:T(8,128)} %copy-done.9, f32[64,1024]{1,0:T(8,128)} %get-tuple-element.28.u0_ref, f32[64,1024]{1,0:T(8,128)} %copy-done.8, ...), custom_call_target="tpu_custom_call" | custom-call | tf_op jit(solution)/shard_map/pallas_call | solution.py:182
  (84 shorter events, 5.5 us)
Async XLA Ops:
  0.0 14.5 %copy-start = (bf16[512,768]{1,0:T(8,128)(2,1)S(1)}, bf16[512,768]{1,0:T(8,128)(2,1)}, u32[]{:S(2)}) copy-start(bf16[512,768]{1,0:T(8,128)(2,1)} %param.5) | copy-start | bytes 2359300
  2.7 18.3 %all-to-all-start = ((bf16[32,16,384]{2,1,0:T(8,128)(2,1)}), bf16[32,16,384]{2,1,0:T(8,128)(2,1)S(1)}, u32[]{:S(2)}, u32[]{:S(2)}) async-start(bf16[32,16,384]{2,1,0:T(8,128)(2,1)} %bitcast.4), calls=%async_computation | async-start | bytes 786432 | tf_op jit(solution)/shard_map/all_to_all | solution.py:23
  22.7 36.2 %all-to-all-start.1 = ((bf16[32,32,1152]{2,1,0:T(8,128)(2,1)}), bf16[32,32,1152]{2,1,0:T(8,128)(2,1)S(1)}, u32[]{:S(2)}, u32[]{:S(2)}) async-start(bf16[32,32,1152]{2,1,0:T(8,128)(2,1)} %broadcast_in_dim.18), calls=%async_computation.1 | async-start | bytes 4718592 | tf_op jit(solution)/shard_map/all_to_all | solution.py:23
  28.8 0.7 copy-start.13
  28.8 0.6 copy-start.12
  59.0 1.4 copy-start.1
  61.7 18.4 %all-to-all-start.2 = ((bf16[32,16,768]{2,1,0:T(8,128)(2,1)}), bf16[32,16,768]{2,1,0:T(8,128)(2,1)S(1)}, u32[]{:S(2)}, u32[]{:S(2)}) async-start(bf16[32,16,768]{2,1,0:T(8,128)(2,1)} %bitcast.12), calls=%async_computation.2 | async-start | bytes 1572864 | tf_op jit(solution)/shard_map/all_to_all | solution.py:23
  72.4 1.2 copy-start.4
  84.8 1.4 copy-start.3
  86.3 33.1 %collective-permute-start = (f32[256,1024]{1,0:T(8,128)S(1)}, f32[256,1024]{1,0:T(8,128)S(1)}, u32[]{:S(2)}, u32[]{:S(2)}) collective-permute-start(f32[256,1024]{1,0:T(8,128)S(1)} %slice.223), channel_id=1, source_target_pairs={{0,1},{1,0},{2,3},{3,2},{4,5},{5,4},{6,7},{7,6},{8,9},{9,8},{10,11... | collective-permute-start | bytes 3145736 | tf_op jit(solution)/shard_map/ppermute | solution.py:258
  88.4 16.9 %all-to-all-start.3 = ((f32[8,2,2304]{2,1,0:T(2,128)}), f32[8,2,2304]{2,1,0:T(2,128)S(1)}, u32[]{:S(2)}, u32[]{:S(2)}) async-start(f32[8,2,2304]{2,1,0:T(2,128)} %all_to_all.35), calls=%async_computation.3 | async-start | bytes 294912 | tf_op jit(solution)/shard_map/all_to_all | solution.py:23
  107.4 12.0 %all-to-all-start.4 = ((f32[8,2,1152]{2,1,0:T(2,128)}), f32[8,2,1152]{2,1,0:T(2,128)S(1)}, u32[]{:S(2)}, u32[]{:S(2)}) async-start(f32[8,2,1152]{2,1,0:T(2,128)} %broadcast_in_dim.34), calls=%async_computation.4 | async-start | bytes 147456 | tf_op jit(solution)/shard_map/all_to_all | solution.py:23
  121.8 6.5 %copy-start.5 = (bf16[512,256]{1,0:T(8,128)(2,1)S(1)}, bf16[512,256]{1,0:T(8,128)(2,1)}, u32[]{:S(2)}) copy-start(bf16[512,256]{1,0:T(8,128)(2,1)} %param.6) | copy-start | bytes 786436
  122.9 22.9 %all-to-all-start.5 = ((f32[32,8,1152]{2,1,0:T(8,128)}), f32[32,8,1152]{2,1,0:T(8,128)}, u32[]{:S(2)}, u32[]{:S(2)}) async-start(f32[32,8,1152]{2,1,0:T(8,128)} %broadcast_in_dim.35), calls=%async_computation.5 | async-start | bytes 2359296 | tf_op jit(solution)/shard_map/all_to_all | solution.py:23
  129.9 15.9 %collective-permute-start.4 = (f32[256,1024]{1,0:T(8,128)}, f32[256,1024]{1,0:T(8,128)}, u32[]{:S(2)}, u32[]{:S(2)}) collective-permute-start(f32[256,1024]{1,0:T(8,128)} %slice.235), channel_id=1, source_target_pairs={{0,1},{1,0},{2,3},{3,2},{4,5},{5,4},{6,7},{7,6},{8,9},{9,8},{10,11... | collective-permute-start | bytes 3145736 | tf_op jit(solution)/shard_map/ppermute | solution.py:258
  145.8 43.0 %collective-permute-start.8 = (f32[32,8,1152]{2,1,0:T(8,128)}, f32[32,8,1152]{2,1,0:T(8,128)}, u32[]{:S(2)}, u32[]{:S(2)}) collective-permute-start(f32[32,8,1152]{2,1,0:T(8,128)} %all-to-all-done.5.mine_ref), channel_id=1, source_target_pairs={{0,1},{1,0},{2,3},{3,2},{4,5},{5,4},{6,7},{7,6},{8,9},{9,8},{10,11... | collective-permute-start | bytes 3538952 | tf_op jit(solution)/shard_map/ppermute | solution.py:283
  145.8 7.0 %copy-start.2 = (f32[256,1024]{1,0:T(8,128)S(1)}, f32[256,1024]{1,0:T(8,128)}, u32[]{:S(2)}) copy-start(f32[256,1024]{1,0:T(8,128)} %slice_add_fusion.1) | copy-start | bytes 3145732
  148.1 38.3 %collective-permute-start.7 = (f32[64,1024]{1,0:T(8,128)S(1)}, f32[64,1024]{1,0:T(8,128)S(1)}, u32[]{:S(2)}, u32[]{:S(2)}) collective-permute-start(f32[64,1024]{1,0:T(8,128)S(1)} %get-tuple-element.25), channel_id=1, source_target_pairs={{0,6},{1,7},{2,0},{3,1},{4,2},{5,3},{6,4},{7,5},{8,14},{9,15},{10,... | collective-permute-start | bytes 786440 | tf_op jit(solution)/shard_map/ppermute | solution.py:265
  148.8 78.3 %collective-permute-start.6 = (f32[64,1024]{1,0:T(8,128)S(1)}, f32[64,1024]{1,0:T(8,128)S(1)}, u32[]{:S(2)}, u32[]{:S(2)}) collective-permute-start(f32[64,1024]{1,0:T(8,128)S(1)} %get-tuple-element.26), channel_id=1, source_target_pairs={{0,4},{1,5},{2,6},{3,7},{4,0},{5,1},{6,2},{7,3},{8,12},{9,13},{10,... | collective-permute-start | bytes 786440 | tf_op jit(solution)/shard_map/ppermute | solution.py:265
  152.8 74.2 %collective-permute-start.5 = (f32[64,1024]{1,0:T(8,128)S(1)}, f32[64,1024]{1,0:T(8,128)S(1)}, u32[]{:S(2)}, u32[]{:S(2)}) collective-permute-start(f32[64,1024]{1,0:T(8,128)S(1)} %get-tuple-element.27), channel_id=1, source_target_pairs={{0,2},{1,3},{2,4},{3,5},{4,6},{5,7},{6,0},{7,1},{8,10},{9,11},{10,... | collective-permute-start | bytes 786440 | tf_op jit(solution)/shard_map/ppermute | solution.py:265
  153.7 73.4 %collective-permute-start.3 = (f32[64,1024]{1,0:T(8,128)}, f32[64,1024]{1,0:T(8,128)S(1)}, u32[]{:S(2)}, u32[]{:S(2)}) collective-permute-start(f32[64,1024]{1,0:T(8,128)} %get-tuple-element.29), channel_id=1, source_target_pairs={{0,6},{1,7},{2,0},{3,1},{4,2},{5,3},{6,4},{7,5},{8,14},{9,15},{10,... | collective-permute-start | bytes 786440 | tf_op jit(solution)/shard_map/ppermute | solution.py:265
  186.4 40.7 %copy-start.6 = (f32[64,1024]{1,0:T(8,128)}, f32[64,1024]{1,0:T(8,128)S(1)}, u32[]{:S(2)}) copy-start(f32[64,1024]{1,0:T(8,128)S(1)} %collective-permute-done.7.u3_ref) | copy-start | bytes 786436
  186.4 40.7 %collective-permute-start.2 = (f32[64,1024]{1,0:T(8,128)S(1)}, f32[64,1024]{1,0:T(8,128)S(1)}, u32[]{:S(2)}, u32[]{:S(2)}) collective-permute-start(f32[64,1024]{1,0:T(8,128)S(1)} %get-tuple-element.30), channel_id=1, source_target_pairs={{0,4},{1,5},{2,6},{3,7},{4,0},{5,1},{6,2},{7,3},{8,12},{9,13},{10,... | collective-permute-start | bytes 786440 | tf_op jit(solution)/shard_map/ppermute | solution.py:265
  188.8 38.3 %collective-permute-start.1 = (f32[64,1024]{1,0:T(8,128)S(1)}, f32[64,1024]{1,0:T(8,128)S(1)}, u32[]{:S(2)}, u32[]{:S(2)}) collective-permute-start(f32[64,1024]{1,0:T(8,128)S(1)} %get-tuple-element.31), channel_id=1, source_target_pairs={{0,2},{1,3},{2,4},{3,5},{4,6},{5,7},{6,0},{7,1},{8,10},{9,11},{10,... | collective-permute-start | bytes 786440 | tf_op jit(solution)/shard_map/ppermute | solution.py:265
  227.0 0.7 copy-start.7
  227.1 0.8 copy-start.8
  227.1 0.9 copy-start.9
  227.1 1.0 copy-start.10
  227.1 1.0 copy-start.11

commit v5 on v4

--- a/solution.py
+++ b/solution.py
@@ -198,12 +198,12 @@
     order = place_order[0]
     coded = jnp.stack([order // CODE, order % CODE], axis=1).astype(jnp.bfloat16)
     coded = jnp.pad(coded, ((0, 0), (0, BK - 2)))
-    slab_part = swap(jnp.concatenate([slab, coded], axis=1), "krow")[:2 * group]
     packed = rows_at(features, pack_order[0])
     feat_dev = packed.shape[1]
-    tiles = from_everyone(jnp.concatenate([packed[:2 * group], slab_part], axis=1), "krow")
-    packed, tiles = lax.optimization_barrier((packed, tiles))
-    arrived = swap(packed, "krow")
+    arrived = swap(jnp.concatenate([packed, slab, coded], axis=1), "krow")
+    mine = jnp.concatenate([packed[:2 * group], arrived[:2 * group, feat_dev:]], axis=1)
+    arrived = arrived[:, :feat_dev]
+    tiles = from_everyone(mine, "krow")
 
     tiles = tiles.reshape(n_krow, 2, group, tiles.shape[-1])
     top = jnp.moveaxis(tiles, 1, 0).reshape(TOP, tiles.shape[-1])
@@ -233,7 +233,6 @@
     dist = fold(dist[:share], dist[share:], pair)
     update = fold(update[:share], update[share:], pair)
     parts = jnp.concatenate([dist, update], axis=1)
-    parts, arrived = lax.optimization_barrier((parts, arrived))
     parts = swap(parts, "col")
     summed = jnp.sum(parts.reshape(n_col, share // n_col, 2 * 9 * BK), axis=0)
     dist, update = summed[:, :9 * BK], summed[:, 9 * BK:]
@@ -243,7 +242,8 @@
     shift = fold((row_hi + ids == col_ids).astype(jnp.float32),
                  (row_lo + ids == col_ids).astype(jnp.float32), pair)
     entries = jnp.exp(-dist / (2.0 * F)) + RIDGE * shift - update
-    entries = from_everyone(entries, "col").reshape(share, 9 * BK)
+    entries = from_everyone(entries, "col")
+    entries = entries.reshape(share, 9 * BK)
 
     core, pair_at = col % 2, col // 2
     pairs = n_col // 2
@@ -273,7 +273,6 @@
     ordered = rows_at(arrived, split_rows(place_order[0]))
     dist = sq_norms(ordered)[:, None] + top_norms[None, :] - 2.0 * inner(ordered, top_feats)
     dists = (dist[half:] + other_core(dist[:half])).reshape(pairs, own, TOP)
-    dists, entries = lax.optimization_barrier((dists, entries))
     dists = spread_over_pairs(dists)
 
     half_share = share // 2

time: 238 us -> 221 us (0.929)
  other arithmetic: 14.9 us -> 8.05 us
  starting transfers between devices: 51.9 us -> 46.1 us
  local copies, waits for them, and re-layouts: 20.8 us -> 15.8 us
  waiting for transfers between devices: 98.3 us -> 101 us
    all_to_all x6 -> x5, starting transfers between devices: 37.2 us -> 31.6 us  [swap(): return lax.all_to_all(value, axis, split_axis=0, concat_axis=0, tiled=True)]
    all_to_all x6 -> x5, waiting for transfers between devices: 69.7 us -> 73.2 us  [swap(): return lax.all_to_all(value, axis, split_axis=0, concat_axis=0, tiled=True)]
    unnamed x10, other arithmetic: 4.48 us -> 1.4 us
    unnamed x36 -> x31, local copies, waits for them, and re-layouts: 5.14 us -> 2.56 us
  transfers between devices with their start and end apart: 15 -> 14, of which waited for: 7 -> 6; matrix products, arithmetic and copies ran while one was open for 10% -> 6% of each run, Pallas kernels for 15% -> 16%
where the time goes in v5:
time: 221 us; the launch traced here: 220 us
  waiting for transfers between devices  101 us (46%)
  starting transfers between devices  46.1 us (21%)
  Pallas kernels  43.4 us (20%)
  local copies, waits for them, and re-layouts  15.8 us (7%)
  other arithmetic  8.05 us (4%)
  matrix products  4.85 us (2%)
    all_to_all x5, waiting for transfers between devices, swap(): return lax.all_to_all(value, axis, split_axis=0, concat_axis=0, tiled=True)  73.2 us
    pallas_call x1, Pallas kernels, factor(): pl.pallas_call(factor_kernel, out_shape=(jax.ShapeDtypeStruct((TOP, TOP),...  34.9 us
    all_to_all x5, starting transfers between devices, swap(): return lax.all_to_all(value, axis, split_axis=0, concat_axis=0, tiled=True)  31.6 us
    ppermute x6, waiting for transfers between devices, spread_over_pairs(): pieces.append(lax.ppermute(piece, 'col', to))  27.9 us
    ppermute x6, starting transfers between devices, spread_over_pairs(): pieces.append(lax.ppermute(piece, 'col', to))  14 us
    pallas_call x1, Pallas kernels, solve(): pl.pallas_call(solve_kernel, out_shape=jax.ShapeDtypeStruct((parts[0].sha...  8.46 us
  transfers between devices with their start and end apart: 14, of which 6 were waited for; matrix products, arithmetic and copies ran while one was open for 6% of the time, Pallas kernels for 16%

profile of v5, /device:TPU:8, one launch (start us, length us, event | category | flops | bytes accessed | tf_op | source)
XLA Modules:
  0.0 220.5 jit_solution(15923273144182099180)
XLA Ops:
  0.0 0.8 fusion.22
  0.8 0.5 broadcast.185
  1.3 1.3 reduce.7
  2.9 0.7 compare_select_fusion
  3.6 0.2 copy.32
  3.8 2.0 gather_fusion
  5.9 1.1 fusion.3
  7.0 8.9 %all-to-all-start = ((bf16[32,16,1152]{2,1,0:T(8,128)(2,1)}), bf16[32,16,1152]{2,1,0:T(8,128)(2,1)S(1)}, u32[]{:S(2)}, u32[]{:S(2)}) async-start(bf16[32,16,1152]{2,1,0:T(8,128)(2,1)} %bitcast.4), calls=%async_computation | async-start | bytes 2359296 | tf_op jit(solution)/shard_map/all_to_all | solution.py:23
  15.9 17.5 %all-to-all-done = bf16[32,16,1152]{2,1,0:T(8,128)(2,1)S(1)} async-done(((bf16[32,16,1152]{2,1,0:T(8,128)(2,1)}), bf16[32,16,1152]{2,1,0:T(8,128)(2,1)S(1)}, u32[]{:S(2)}, u32[]{:S(2)}) %all-to-all-start) | async-done | bytes 1179680 | tf_op jit(solution)/shard_map/all_to_all | solution.py:23
  33.4 1.7 broadcast_in_dim.18
  35.2 5.2 %all-to-all-start.1 = ((bf16[32,32,1152]{2,1,0:T(8,128)(2,1)}), bf16[32,32,1152]{2,1,0:T(8,128)(2,1)S(1)}, u32[]{:S(2)}, u32[]{:S(2)}) async-start(bf16[32,32,1152]{2,1,0:T(8,128)(2,1)} %broadcast_in_dim.18), calls=%async_computation.1 | async-start | bytes 4718592 | tf_op jit(solution)/shard_map/all_to_all | solution.py:23
  41.3 28.7 %all-to-all-done.1 = bf16[32,32,1152]{2,1,0:T(8,128)(2,1)S(1)} async-done(((bf16[32,32,1152]{2,1,0:T(8,128)(2,1)}), bf16[32,32,1152]{2,1,0:T(8,128)(2,1)S(1)}, u32[]{:S(2)}, u32[]{:S(2)}) %all-to-all-start.1) | async-done | bytes 2359328 | tf_op jit(solution)/shard_map/all_to_all | solution.py:23
  70.0 0.2 copy.35
  70.4 0.4 fusion.6
  70.8 1.2 multiply_reduce_fusion
  72.2 1.0 copy-done.4
  73.2 0.6 fusion.4
  73.8 0.2 fusion.14
  74.1 0.7 all_to_all.27
  74.9 7.6 %all-to-all-start.2 = ((f32[8,2,2304]{2,1,0:T(2,128)}), f32[8,2,2304]{2,1,0:T(2,128)S(1)}, u32[]{:S(2)}, u32[]{:S(2)}) async-start(f32[8,2,2304]{2,1,0:T(2,128)} %all_to_all.27), calls=%async_computation.2 | async-start | bytes 294912 | tf_op jit(solution)/shard_map/all_to_all | solution.py:23
  82.5 9.2 %all-to-all-done.2 = f32[8,2,2304]{2,1,0:T(2,128)S(1)} async-done(((f32[8,2,2304]{2,1,0:T(2,128)}), f32[8,2,2304]{2,1,0:T(2,128)S(1)}, u32[]{:S(2)}, u32[]{:S(2)}) %all-to-all-start.2) | async-done | bytes 147488 | tf_op jit(solution)/shard_map/all_to_all | solution.py:23
  91.8 0.7 broadcast_in_dim.34
  92.4 3.4 %all-to-all-start.3 = ((f32[8,2,1152]{2,1,0:T(2,128)}), f32[8,2,1152]{2,1,0:T(2,128)S(1)}, u32[]{:S(2)}, u32[]{:S(2)}) async-start(f32[8,2,1152]{2,1,0:T(2,128)} %broadcast_in_dim.34), calls=%async_computation.3 | async-start | bytes 147456 | tf_op jit(solution)/shard_map/all_to_all | solution.py:23
  95.8 8.6 %all-to-all-done.3 = f32[8,2,1152]{2,1,0:T(2,128)S(1)} async-done(((f32[8,2,1152]{2,1,0:T(2,128)}), f32[8,2,1152]{2,1,0:T(2,128)S(1)}, u32[]{:S(2)}, u32[]{:S(2)}) %all-to-all-start.3) | async-done | bytes 73760 | tf_op jit(solution)/shard_map/all_to_all | solution.py:23
  104.5 1.1 broadcast_in_dim.35
  105.6 6.5 %all-to-all-start.4 = ((f32[32,8,1152]{2,1,0:T(8,128)}), f32[32,8,1152]{2,1,0:T(8,128)}, u32[]{:S(2)}, u32[]{:S(2)}) async-start(f32[32,8,1152]{2,1,0:T(8,128)} %broadcast_in_dim.35), calls=%async_computation.4 | async-start | bytes 2359296 | tf_op jit(solution)/shard_map/all_to_all | solution.py:23
  112.2 2.0 gather_fusion.1
  114.2 0.2 multiply_reduce_fusion.1
  114.5 2.4 %multiply_subtract_fusion = f32[512,1024]{1,0:T(8,128)S(1)} fusion(bf16[512,768]{1,0:T(8,128)(2,1)S(1)} %gather_fusion.1, bf16[1024,768]{1,0:T(8,128)(2,1)} %bitcast.75, f32[1024]{0:T(1024)S(1)} %bitcast.82, f32[512]{0:T(512)S(1)} %multiply_reduce_fusion.1), kind=kOutput, calls=%fused_computation.5 | convolution fusion | flops 806879232 | bytes 4462592 | tf_op jit(solution)/shard_map/dot_general | solution.py:35
  116.9 1.1 slice.207
  118.1 0.5 fusion.7
  118.6 1.1 slice.210
  119.7 0.5 collective-permute-start.4
  120.1 9.2 %all-to-all-done.4.mine_ref = f32[32,8,1152]{2,1,0:T(8,128)} async-done(((f32[32,8,1152]{2,1,0:T(8,128)}), f32[32,8,1152]{2,1,0:T(8,128)}, u32[]{:S(2)}, u32[]{:S(2)}) %all-to-all-start.4) | async-done | bytes 1179680 | tf_op jit(solution)/shard_map/all_to_all | solution.py:23
  129.3 1.7 slice_add_fusion.1
  131.0 0.9 dynamic-slice_bitcast_fusion.4
  131.9 0.6 collective-permute-start.3
  132.6 3.6 %collective-permute-start.2 = (f32[64,1024]{1,0:T(8,128)}, f32[64,1024]{1,0:T(8,128)S(1)}, u32[]{:S(2)}, u32[]{:S(2)}) collective-permute-start(f32[64,1024]{1,0:T(8,128)} %get-tuple-element.18), channel_id=1, source_target_pairs={{0,4},{1,5},{2,6},{3,7},{4,0},{5,1},{6,2},{7,3},{8,12},{9,13},{10,... | collective-permute-start | bytes 786440 | tf_op jit(solution)/shard_map/ppermute | solution.py:265
  136.2 1.4 slice_add_fusion
  137.6 0.8 dynamic-slice_bitcast_fusion
  138.4 4.1 %collective-permute-start.7 = (f32[64,1024]{1,0:T(8,128)S(1)}, f32[64,1024]{1,0:T(8,128)S(1)}, u32[]{:S(2)}, u32[]{:S(2)}) collective-permute-start(f32[64,1024]{1,0:T(8,128)S(1)} %get-tuple-element.13), channel_id=1, source_target_pairs={{0,6},{1,7},{2,0},{3,1},{4,2},{5,3},{6,4},{7,5},{8,14},{9,15},{10,... | collective-permute-start | bytes 786440 | tf_op jit(solution)/shard_map/ppermute | solution.py:265
  142.5 27.9 %collective-permute-done.3.d3_ref = f32[64,1024]{1,0:T(8,128)S(1)} collective-permute-done((f32[64,1024]{1,0:T(8,128)S(1)}, f32[64,1024]{1,0:T(8,128)S(1)}, u32[]{:S(2)}, u32[]{:S(2)}) %collective-permute-start.3) | collective-permute-done | bytes 262176 | tf_op jit(solution)/shard_map/ppermute | solution.py:265
  170.4 1.8 collective-permute-start.6
  172.2 3.9 %collective-permute-start.5 = (f32[64,1024]{1,0:T(8,128)S(1)}, f32[64,1024]{1,0:T(8,128)S(1)}, u32[]{:S(2)}, u32[]{:S(2)}) collective-permute-start(f32[64,1024]{1,0:T(8,128)S(1)} %get-tuple-element.15), channel_id=1, source_target_pairs={{0,2},{1,3},{2,4},{3,5},{4,6},{5,7},{6,0},{7,1},{8,10},{9,11},{10,... | collective-permute-start | bytes 786440 | tf_op jit(solution)/shard_map/ppermute | solution.py:265
  176.1 34.9 %shard_map.55 = (f32[1024,1024]{1,0:T(8,128)}, f32[1024,128]{1,0:T(8,128)}) custom-call(s32[1]{0:T(128)} %bitcast.26.core_ref, f32[32,8,1152]{2,1,0:T(8,128)} %all-to-all-done.4.mine_ref, f32[32,8,1152]{2,1,0:T(8,128)} %collective-permute-done.8.other_ref), custom_call_target="tpu_custom_call" | custom-call | tf_op jit(solution)/shard_map/pallas_call | solution.py:172
  211.1 0.6 copy-done.8
  211.7 0.1 copy-done.9
  212.0 8.5 %shard_map.56 = f32[64,1024]{1,0:T(8,128)} custom-call(s32[1]{0:T(128)} %bitcast.first_ref, f32[64,1024]{1,0:T(8,128)} %get-tuple-element.20.d0_ref, f32[64,1024]{1,0:T(8,128)} %collective-permute-done.1.d1_ref, f32[64,1024]{1,0:T(8,128)} %copy-done.8, f32[64,1024]{1,0:T(8,128)} %copy-done.7, f32[64,1024]{1,0:T(8,128)} %get-tuple-element.16.u0_ref, ...), custom_call_target="tpu_custom_call" | custom-call | tf_op jit(solution)/shard_map/pallas_call | solution.py:182
  (79 shorter events, 1.5 us)
Async XLA Ops:
  0.0 3.8 %copy-start = (bf16[512,768]{1,0:T(8,128)(2,1)S(1)}, bf16[512,768]{1,0:T(8,128)(2,1)}, u32[]{:S(2)}) copy-start(bf16[512,768]{1,0:T(8,128)(2,1)} %param.5) | copy-start | bytes 2359300
  3.8 2.0 copy-start.5
  7.0 26.4 %all-to-all-start = ((bf16[32,16,1152]{2,1,0:T(8,128)(2,1)}), bf16[32,16,1152]{2,1,0:T(8,128)(2,1)S(1)}, u32[]{:S(2)}, u32[]{:S(2)}) async-start(bf16[32,16,1152]{2,1,0:T(8,128)(2,1)} %bitcast.4), calls=%async_computation | async-start | bytes 2359296 | tf_op jit(solution)/shard_map/all_to_all | solution.py:23
  33.4 1.8 copy-start.1
  35.2 34.9 %all-to-all-start.1 = ((bf16[32,32,1152]{2,1,0:T(8,128)(2,1)}), bf16[32,32,1152]{2,1,0:T(8,128)(2,1)S(1)}, u32[]{:S(2)}, u32[]{:S(2)}) async-start(bf16[32,32,1152]{2,1,0:T(8,128)(2,1)} %broadcast_in_dim.18), calls=%async_computation.1 | async-start | bytes 4718592 | tf_op jit(solution)/shard_map/all_to_all | solution.py:23
  72.0 1.2 copy-start.4
  74.9 16.8 %all-to-all-start.2 = ((f32[8,2,2304]{2,1,0:T(2,128)}), f32[8,2,2304]{2,1,0:T(2,128)S(1)}, u32[]{:S(2)}, u32[]{:S(2)}) async-start(f32[8,2,2304]{2,1,0:T(2,128)} %all_to_all.27), calls=%async_computation.2 | async-start | bytes 294912 | tf_op jit(solution)/shard_map/all_to_all | solution.py:23
  82.4 29.7 %copy-start.2 = (bf16[32,16,1152]{2,1,0:T(8,128)(2,1)S(1)}, bf16[32,16,1152]{2,1,0:T(8,128)(2,1)}, u32[]{:S(2)}) copy-start(bf16[32,16,1152]{2,1,0:T(8,128)(2,1)} %copy-done.1) | copy-start | bytes 3538948
  92.4 12.0 %all-to-all-start.3 = ((f32[8,2,1152]{2,1,0:T(2,128)}), f32[8,2,1152]{2,1,0:T(2,128)S(1)}, u32[]{:S(2)}, u32[]{:S(2)}) async-start(f32[8,2,1152]{2,1,0:T(2,128)} %broadcast_in_dim.34), calls=%async_computation.3 | async-start | bytes 147456 | tf_op jit(solution)/shard_map/all_to_all | solution.py:23
  105.6 23.8 %all-to-all-start.4 = ((f32[32,8,1152]{2,1,0:T(8,128)}), f32[32,8,1152]{2,1,0:T(8,128)}, u32[]{:S(2)}, u32[]{:S(2)}) async-start(f32[32,8,1152]{2,1,0:T(8,128)} %broadcast_in_dim.35), calls=%async_computation.4 | async-start | bytes 2359296 | tf_op jit(solution)/shard_map/all_to_all | solution.py:23
  116.9 1.7 copy-start.3
  116.9 1.2 copy-start.6
  118.1 11.3 %collective-permute-start = (f32[256,1024]{1,0:T(8,128)}, f32[256,1024]{1,0:T(8,128)}, u32[]{:S(2)}, u32[]{:S(2)}) collective-permute-start(f32[256,1024]{1,0:T(8,128)} %slice.207), channel_id=1, source_target_pairs={{0,1},{1,0},{2,3},{3,2},{4,5},{5,4},{6,7},{7,6},{8,9},{9,8},{10,11... | collective-permute-start | bytes 3145736 | tf_op jit(solution)/shard_map/ppermute | solution.py:258
  119.7 16.5 %collective-permute-start.4 = (f32[256,1024]{1,0:T(8,128)}, f32[256,1024]{1,0:T(8,128)}, u32[]{:S(2)}, u32[]{:S(2)}) collective-permute-start(f32[256,1024]{1,0:T(8,128)} %slice.210), channel_id=1, source_target_pairs={{0,1},{1,0},{2,3},{3,2},{4,5},{5,4},{6,7},{7,6},{8,9},{9,8},{10,11... | collective-permute-start | bytes 3145736 | tf_op jit(solution)/shard_map/ppermute | solution.py:258
  129.3 42.9 %collective-permute-start.8 = (f32[32,8,1152]{2,1,0:T(8,128)}, f32[32,8,1152]{2,1,0:T(8,128)}, u32[]{:S(2)}, u32[]{:S(2)}) collective-permute-start(f32[32,8,1152]{2,1,0:T(8,128)} %all-to-all-done.4.mine_ref), channel_id=1, source_target_pairs={{0,1},{1,0},{2,3},{3,2},{4,5},{5,4},{6,7},{7,6},{8,9},{9,8},{10,11... | collective-permute-start | bytes 3538952 | tf_op jit(solution)/shard_map/ppermute | solution.py:282
  131.9 38.5 %collective-permute-start.3 = (f32[64,1024]{1,0:T(8,128)S(1)}, f32[64,1024]{1,0:T(8,128)S(1)}, u32[]{:S(2)}, u32[]{:S(2)}) collective-permute-start(f32[64,1024]{1,0:T(8,128)S(1)} %get-tuple-element.17), channel_id=1, source_target_pairs={{0,6},{1,7},{2,0},{3,1},{4,2},{5,3},{6,4},{7,5},{8,14},{9,15},{10,... | collective-permute-start | bytes 786440 | tf_op jit(solution)/shard_map/ppermute | solution.py:265
  132.6 78.4 %collective-permute-start.2 = (f32[64,1024]{1,0:T(8,128)}, f32[64,1024]{1,0:T(8,128)S(1)}, u32[]{:S(2)}, u32[]{:S(2)}) collective-permute-start(f32[64,1024]{1,0:T(8,128)} %get-tuple-element.18), channel_id=1, source_target_pairs={{0,4},{1,5},{2,6},{3,7},{4,0},{5,1},{6,2},{7,3},{8,12},{9,13},{10,... | collective-permute-start | bytes 786440 | tf_op jit(solution)/shard_map/ppermute | solution.py:265
  136.2 74.8 %collective-permute-start.1 = (f32[64,1024]{1,0:T(8,128)}, f32[64,1024]{1,0:T(8,128)}, u32[]{:S(2)}, u32[]{:S(2)}) collective-permute-start(f32[64,1024]{1,0:T(8,128)} %get-tuple-element.19), channel_id=1, source_target_pairs={{0,2},{1,3},{2,4},{3,5},{4,6},{5,7},{6,0},{7,1},{8,10},{9,11},{10,... | collective-permute-start | bytes 786440 | tf_op jit(solution)/shard_map/ppermute | solution.py:265
  138.4 72.6 %collective-permute-start.7 = (f32[64,1024]{1,0:T(8,128)S(1)}, f32[64,1024]{1,0:T(8,128)S(1)}, u32[]{:S(2)}, u32[]{:S(2)}) collective-permute-start(f32[64,1024]{1,0:T(8,128)S(1)} %get-tuple-element.13), channel_id=1, source_target_pairs={{0,6},{1,7},{2,0},{3,1},{4,2},{5,3},{6,4},{7,5},{8,14},{9,15},{10,... | collective-permute-start | bytes 786440 | tf_op jit(solution)/shard_map/ppermute | solution.py:265
  170.4 40.7 %copy-start.7 = (f32[64,1024]{1,0:T(8,128)}, f32[64,1024]{1,0:T(8,128)S(1)}, u32[]{:S(2)}) copy-start(f32[64,1024]{1,0:T(8,128)S(1)} %collective-permute-done.3.d3_ref) | copy-start | bytes 786436
  170.4 40.6 %collective-permute-start.6 = (f32[64,1024]{1,0:T(8,128)S(1)}, f32[64,1024]{1,0:T(8,128)S(1)}, u32[]{:S(2)}, u32[]{:S(2)}) collective-permute-start(f32[64,1024]{1,0:T(8,128)S(1)} %get-tuple-element.14), channel_id=1, source_target_pairs={{0,4},{1,5},{2,6},{3,7},{4,0},{5,1},{6,2},{7,3},{8,12},{9,13},{10,... | collective-permute-start | bytes 786440 | tf_op jit(solution)/shard_map/ppermute | solution.py:265
  172.2 38.9 %collective-permute-start.5 = (f32[64,1024]{1,0:T(8,128)S(1)}, f32[64,1024]{1,0:T(8,128)S(1)}, u32[]{:S(2)}, u32[]{:S(2)}) collective-permute-start(f32[64,1024]{1,0:T(8,128)S(1)} %get-tuple-element.15), channel_id=1, source_target_pairs={{0,2},{1,3},{2,4},{3,5},{4,6},{5,7},{6,0},{7,1},{8,10},{9,11},{10,... | collective-permute-start | bytes 786440 | tf_op jit(solution)/shard_map/ppermute | solution.py:265
  211.0 0.7 copy-start.8
  211.0 0.8 copy-start.9
  211.0 0.8 copy-start.10
  211.1 0.9 copy-start.11

commit v6 on v5

--- a/solution.py
+++ b/solution.py
@@ -12,11 +12,12 @@
 CODE = 32
 MB = 16
 RIDGE = 0.5
-HI = lax.Precision.HIGHEST
 
 
 def rows_at(array, where):
-    return array.at[where].get(mode="promise_in_bounds", unique_indices=True)
+    dims = lax.GatherDimensionNumbers(offset_dims=(1,), collapsed_slice_dims=(0,), start_index_map=(0,))
+    return lax.gather(array, where[:, None], dims, (1, array.shape[1]), unique_indices=True,
+                      mode=lax.GatherScatterMode.PROMISE_IN_BOUNDS)
 
 
 def swap(value, axis):
@@ -50,8 +51,26 @@
     return jnp.concatenate(blocks, axis=1)
 
 
-def dot_t(a, b):
-    return lax.dot_general(a, b, (((1,), (1,)), ((), ())), precision=HI, preferred_element_type=jnp.float32)
+def parts_of(x):
+    high = x.astype(jnp.bfloat16)
+    rest = x - high.astype(jnp.float32)
+    mid = rest.astype(jnp.bfloat16)
+    low = (rest - mid.astype(jnp.float32)).astype(jnp.bfloat16)
+    return high, mid, low
+
+
+def left(x):
+    h, m, l = parts_of(x)
+    return jnp.concatenate([h, h, m, m, h, l], axis=1)
+
+
+def right(x):
+    h, m, l = parts_of(x)
+    return jnp.concatenate([h, m, h, m, l, h], axis=1)
+
+
+def long_dot(a, b):
+    return lax.dot_general(a, b, (((1,), (1,)), ((), ())), preferred_element_type=jnp.float32)
 
 
 def over_rows(v, k):
@@ -139,11 +158,12 @@
             @pl.when(j == b)
             def _():
                 lo, hi = b * BK, (b + 1) * BK
-                panel = dot_t(a_ref[hi:, lo:hi], w_ref[lo:hi, :])
+                panel = long_dot(left(a_ref[hi:, lo:hi]), right(w_ref[lo:hi, :]))
                 a_ref[hi:, lo:hi] = panel
-                for c in range(b + 1, nb):
-                    at = c * BK
-                    a_ref[at:, at:at + BK] -= dot_t(panel[at - hi:, :], panel[at - hi:at - hi + BK, :])
+                pl_, pr_ = left(panel), right(panel)
+                for at in range(hi, TOP, 256):
+                    to = min(at + 256, TOP)
+                    a_ref[at:, at:to] -= long_dot(pl_[at - hi:], pr_[at - hi:to - hi])
         return carry
 
     lax.fori_loop(0, nb, step, 0)
@@ -160,11 +180,11 @@
     m = jnp.exp(-dist / (2.0 * F)) + shift - update
     for b in range(nb):
         lo, hi = b * BK, (b + 1) * BK
-        x = dot_t(m[:, :BK], w_ref[lo:hi, :])
+        x = long_dot(left(m[:, :BK]), right(w_ref[lo:hi, :]))
         keep = (pos[:, lo:hi] >= PW) | (lo < PW)
         o_ref[:, lo:hi] = jnp.where(keep, x, 0.0)
         if b + 1 < nb:
-            m = m[:, BK:] - dot_t(x, a_ref[hi:, lo:hi])
+            m = m[:, BK:] - long_dot(left(x), right(a_ref[hi:, lo:hi]))
 
 
 def factor(core, mine, other):
@@ -267,12 +287,14 @@
 
     half = pairs * own
     update = inner(split_rows(slab), top_slab)
-    updates = (update[half:] + other_core(update[:half])).reshape(pairs, own, TOP)
+    update_got = other_core(update[:half])
+    updates = (update[half:] + update_got).reshape(pairs, own, TOP)
     updates = spread_over_pairs(updates)
 
     ordered = rows_at(arrived, split_rows(place_order[0]))
     dist = sq_norms(ordered)[:, None] + top_norms[None, :] - 2.0 * inner(ordered, top_feats)
-    dists = (dist[half:] + other_core(dist[:half])).reshape(pairs, own, TOP)
+    dist_got = other_core(dist[:half])
+    dists = (dist[half:] + dist_got).reshape(pairs, own, TOP)
     dists = spread_over_pairs(dists)
 
     half_share = share // 2

time: 221 us -> 215 us (0.973)
  Pallas kernels: 43.4 us -> 39 us
    pallas_call x1, Pallas kernels: 34.9 us -> 31.9 us  [factor(): pl.pallas_call(factor_kernel, out_shape=(jax.ShapeDtypeStruct((TOP, TOP),...]
  transfers between devices with their start and end apart: 14 -> 14, of which waited for: 6 -> 6; matrix products, arithmetic and copies ran while one was open for 6% -> 7% of each run, Pallas kernels for 16% -> 15%
where the time goes in v6:
time: 215 us; the launch traced here: 214 us
  waiting for transfers between devices  99.6 us (46%)
  starting transfers between devices  46.1 us (21%)
  Pallas kernels  39 us (18%)
  local copies, waits for them, and re-layouts  15.8 us (7%)
  other arithmetic  7.39 us (3%)
  matrix products  4.85 us (2%)
    all_to_all x5, waiting for transfers between devices, swap(): return lax.all_to_all(value, axis, split_axis=0, concat_axis=0, tiled=True)  71.7 us
    pallas_call x1, Pallas kernels, factor(): pl.pallas_call(factor_kernel, out_shape=(jax.ShapeDtypeStruct((TOP, TOP),...  31.9 us
    all_to_all x5, starting transfers between devices, swap(): return lax.all_to_all(value, axis, split_axis=0, concat_axis=0, tiled=True)  31.6 us
    ppermute x6, waiting for transfers between devices, spread_over_pairs(): pieces.append(lax.ppermute(piece, 'col', to))  27.9 us
    ppermute x6, starting transfers between devices, spread_over_pairs(): pieces.append(lax.ppermute(piece, 'col', to))  14 us
    pallas_call x1, Pallas kernels, solve(): pl.pallas_call(solve_kernel, out_shape=jax.ShapeDtypeStruct((parts[0].sha...  7.08 us
  transfers between devices with their start and end apart: 14, of which 6 were waited for; matrix products, arithmetic and copies ran while one was open for 7% of the time, Pallas kernels for 15%

profile of v6, /device:TPU:8, one launch (start us, length us, event | category | flops | bytes accessed | tf_op | source)
XLA Modules:
  0.0 213.9 jit_solution(2521531773335739739)
XLA Ops:
  0.0 0.8 pad_clamp_fusion.1
  0.8 0.7 fusion.24
  1.5 0.2 copy.16
  1.7 2.0 gather_fusion
  3.7 1.1 fusion.3
  4.9 8.9 %all-to-all-start = ((bf16[32,16,1152]{2,1,0:T(8,128)(2,1)}), bf16[32,16,1152]{2,1,0:T(8,128)(2,1)S(1)}, u32[]{:S(2)}, u32[]{:S(2)}) async-start(bf16[32,16,1152]{2,1,0:T(8,128)(2,1)} %bitcast.3), calls=%async_computation | async-start | bytes 2359296 | tf_op jit(solution)/shard_map/all_to_all | solution.py:24
  13.8 17.5 %all-to-all-done = bf16[32,16,1152]{2,1,0:T(8,128)(2,1)S(1)} async-done(((bf16[32,16,1152]{2,1,0:T(8,128)(2,1)}), bf16[32,16,1152]{2,1,0:T(8,128)(2,1)S(1)}, u32[]{:S(2)}, u32[]{:S(2)}) %all-to-all-start) | async-done | bytes 1179680 | tf_op jit(solution)/shard_map/all_to_all | solution.py:24
  31.3 1.7 broadcast_in_dim.33
  33.0 5.3 %all-to-all-start.1 = ((bf16[32,32,1152]{2,1,0:T(8,128)(2,1)}), bf16[32,32,1152]{2,1,0:T(8,128)(2,1)S(1)}, u32[]{:S(2)}, u32[]{:S(2)}) async-start(bf16[32,32,1152]{2,1,0:T(8,128)(2,1)} %broadcast_in_dim.33), calls=%async_computation.1 | async-start | bytes 4718592 | tf_op jit(solution)/shard_map/all_to_all | solution.py:24
  39.1 28.7 %all-to-all-done.1 = bf16[32,32,1152]{2,1,0:T(8,128)(2,1)S(1)} async-done(((bf16[32,32,1152]{2,1,0:T(8,128)(2,1)}), bf16[32,32,1152]{2,1,0:T(8,128)(2,1)S(1)}, u32[]{:S(2)}, u32[]{:S(2)}) %all-to-all-start.1) | async-done | bytes 2359328 | tf_op jit(solution)/shard_map/all_to_all | solution.py:24
  67.9 0.2 copy.17
  68.3 0.4 fusion.6
  68.7 1.2 multiply_reduce_fusion
  70.0 1.0 copy-done.4
  71.0 0.6 fusion.4
  71.6 0.2 fusion.14
  72.0 0.7 all_to_all.27
  72.7 7.6 %all-to-all-start.2 = ((f32[8,2,2304]{2,1,0:T(2,128)}), f32[8,2,2304]{2,1,0:T(2,128)S(1)}, u32[]{:S(2)}, u32[]{:S(2)}) async-start(f32[8,2,2304]{2,1,0:T(2,128)} %all_to_all.27), calls=%async_computation.2 | async-start | bytes 294912 | tf_op jit(solution)/shard_map/all_to_all | solution.py:24
  80.3 9.2 %all-to-all-done.2 = f32[8,2,2304]{2,1,0:T(2,128)S(1)} async-done(((f32[8,2,2304]{2,1,0:T(2,128)}), f32[8,2,2304]{2,1,0:T(2,128)S(1)}, u32[]{:S(2)}, u32[]{:S(2)}) %all-to-all-start.2) | async-done | bytes 147488 | tf_op jit(solution)/shard_map/all_to_all | solution.py:24
  89.6 0.7 broadcast_in_dim.36
  90.3 3.4 %all-to-all-start.3 = ((f32[8,2,1152]{2,1,0:T(2,128)}), f32[8,2,1152]{2,1,0:T(2,128)S(1)}, u32[]{:S(2)}, u32[]{:S(2)}) async-start(f32[8,2,1152]{2,1,0:T(2,128)} %broadcast_in_dim.36), calls=%async_computation.3 | async-start | bytes 147456 | tf_op jit(solution)/shard_map/all_to_all | solution.py:24
  93.6 8.6 %all-to-all-done.3 = f32[8,2,1152]{2,1,0:T(2,128)S(1)} async-done(((f32[8,2,1152]{2,1,0:T(2,128)}), f32[8,2,1152]{2,1,0:T(2,128)S(1)}, u32[]{:S(2)}, u32[]{:S(2)}) %all-to-all-start.3) | async-done | bytes 73760 | tf_op jit(solution)/shard_map/all_to_all | solution.py:24
  102.3 1.1 broadcast_in_dim.37
  103.4 6.5 %all-to-all-start.4 = ((f32[32,8,1152]{2,1,0:T(8,128)}), f32[32,8,1152]{2,1,0:T(8,128)}, u32[]{:S(2)}, u32[]{:S(2)}) async-start(f32[32,8,1152]{2,1,0:T(8,128)} %broadcast_in_dim.37), calls=%async_computation.4 | async-start | bytes 2359296 | tf_op jit(solution)/shard_map/all_to_all | solution.py:24
  110.0 0.5 broadcast.154
  110.5 0.7 reduce.15
  111.5 2.0 gather_fusion.1
  113.6 0.2 multiply_reduce_fusion.1
  113.8 2.4 %multiply_subtract_fusion = f32[512,1024]{1,0:T(8,128)S(1)} fusion(bf16[512,768]{1,0:T(8,128)(2,1)S(1)} %gather_fusion.1, bf16[1024,768]{1,0:T(8,128)(2,1)} %bitcast.66, f32[1024]{0:T(1024)S(1)} %bitcast.73, f32[512]{0:T(512)S(1)} %multiply_reduce_fusion.1), kind=kOutput, calls=%fused_computation.5 | convolution fusion | flops 806879232 | bytes 4462592 | tf_op jit(solution)/shard_map/dot_general | solution.py:36
  116.2 1.2 slice.207
  117.5 0.5 fusion.7
  118.0 1.1 slice.210
  119.0 0.5 collective-permute-start.4
  119.5 7.6 %all-to-all-done.4.mine_ref = f32[32,8,1152]{2,1,0:T(8,128)} async-done(((f32[32,8,1152]{2,1,0:T(8,128)}), f32[32,8,1152]{2,1,0:T(8,128)}, u32[]{:S(2)}, u32[]{:S(2)}) %all-to-all-start.4) | async-done | bytes 1179680 | tf_op jit(solution)/shard_map/all_to_all | solution.py:24
  127.2 1.7 slice_add_fusion.1
  128.9 0.9 dynamic-slice_bitcast_fusion.4
  129.8 0.6 collective-permute-start.3
  130.4 3.6 %collective-permute-start.2 = (f32[64,1024]{1,0:T(8,128)}, f32[64,1024]{1,0:T(8,128)S(1)}, u32[]{:S(2)}, u32[]{:S(2)}) collective-permute-start(f32[64,1024]{1,0:T(8,128)} %get-tuple-element.20), channel_id=1, source_target_pairs={{0,4},{1,5},{2,6},{3,7},{4,0},{5,1},{6,2},{7,3},{8,12},{9,13},{10,... | collective-permute-start | bytes 786440 | tf_op jit(solution)/shard_map/ppermute | solution.py:285
  134.1 1.4 slice_add_fusion
  135.4 0.9 dynamic-slice_bitcast_fusion
  136.3 4.1 %collective-permute-start.7 = (f32[64,1024]{1,0:T(8,128)S(1)}, f32[64,1024]{1,0:T(8,128)S(1)}, u32[]{:S(2)}, u32[]{:S(2)}) collective-permute-start(f32[64,1024]{1,0:T(8,128)S(1)} %get-tuple-element.15), channel_id=1, source_target_pairs={{0,6},{1,7},{2,0},{3,1},{4,2},{5,3},{6,4},{7,5},{8,14},{9,15},{10,... | collective-permute-start | bytes 786440 | tf_op jit(solution)/shard_map/ppermute | solution.py:285
  140.4 27.9 %collective-permute-done.3.d3_ref = f32[64,1024]{1,0:T(8,128)S(1)} collective-permute-done((f32[64,1024]{1,0:T(8,128)S(1)}, f32[64,1024]{1,0:T(8,128)S(1)}, u32[]{:S(2)}, u32[]{:S(2)}) %collective-permute-start.3) | collective-permute-done | bytes 262176 | tf_op jit(solution)/shard_map/ppermute | solution.py:285
  168.3 1.8 collective-permute-start.6
  170.1 3.9 %collective-permute-start.5 = (f32[64,1024]{1,0:T(8,128)S(1)}, f32[64,1024]{1,0:T(8,128)S(1)}, u32[]{:S(2)}, u32[]{:S(2)}) collective-permute-start(f32[64,1024]{1,0:T(8,128)S(1)} %get-tuple-element.17), channel_id=1, source_target_pairs={{0,2},{1,3},{2,4},{3,5},{4,6},{5,7},{6,0},{7,1},{8,10},{9,11},{10,... | collective-permute-start | bytes 786440 | tf_op jit(solution)/shard_map/ppermute | solution.py:285
  173.9 31.9 %shard_map.55 = (f32[1024,1024]{1,0:T(8,128)}, f32[1024,128]{1,0:T(8,128)}) custom-call(s32[1]{0:T(128)} %bitcast.24.core_ref, f32[32,8,1152]{2,1,0:T(8,128)} %all-to-all-done.4.mine_ref, f32[32,8,1152]{2,1,0:T(8,128)} %collective-permute-done.8.other_ref), custom_call_target="tpu_custom_call" | custom-call | tf_op jit(solution)/shard_map/pallas_call | solution.py:192
  205.9 0.6 copy-done.7
  206.6 0.1 copy-done.9
  206.8 7.1 %shard_map.56 = f32[64,1024]{1,0:T(8,128)} custom-call(s32[1]{0:T(128)} %bitcast.first_ref, f32[64,1024]{1,0:T(8,128)} %get-tuple-element.22.d0_ref, f32[64,1024]{1,0:T(8,128)} %collective-permute-done.1.d1_ref, f32[64,1024]{1,0:T(8,128)} %copy-done.7, f32[64,1024]{1,0:T(8,128)} %copy-done.6, f32[64,1024]{1,0:T(8,128)} %get-tuple-element.18.u0_ref, ...), custom_call_target="tpu_custom_call" | custom-call | tf_op jit(solution)/shard_map/pallas_call | solution.py:202
  (77 shorter events, 1.4 us)
Async XLA Ops:
  0.0 1.7 copy-start
  1.7 2.0 copy-start.5
  4.9 26.4 %all-to-all-start = ((bf16[32,16,1152]{2,1,0:T(8,128)(2,1)}), bf16[32,16,1152]{2,1,0:T(8,128)(2,1)S(1)}, u32[]{:S(2)}, u32[]{:S(2)}) async-start(bf16[32,16,1152]{2,1,0:T(8,128)(2,1)} %bitcast.3), calls=%async_computation | async-start | bytes 2359296 | tf_op jit(solution)/shard_map/all_to_all | solution.py:24
  31.3 1.8 copy-start.1
  33.0 34.9 %all-to-all-start.1 = ((bf16[32,32,1152]{2,1,0:T(8,128)(2,1)}), bf16[32,32,1152]{2,1,0:T(8,128)(2,1)S(1)}, u32[]{:S(2)}, u32[]{:S(2)}) async-start(bf16[32,32,1152]{2,1,0:T(8,128)(2,1)} %broadcast_in_dim.33), calls=%async_computation.1 | async-start | bytes 4718592 | tf_op jit(solution)/shard_map/all_to_all | solution.py:24
  69.8 1.2 copy-start.4
  72.7 16.8 %all-to-all-start.2 = ((f32[8,2,2304]{2,1,0:T(2,128)}), f32[8,2,2304]{2,1,0:T(2,128)S(1)}, u32[]{:S(2)}, u32[]{:S(2)}) async-start(f32[8,2,2304]{2,1,0:T(2,128)} %all_to_all.27), calls=%async_computation.2 | async-start | bytes 294912 | tf_op jit(solution)/shard_map/all_to_all | solution.py:24
  80.3 30.2 %copy-start.11 = (s32[1,512]{1,0:T(1,128)S(1)}, s32[1,512]{1,0:T(1,128)}, u32[]{:S(2)}) copy-start(s32[1,512]{1,0:T(1,128)} %param.8) | copy-start | bytes 6148
  89.6 21.9 %copy-start.2 = (bf16[32,16,1152]{2,1,0:T(8,128)(2,1)S(1)}, bf16[32,16,1152]{2,1,0:T(8,128)(2,1)}, u32[]{:S(2)}) copy-start(bf16[32,16,1152]{2,1,0:T(8,128)(2,1)} %copy-done.1) | copy-start | bytes 3538948
  90.3 12.0 %all-to-all-start.3 = ((f32[8,2,1152]{2,1,0:T(2,128)}), f32[8,2,1152]{2,1,0:T(2,128)S(1)}, u32[]{:S(2)}, u32[]{:S(2)}) async-start(f32[8,2,1152]{2,1,0:T(2,128)} %broadcast_in_dim.36), calls=%async_computation.3 | async-start | bytes 147456 | tf_op jit(solution)/shard_map/all_to_all | solution.py:24
  103.4 23.8 %all-to-all-start.4 = ((f32[32,8,1152]{2,1,0:T(8,128)}), f32[32,8,1152]{2,1,0:T(8,128)}, u32[]{:S(2)}, u32[]{:S(2)}) async-start(f32[32,8,1152]{2,1,0:T(8,128)} %broadcast_in_dim.37), calls=%async_computation.4 | async-start | bytes 2359296 | tf_op jit(solution)/shard_map/all_to_all | solution.py:24
  116.2 1.7 copy-start.3
  117.5 9.7 %collective-permute-start = (f32[256,1024]{1,0:T(8,128)}, f32[256,1024]{1,0:T(8,128)}, u32[]{:S(2)}, u32[]{:S(2)}) collective-permute-start(f32[256,1024]{1,0:T(8,128)} %slice.207), channel_id=1, source_target_pairs={{0,1},{1,0},{2,3},{3,2},{4,5},{5,4},{6,7},{7,6},{8,9},{9,8},{10,11... | collective-permute-start | bytes 3145736 | tf_op jit(solution)/shard_map/ppermute | solution.py:278
  119.0 15.0 %collective-permute-start.4 = (f32[256,1024]{1,0:T(8,128)}, f32[256,1024]{1,0:T(8,128)}, u32[]{:S(2)}, u32[]{:S(2)}) collective-permute-start(f32[256,1024]{1,0:T(8,128)} %slice.210), channel_id=1, source_target_pairs={{0,1},{1,0},{2,3},{3,2},{4,5},{5,4},{6,7},{7,6},{8,9},{9,8},{10,11... | collective-permute-start | bytes 3145736 | tf_op jit(solution)/shard_map/ppermute | solution.py:278
  127.2 42.9 %collective-permute-start.8 = (f32[32,8,1152]{2,1,0:T(8,128)}, f32[32,8,1152]{2,1,0:T(8,128)}, u32[]{:S(2)}, u32[]{:S(2)}) collective-permute-start(f32[32,8,1152]{2,1,0:T(8,128)} %all-to-all-done.4.mine_ref), channel_id=1, source_target_pairs={{0,1},{1,0},{2,3},{3,2},{4,5},{5,4},{6,7},{7,6},{8,9},{9,8},{10,11... | collective-permute-start | bytes 3538952 | tf_op jit(solution)/shard_map/ppermute | solution.py:304
  129.8 38.5 %collective-permute-start.3 = (f32[64,1024]{1,0:T(8,128)S(1)}, f32[64,1024]{1,0:T(8,128)S(1)}, u32[]{:S(2)}, u32[]{:S(2)}) collective-permute-start(f32[64,1024]{1,0:T(8,128)S(1)} %get-tuple-element.19), channel_id=1, source_target_pairs={{0,6},{1,7},{2,0},{3,1},{4,2},{5,3},{6,4},{7,5},{8,14},{9,15},{10,... | collective-permute-start | bytes 786440 | tf_op jit(solution)/shard_map/ppermute | solution.py:285
  130.4 75.4 %collective-permute-start.2 = (f32[64,1024]{1,0:T(8,128)}, f32[64,1024]{1,0:T(8,128)S(1)}, u32[]{:S(2)}, u32[]{:S(2)}) collective-permute-start(f32[64,1024]{1,0:T(8,128)} %get-tuple-element.20), channel_id=1, source_target_pairs={{0,4},{1,5},{2,6},{3,7},{4,0},{5,1},{6,2},{7,3},{8,12},{9,13},{10,... | collective-permute-start | bytes 786440 | tf_op jit(solution)/shard_map/ppermute | solution.py:285
  134.0 71.8 %collective-permute-start.1 = (f32[64,1024]{1,0:T(8,128)}, f32[64,1024]{1,0:T(8,128)}, u32[]{:S(2)}, u32[]{:S(2)}) collective-permute-start(f32[64,1024]{1,0:T(8,128)} %get-tuple-element.21), channel_id=1, source_target_pairs={{0,2},{1,3},{2,4},{3,5},{4,6},{5,7},{6,0},{7,1},{8,10},{9,11},{10,... | collective-permute-start | bytes 786440 | tf_op jit(solution)/shard_map/ppermute | solution.py:285
  136.3 69.6 %collective-permute-start.7 = (f32[64,1024]{1,0:T(8,128)S(1)}, f32[64,1024]{1,0:T(8,128)S(1)}, u32[]{:S(2)}, u32[]{:S(2)}) collective-permute-start(f32[64,1024]{1,0:T(8,128)S(1)} %get-tuple-element.15), channel_id=1, source_target_pairs={{0,6},{1,7},{2,0},{3,1},{4,2},{5,3},{6,4},{7,5},{8,14},{9,15},{10,... | collective-permute-start | bytes 786440 | tf_op jit(solution)/shard_map/ppermute | solution.py:285
  168.3 37.6 %copy-start.6 = (f32[64,1024]{1,0:T(8,128)}, f32[64,1024]{1,0:T(8,128)S(1)}, u32[]{:S(2)}) copy-start(f32[64,1024]{1,0:T(8,128)S(1)} %collective-permute-done.3.d3_ref) | copy-start | bytes 786436
  168.3 37.6 %collective-permute-start.6 = (f32[64,1024]{1,0:T(8,128)S(1)}, f32[64,1024]{1,0:T(8,128)S(1)}, u32[]{:S(2)}, u32[]{:S(2)}) collective-permute-start(f32[64,1024]{1,0:T(8,128)S(1)} %get-tuple-element.16), channel_id=1, source_target_pairs={{0,4},{1,5},{2,6},{3,7},{4,0},{5,1},{6,2},{7,3},{8,12},{9,13},{10,... | collective-permute-start | bytes 786440 | tf_op jit(solution)/shard_map/ppermute | solution.py:285
  170.1 35.8 %collective-permute-start.5 = (f32[64,1024]{1,0:T(8,128)S(1)}, f32[64,1024]{1,0:T(8,128)S(1)}, u32[]{:S(2)}, u32[]{:S(2)}) collective-permute-start(f32[64,1024]{1,0:T(8,128)S(1)} %get-tuple-element.17), channel_id=1, source_target_pairs={{0,2},{1,3},{2,4},{3,5},{4,6},{5,7},{6,0},{7,1},{8,10},{9,11},{10,... | collective-permute-start | bytes 786440 | tf_op jit(solution)/shard_map/ppermute | solution.py:285
  205.8 0.7 copy-start.7
  205.9 0.8 copy-start.8
  205.9 0.9 copy-start.9
  205.9 0.9 copy-start.10

commit v7 on v6

--- a/solution.py
+++ b/solution.py
@@ -169,10 +169,10 @@
     lax.fori_loop(0, nb, step, 0)
 
 
-def solve_kernel(first_ref, d0_ref, d1_ref, d2_ref, d3_ref, u0_ref, u1_ref, u2_ref, u3_ref, a_ref, w_ref, o_ref):
+def solve_kernel(first_ref, d0_ref, d1_ref, d2_ref, d3_ref, u0_ref, u1_ref, u2_ref, a_ref, w_ref, o_ref):
     nb = TOP // BK
     dist = (d0_ref[...] + d1_ref[...]) + (d2_ref[...] + d3_ref[...])
-    update = (u0_ref[...] + u1_ref[...]) + (u2_ref[...] + u3_ref[...])
+    update = (u0_ref[...] + u1_ref[...]) + u2_ref[...]
     rows = dist.shape[0]
     pos = first_ref[0] + lax.broadcasted_iota(jnp.int32, (rows, TOP), 0)
     col = lax.broadcasted_iota(jnp.int32, (rows, TOP), 1)
@@ -257,10 +257,11 @@
     summed = jnp.sum(parts.reshape(n_col, share // n_col, 2 * 9 * BK), axis=0)
     dist, update = summed[:, :9 * BK], summed[:, 9 * BK:]
     mine = share // n_col
-    col_ids = jnp.arange(TOP)[None, :]
     ids = jnp.arange(mine)[:, None] + col * mine
-    shift = fold((row_hi + ids == col_ids).astype(jnp.float32),
-                 (row_lo + ids == col_ids).astype(jnp.float32), pair)
+    at_col = jnp.arange(9 * BK)[None, :]
+    from_hi = at_col // BK + pair <= 7
+    col_ids = jnp.where(from_hi, at_col, (8 - at_col // BK) * BK + at_col % BK)
+    shift = (jnp.where(from_hi, row_hi, row_lo) + ids == col_ids).astype(jnp.float32)
     entries = jnp.exp(-dist / (2.0 * F)) + RIDGE * shift - update
     entries = from_everyone(entries, "col")
     entries = entries.reshape(share, 9 * BK)
@@ -285,11 +286,26 @@
             pieces.append(lax.ppermute(piece, "col", to))
         return pieces
 
+    def relayed_over_pairs(value):
+        def step(piece, by):
+            return lax.ppermute(piece, "col", [(c, (c // 2 + by) % pairs * 2 + c % 2) for c in range(n_col)])
+
+        def piece_at(away):
+            return lax.dynamic_index_in_dim(value, (pair_at + away) % pairs, 0, keepdims=False)
+
+        middle = own // 2
+        opposite, nxt, prev = piece_at(2), piece_at(1), piece_at(pairs - 1)
+        up = step(opposite[:middle], 1)
+        down = step(opposite[middle:], -1)
+        nxt = jnp.concatenate([nxt[:middle] + up, nxt[middle:]], axis=0)
+        prev = jnp.concatenate([prev[:middle], prev[middle:] + down], axis=0)
+        return [piece_at(0), step(nxt, 1), step(prev, -1)]
+
     half = pairs * own
     update = inner(split_rows(slab), top_slab)
     update_got = other_core(update[:half])
     updates = (update[half:] + update_got).reshape(pairs, own, TOP)
-    updates = spread_over_pairs(updates)
+    updates = relayed_over_pairs(updates)
 
     ordered = rows_at(arrived, split_rows(place_order[0]))
     dist = sq_norms(ordered)[:, None] + top_norms[None, :] - 2.0 * inner(ordered, top_feats)

time: 215 us -> 188 us (0.87)
  the two profiles are of different devices: /device:TPU:8 before, /device:TPU:2 now
where the time goes in v7:
time: 188 us; the launch traced here: 185 us
  waiting for transfers between devices  67.6 us (36%)
  starting transfers between devices  45.6 us (24%)
  Pallas kernels  39.2 us (21%)
  local copies, waits for them, and re-layouts  19.8 us (11%)
  other arithmetic  7.2 us (4%)
  matrix products  4.41 us (2%)
    all_to_all x5, waiting for transfers between devices, swap(): return lax.all_to_all(value, axis, split_axis=0, concat_axis=0, tiled=True)  66.7 us
    all_to_all x5, starting transfers between devices, swap(): return lax.all_to_all(value, axis, split_axis=0, concat_axis=0, tiled=True)  33.7 us
    pallas_call x1, Pallas kernels, factor(): pl.pallas_call(factor_kernel, out_shape=(jax.ShapeDtypeStruct((TOP, TOP),...  32.1 us
    ppermute x4, starting transfers between devices, step(): lax.ppermute(piece, 'col', [(c, (c // 2 + by) % pairs * 2 + c % 2) for c...  8.81 us
    pallas_call x1, Pallas kernels, solve(): pl.pallas_call(solve_kernel, out_shape=jax.ShapeDtypeStruct((parts[0].sha...  7.03 us
    gather x2, local copies, waits for them, and re-layouts, rows_at(): lax.gather(array, where[:, None], dims, (1, array.shape[1]), unique_indic...  4.73 us
    unnamed x39, local copies, waits for them, and re-layouts  4.39 us
  transfers between devices with their start and end apart: 15, of which 6 were waited for; matrix products, arithmetic and copies ran while one was open for 8% of the time, Pallas kernels for 17%

profile of v7, /device:TPU:2, one launch (start us, length us, event | category | flops | bytes accessed | tf_op | source)
XLA Modules:
  0.0 185.0 jit_solution(2900660294460684805)
XLA Ops:
  0.0 0.8 pad_clamp_fusion.1
  0.8 0.7 fusion.40
  1.5 0.2 copy.16
  1.7 2.0 %gather_fusion = bf16[512,768]{1,0:T(8,128)(2,1)S(1)} fusion(bf16[512,768]{1,0:T(8,128)(2,1)S(1)} %copy-done, s32[1024]{0:T(1024)S(1)} %pad_clamp_fusion.1), kind=kCustom, calls=%fused_computation | custom fusion | bytes 1574912 | tf_op jit(solution)/shard_map/gather | solution.py:19
  3.7 1.1 fusion.3
  4.9 9.0 %all-to-all-start = ((bf16[32,16,1152]{2,1,0:T(8,128)(2,1)}), bf16[32,16,1152]{2,1,0:T(8,128)(2,1)S(1)}, u32[]{:S(2)}, u32[]{:S(2)}) async-start(bf16[32,16,1152]{2,1,0:T(8,128)(2,1)} %bitcast.3), calls=%async_computation | async-start | bytes 2359296 | tf_op jit(solution)/shard_map/all_to_all | solution.py:24
  13.9 16.5 %all-to-all-done = bf16[32,16,1152]{2,1,0:T(8,128)(2,1)S(1)} async-done(((bf16[32,16,1152]{2,1,0:T(8,128)(2,1)}), bf16[32,16,1152]{2,1,0:T(8,128)(2,1)S(1)}, u32[]{:S(2)}, u32[]{:S(2)}) %all-to-all-start) | async-done | bytes 1179680 | tf_op jit(solution)/shard_map/all_to_all | solution.py:24
  30.4 1.7 broadcast_in_dim.41
  32.2 6.2 %all-to-all-start.1 = ((bf16[32,32,1152]{2,1,0:T(8,128)(2,1)}), bf16[32,32,1152]{2,1,0:T(8,128)(2,1)S(1)}, u32[]{:S(2)}, u32[]{:S(2)}) async-start(bf16[32,32,1152]{2,1,0:T(8,128)(2,1)} %broadcast_in_dim.41), calls=%async_computation.1 | async-start | bytes 4718592 | tf_op jit(solution)/shard_map/all_to_all | solution.py:24
  39.1 27.9 %all-to-all-done.1 = bf16[32,32,1152]{2,1,0:T(8,128)(2,1)S(1)} async-done(((bf16[32,32,1152]{2,1,0:T(8,128)(2,1)}), bf16[32,32,1152]{2,1,0:T(8,128)(2,1)S(1)}, u32[]{:S(2)}, u32[]{:S(2)}) %all-to-all-start.1) | async-done | bytes 2359328 | tf_op jit(solution)/shard_map/all_to_all | solution.py:24
  67.4 0.4 fusion.6
  67.7 1.2 multiply_reduce_fusion
  69.1 1.0 copy-done.7
  70.1 0.6 fusion.4
  70.7 0.2 fusion.16
  71.0 0.7 all_to_all.27
  71.8 7.6 %all-to-all-start.2 = ((f32[8,2,2304]{2,1,0:T(2,128)}), f32[8,2,2304]{2,1,0:T(2,128)S(1)}, u32[]{:S(2)}, u32[]{:S(2)}) async-start(f32[8,2,2304]{2,1,0:T(2,128)} %all_to_all.27), calls=%async_computation.2 | async-start | bytes 294912 | tf_op jit(solution)/shard_map/all_to_all | solution.py:24
  79.4 9.2 %all-to-all-done.2 = f32[8,2,2304]{2,1,0:T(2,128)S(1)} async-done(((f32[8,2,2304]{2,1,0:T(2,128)}), f32[8,2,2304]{2,1,0:T(2,128)S(1)}, u32[]{:S(2)}, u32[]{:S(2)}) %all-to-all-start.2) | async-done | bytes 147488 | tf_op jit(solution)/shard_map/all_to_all | solution.py:24
  88.7 0.7 broadcast_in_dim.46
  89.4 3.4 %all-to-all-start.3 = ((f32[8,2,1152]{2,1,0:T(2,128)}), f32[8,2,1152]{2,1,0:T(2,128)S(1)}, u32[]{:S(2)}, u32[]{:S(2)}) async-start(f32[8,2,1152]{2,1,0:T(2,128)} %broadcast_in_dim.46), calls=%async_computation.3 | async-start | bytes 147456 | tf_op jit(solution)/shard_map/all_to_all | solution.py:24
  92.8 8.6 %all-to-all-done.3 = f32[8,2,1152]{2,1,0:T(2,128)S(1)} async-done(((f32[8,2,1152]{2,1,0:T(2,128)}), f32[8,2,1152]{2,1,0:T(2,128)S(1)}, u32[]{:S(2)}, u32[]{:S(2)}) %all-to-all-start.3) | async-done | bytes 73760 | tf_op jit(solution)/shard_map/all_to_all | solution.py:24
  101.5 1.1 broadcast_in_dim.47
  102.6 7.6 %all-to-all-start.4 = ((f32[32,8,1152]{2,1,0:T(8,128)}), f32[32,8,1152]{2,1,0:T(8,128)}, u32[]{:S(2)}, u32[]{:S(2)}) async-start(f32[32,8,1152]{2,1,0:T(8,128)} %broadcast_in_dim.47), calls=%async_computation.4 | async-start | bytes 2359296 | tf_op jit(solution)/shard_map/all_to_all | solution.py:24
  110.1 0.5 broadcast.272
  110.7 0.7 reduce.15
  111.6 0.7 constant_dynamic-slice_fusion.6
  112.4 2.7 %gather_fusion.1 = bf16[512,768]{1,0:T(8,128)(2,1)} fusion(bf16[512,768]{1,0:T(8,128)(2,1)S(1)} %slice.210, s32[1024]{0:T(1024)S(1)} %pad_clamp_fusion), kind=kCustom, calls=%fused_computation.1 | custom fusion | bytes 1574912 | tf_op jit(solution)/shard_map/gather | solution.py:19
  115.1 1.4 fusion.7
  116.6 1.1 slice.221
  117.7 0.2 multiply_reduce_fusion.1
  117.9 0.5 copy-done.8
  118.4 1.0 multiply_subtract_fusion
  119.4 1.3 copy-done.5
  120.7 1.1 slice.218
  121.9 4.4 %all-to-all-done.4.mine_ref = f32[32,8,1152]{2,1,0:T(8,128)} async-done(((f32[32,8,1152]{2,1,0:T(8,128)}), f32[32,8,1152]{2,1,0:T(8,128)}, u32[]{:S(2)}, u32[]{:S(2)}) %all-to-all-start.4) | async-done | bytes 1179680 | tf_op jit(solution)/shard_map/all_to_all | solution.py:24
  126.3 1.5 slice_add_fusion
  127.9 0.8 collective-permute-start.5
  128.7 3.4 %collective-permute-start.7 = (f32[32,1024]{1,0:T(8,128)S(1)}, f32[32,1024]{1,0:T(8,128)S(1)}, u32[]{:S(2)}, u32[]{:S(2)}) collective-permute-start(f32[32,1024]{1,0:T(8,128)S(1)} %get-tuple-element.17), channel_id=1, source_target_pairs={{0,6},{1,7},{2,0},{3,1},{4,2},{5,3},{6,4},{7,5},{8,14},{9,15},{10,... | collective-permute-start | bytes 393224 | tf_op jit(solution)/shard_map/ppermute | solution.py:291
  132.1 1.4 slice_add_fusion.1
  133.5 0.8 dynamic-slice_bitcast_fusion.1
  134.3 3.1 %collective-permute-start.2 = (f32[64,1024]{1,0:T(8,128)S(1)}, f32[64,1024]{1,0:T(8,128)S(1)}, u32[]{:S(2)}, u32[]{:S(2)}) collective-permute-start(f32[64,1024]{1,0:T(8,128)S(1)} %get-tuple-element.22), channel_id=1, source_target_pairs={{0,4},{1,5},{2,6},{3,7},{4,0},{5,1},{6,2},{7,3},{8,12},{9,13},{10,... | collective-permute-start | bytes 786440 | tf_op jit(solution)/shard_map/ppermute | solution.py:286
  137.4 0.9 collective-permute-done.5
  138.4 3.1 %collective-permute-start.6 = (f32[64,1024]{1,0:T(8,128)S(1)}, f32[64,1024]{1,0:T(8,128)S(1)}, u32[]{:S(2)}, u32[]{:S(2)}) collective-permute-start(f32[64,1024]{1,0:T(8,128)S(1)} %pad_maximum_fusion), channel_id=1, source_target_pairs={{0,2},{1,3},{2,4},{3,5},{4,6},{5,7},{6,0},{7,1},{8,10},{9,11},{10,... | collective-permute-start | bytes 786440 | tf_op jit(solution)/shard_map/ppermute | solution.py:291
  141.6 1.5 collective-permute-start.8
  143.1 1.7 dynamic-slice_bitcast_fusion.u0_ref
  144.8 32.1 %shard_map.55 = (f32[1024,1024]{1,0:T(8,128)}, f32[1024,128]{1,0:T(8,128)}) custom-call(s32[1]{0:T(128)} %bitcast.27.core_ref, f32[32,8,1152]{2,1,0:T(8,128)} %all-to-all-done.4.mine_ref, f32[32,8,1152]{2,1,0:T(8,128)} %collective-permute-done.9.other_ref), custom_call_target="tpu_custom_call" | custom-call | tf_op jit(solution)/shard_map/pallas_call | solution.py:192
  177.0 0.6 copy-done.11
  178.0 7.0 %shard_map.56 = f32[64,1024]{1,0:T(8,128)} custom-call(s32[1]{0:T(128)} %bitcast.first_ref, f32[64,1024]{1,0:T(8,128)} %get-tuple-element.24.d0_ref, f32[64,1024]{1,0:T(8,128)} %copy-done.13, f32[64,1024]{1,0:T(8,128)} %copy-done.12, f32[64,1024]{1,0:T(8,128)} %copy-done.11, f32[64,1024]{1,0:T(8,128)} %dynamic-slice_bitcast_fusion.u0_ref, ...), custom_call_target="tpu_custom_call" | custom-call | tf_op jit(solution)/shard_map/pallas_call | solution.py:202
  (87 shorter events, 1.9 us)
Async XLA Ops:
  0.0 1.7 copy-start
  1.7 2.0 %copy-start.9 = (bf16[512,256]{1,0:T(8,128)(2,1)S(1)}, bf16[512,256]{1,0:T(8,128)(2,1)}, u32[]{:S(2)}) copy-start(bf16[512,256]{1,0:T(8,128)(2,1)} %param.6) | copy-start | bytes 786436
  4.9 25.5 %all-to-all-start = ((bf16[32,16,1152]{2,1,0:T(8,128)(2,1)}), bf16[32,16,1152]{2,1,0:T(8,128)(2,1)S(1)}, u32[]{:S(2)}, u32[]{:S(2)}) async-start(bf16[32,16,1152]{2,1,0:T(8,128)(2,1)} %bitcast.3), calls=%async_computation | async-start | bytes 2359296 | tf_op jit(solution)/shard_map/all_to_all | solution.py:24
  30.4 1.8 copy-start.2
  32.2 34.8 %all-to-all-start.1 = ((bf16[32,32,1152]{2,1,0:T(8,128)(2,1)}), bf16[32,32,1152]{2,1,0:T(8,128)(2,1)S(1)}, u32[]{:S(2)}, u32[]{:S(2)}) async-start(bf16[32,32,1152]{2,1,0:T(8,128)(2,1)} %broadcast_in_dim.41), calls=%async_computation.1 | async-start | bytes 4718592 | tf_op jit(solution)/shard_map/all_to_all | solution.py:24
  68.9 1.2 copy-start.7
  71.8 16.8 %all-to-all-start.2 = ((f32[8,2,2304]{2,1,0:T(2,128)}), f32[8,2,2304]{2,1,0:T(2,128)S(1)}, u32[]{:S(2)}, u32[]{:S(2)}) async-start(f32[8,2,2304]{2,1,0:T(2,128)} %all_to_all.27), calls=%async_computation.2 | async-start | bytes 294912 | tf_op jit(solution)/shard_map/all_to_all | solution.py:24
  88.7 22.0 %copy-start.16 = (s32[1,512]{1,0:T(1,128)S(1)}, s32[1,512]{1,0:T(1,128)}, u32[]{:S(2)}) copy-start(s32[1,512]{1,0:T(1,128)} %param.8) | copy-start | bytes 6148
  89.4 12.0 %all-to-all-start.3 = ((f32[8,2,1152]{2,1,0:T(2,128)}), f32[8,2,1152]{2,1,0:T(2,128)S(1)}, u32[]{:S(2)}, u32[]{:S(2)}) async-start(f32[8,2,1152]{2,1,0:T(2,128)} %broadcast_in_dim.46), calls=%async_computation.3 | async-start | bytes 147456 | tf_op jit(solution)/shard_map/all_to_all | solution.py:24
  101.5 10.9 %copy-start.3 = (bf16[32,16,1152]{2,1,0:T(8,128)(2,1)S(1)}, bf16[32,16,1152]{2,1,0:T(8,128)(2,1)}, u32[]{:S(2)}) copy-start(bf16[32,16,1152]{2,1,0:T(8,128)(2,1)} %copy-done.2) | copy-start | bytes 3538948
  102.6 23.7 %all-to-all-start.4 = ((f32[32,8,1152]{2,1,0:T(8,128)}), f32[32,8,1152]{2,1,0:T(8,128)}, u32[]{:S(2)}, u32[]{:S(2)}) async-start(f32[32,8,1152]{2,1,0:T(8,128)} %broadcast_in_dim.47), calls=%async_computation.4 | async-start | bytes 2359296 | tf_op jit(solution)/shard_map/all_to_all | solution.py:24
  112.4 2.7 %copy-start.10 = (bf16[4,1,64,256]{3,2,1,0:T(8,128)(2,1)S(1)}, bf16[4,1,64,256]{3,2,1,0:T(8,128)(2,1)}, u32[]{:S(2)}) copy-start(bf16[4,1,64,256]{3,2,1,0:T(8,128)(2,1)} %get-tuple-element.27) | copy-start | bytes 393220
  115.1 2.5 %copy-start.4 = (bf16[512,768]{1,0:T(8,128)(2,1)S(1)}, bf16[512,768]{1,0:T(8,128)(2,1)}, u32[]{:S(2)}) copy-start(bf16[512,768]{1,0:T(8,128)(2,1)} %gather_fusion.1) | copy-start | bytes 2359300
  116.6 1.8 copy-start.8
  117.7 8.7 %collective-permute-start.4 = (f32[256,1024]{1,0:T(8,128)}, f32[256,1024]{1,0:T(8,128)}, u32[]{:S(2)}, u32[]{:S(2)}) collective-permute-start(f32[256,1024]{1,0:T(8,128)} %slice.221), channel_id=1, source_target_pairs={{0,1},{1,0},{2,3},{3,2},{4,5},{5,4},{6,7},{7,6},{8,9},{9,8},{10,11... | collective-permute-start | bytes 3145736 | tf_op jit(solution)/shard_map/ppermute | solution.py:279
  119.4 1.3 copy-start.5
  121.8 10.3 %collective-permute-start = (f32[256,1024]{1,0:T(8,128)}, f32[256,1024]{1,0:T(8,128)}, u32[]{:S(2)}, u32[]{:S(2)}) collective-permute-start(f32[256,1024]{1,0:T(8,128)} %slice.218), channel_id=1, source_target_pairs={{0,1},{1,0},{2,3},{3,2},{4,5},{5,4},{6,7},{7,6},{8,9},{9,8},{10,11... | collective-permute-start | bytes 3145736 | tf_op jit(solution)/shard_map/ppermute | solution.py:279
  126.3 5.8 %copy-start.6 = (f32[512,1024]{1,0:T(8,128)S(1)}, f32[512,1024]{1,0:T(8,128)}, u32[]{:S(2)}) copy-start(f32[512,1024]{1,0:T(8,128)} %copy-done.5) | copy-start | bytes 6291460
  126.3 15.3 %collective-permute-start.9 = (f32[32,8,1152]{2,1,0:T(8,128)}, f32[32,8,1152]{2,1,0:T(8,128)}, u32[]{:S(2)}, u32[]{:S(2)}) collective-permute-start(f32[32,8,1152]{2,1,0:T(8,128)} %all-to-all-done.4.mine_ref), channel_id=1, source_target_pairs={{0,1},{1,0},{2,3},{3,2},{4,5},{5,4},{6,7},{7,6},{8,9},{9,8},{10,11... | collective-permute-start | bytes 3538952 | tf_op jit(solution)/shard_map/ppermute | solution.py:320
  127.8 10.5 %copy-start.1 = (f32[256,1024]{1,0:T(8,128)}, f32[256,1024]{1,0:T(8,128)S(1)}, u32[]{:S(2)}) copy-start(f32[256,1024]{1,0:T(8,128)S(1)} %slice_add_fusion) | copy-start | bytes 3145732
  127.9 10.4 %collective-permute-start.5 = (f32[32,1024]{1,0:T(8,128)S(1)}, f32[32,1024]{1,0:T(8,128)S(1)}, u32[]{:S(2)}, u32[]{:S(2)}) collective-permute-start(f32[32,1024]{1,0:T(8,128)S(1)} %get-tuple-element.16), channel_id=1, source_target_pairs={{0,2},{1,3},{2,4},{3,5},{4,6},{5,7},{6,0},{7,1},{8,10},{9,11},{10,... | collective-permute-start | bytes 393224 | tf_op jit(solution)/shard_map/ppermute | solution.py:291
  128.7 9.6 %collective-permute-start.7 = (f32[32,1024]{1,0:T(8,128)S(1)}, f32[32,1024]{1,0:T(8,128)S(1)}, u32[]{:S(2)}, u32[]{:S(2)}) collective-permute-start(f32[32,1024]{1,0:T(8,128)S(1)} %get-tuple-element.17), channel_id=1, source_target_pairs={{0,6},{1,7},{2,0},{3,1},{4,2},{5,3},{6,4},{7,5},{8,14},{9,15},{10,... | collective-permute-start | bytes 393224 | tf_op jit(solution)/shard_map/ppermute | solution.py:291
  134.3 42.6 %collective-permute-start.3 = (f32[64,1024]{1,0:T(8,128)S(1)}, f32[64,1024]{1,0:T(8,128)S(1)}, u32[]{:S(2)}, u32[]{:S(2)}) collective-permute-start(f32[64,1024]{1,0:T(8,128)S(1)} %get-tuple-element.21), channel_id=1, source_target_pairs={{0,6},{1,7},{2,0},{3,1},{4,2},{5,3},{6,4},{7,5},{8,14},{9,15},{10,... | collective-permute-start | bytes 786440 | tf_op jit(solution)/shard_map/ppermute | solution.py:286
  134.3 42.6 %collective-permute-start.2 = (f32[64,1024]{1,0:T(8,128)S(1)}, f32[64,1024]{1,0:T(8,128)S(1)}, u32[]{:S(2)}, u32[]{:S(2)}) collective-permute-start(f32[64,1024]{1,0:T(8,128)S(1)} %get-tuple-element.22), channel_id=1, source_target_pairs={{0,4},{1,5},{2,6},{3,7},{4,0},{5,1},{6,2},{7,3},{8,12},{9,13},{10,... | collective-permute-start | bytes 786440 | tf_op jit(solution)/shard_map/ppermute | solution.py:286
  138.4 38.6 %collective-permute-start.1 = (f32[64,1024]{1,0:T(8,128)S(1)}, f32[64,1024]{1,0:T(8,128)S(1)}, u32[]{:S(2)}, u32[]{:S(2)}) collective-permute-start(f32[64,1024]{1,0:T(8,128)S(1)} %get-tuple-element.23), channel_id=1, source_target_pairs={{0,2},{1,3},{2,4},{3,5},{4,6},{5,7},{6,0},{7,1},{8,10},{9,11},{10,... | collective-permute-start | bytes 786440 | tf_op jit(solution)/shard_map/ppermute | solution.py:286
  138.4 38.5 %collective-permute-start.6 = (f32[64,1024]{1,0:T(8,128)S(1)}, f32[64,1024]{1,0:T(8,128)S(1)}, u32[]{:S(2)}, u32[]{:S(2)}) collective-permute-start(f32[64,1024]{1,0:T(8,128)S(1)} %pad_maximum_fusion), channel_id=1, source_target_pairs={{0,2},{1,3},{2,4},{3,5},{4,6},{5,7},{6,0},{7,1},{8,10},{9,11},{10,... | collective-permute-start | bytes 786440 | tf_op jit(solution)/shard_map/ppermute | solution.py:291
  141.6 35.3 %collective-permute-start.8 = (f32[64,1024]{1,0:T(8,128)S(1)}, f32[64,1024]{1,0:T(8,128)S(1)}, u32[]{:S(2)}, u32[]{:S(2)}) collective-permute-start(f32[64,1024]{1,0:T(8,128)S(1)} %pad_maximum_fusion.1), channel_id=1, source_target_pairs={{0,6},{1,7},{2,0},{3,1},{4,2},{5,3},{6,4},{7,5},{8,14},{9,15},{10,... | collective-permute-start | bytes 786440 | tf_op jit(solution)/shard_map/ppermute | solution.py:291
  176.9 0.7 copy-start.11
  176.9 0.8 copy-start.12
  176.9 0.9 copy-start.13
  176.9 1.0 copy-start.14
  177.0 1.0 copy-start.15

commit v8 on v7

--- a/solution.py
+++ b/solution.py
@@ -221,9 +221,20 @@
     packed = rows_at(features, pack_order[0])
     feat_dev = packed.shape[1]
     arrived = swap(jnp.concatenate([packed, slab, coded], axis=1), "krow")
+    core, pair_at = col % 2, col // 2
+    pairs = n_col // 2
+    own = rows_dev // n_col
+
+    def split_rows(array):
+        array = array.reshape(pairs, 2, own, *array.shape[1:])
+        halves = [lax.dynamic_index_in_dim(array, which, 1, keepdims=False) for which in (1 - core, core)]
+        return jnp.concatenate([h.reshape(pairs * own, *h.shape[2:]) for h in halves], axis=0)
+
     mine = jnp.concatenate([packed[:2 * group], arrived[:2 * group, feat_dev:]], axis=1)
-    arrived = arrived[:, :feat_dev]
     tiles = from_everyone(mine, "krow")
+    own_places = split_rows(place_order[0])
+    ordered = rows_at(arrived[:, :feat_dev], own_places)
+    own_norms = sq_norms(ordered)
 
     tiles = tiles.reshape(n_krow, 2, group, tiles.shape[-1])
     top = jnp.moveaxis(tiles, 1, 0).reshape(TOP, tiles.shape[-1])
@@ -266,15 +277,6 @@
     entries = from_everyone(entries, "col")
     entries = entries.reshape(share, 9 * BK)
 
-    core, pair_at = col % 2, col // 2
-    pairs = n_col // 2
-    own = rows_dev // n_col
-
-    def split_rows(array):
-        array = array.reshape(pairs, 2, own, *array.shape[1:])
-        halves = [lax.dynamic_index_in_dim(array, which, 1, keepdims=False) for which in (1 - core, core)]
-        return jnp.concatenate([h.reshape(pairs * own, *h.shape[2:]) for h in halves], axis=0)
-
     def other_core(value):
         return lax.ppermute(value, "col", [(c, c ^ 1) for c in range(n_col)])
 
@@ -299,7 +301,8 @@
         down = step(opposite[middle:], -1)
         nxt = jnp.concatenate([nxt[:middle] + up, nxt[middle:]], axis=0)
         prev = jnp.concatenate([prev[:middle], prev[middle:] + down], axis=0)
-        return [piece_at(0), step(nxt, 1), step(prev, -1)]
+        kept_piece = piece_at(0)
+        return [kept_piece, step(nxt, 1), step(prev, -1)]
 
     half = pairs * own
     update = inner(split_rows(slab), top_slab)
@@ -307,8 +310,7 @@
     updates = (update[half:] + update_got).reshape(pairs, own, TOP)
     updates = relayed_over_pairs(updates)
 
-    ordered = rows_at(arrived, split_rows(place_order[0]))
-    dist = sq_norms(ordered)[:, None] + top_norms[None, :] - 2.0 * inner(ordered, top_feats)
+    dist = own_norms[:, None] + top_norms[None, :] - 2.0 * inner(ordered, top_feats)
     dist_got = other_core(dist[:half])
     dists = (dist[half:] + dist_got).reshape(pairs, own, TOP)
     dists = spread_over_pairs(dists)

time: 188 us -> 188 us (level)
  no operation moved by 1% of the time
where the time goes in v8:
time: 188 us; the launch traced here: 185 us
  waiting for transfers between devices  67.6 us (36%)
  starting transfers between devices  45.6 us (24%)
  Pallas kernels  39.2 us (21%)
  local copies, waits for them, and re-layouts  19.8 us (11%)
  other arithmetic  7.2 us (4%)
  matrix products  4.41 us (2%)
    all_to_all x5, waiting for transfers between devices, swap(): return lax.all_to_all(value, axis, split_axis=0, concat_axis=0, tiled=True)  66.7 us
    all_to_all x5, starting transfers between devices, swap(): return lax.all_to_all(value, axis, split_axis=0, concat_axis=0, tiled=True)  33.7 us
    pallas_call x1, Pallas kernels, factor(): pl.pallas_call(factor_kernel, out_shape=(jax.ShapeDtypeStruct((TOP, TOP),...  32.1 us
    ppermute x4, starting transfers between devices, step(): lax.ppermute(piece, 'col', [(c, (c // 2 + by) % pairs * 2 + c % 2) for c...  8.81 us
    pallas_call x1, Pallas kernels, solve(): pl.pallas_call(solve_kernel, out_shape=jax.ShapeDtypeStruct((parts[0].sha...  7.03 us
    gather x2, local copies, waits for them, and re-layouts, rows_at(): lax.gather(array, where[:, None], dims, (1, array.shape[1]), unique_indic...  4.73 us
    unnamed x39, local copies, waits for them, and re-layouts  4.39 us
  transfers between devices with their start and end apart: 15, of which 6 were waited for; matrix products, arithmetic and copies ran while one was open for 8% of the time, Pallas kernels for 17%

profile of v8, /device:TPU:2, one launch (start us, length us, event | category | flops | bytes accessed | tf_op | source)
XLA Modules:
  0.0 185.0 jit_solution(2900660294460684805)
XLA Ops:
  0.0 0.8 pad_clamp_fusion.1
  0.8 0.7 fusion.40
  1.5 0.2 copy.16
  1.7 2.0 %gather_fusion = bf16[512,768]{1,0:T(8,128)(2,1)S(1)} fusion(bf16[512,768]{1,0:T(8,128)(2,1)S(1)} %copy-done, s32[1024]{0:T(1024)S(1)} %pad_clamp_fusion.1), kind=kCustom, calls=%fused_computation | custom fusion | bytes 1574912 | tf_op jit(solution)/shard_map/gather | solution.py:19
  3.7 1.1 fusion.3
  4.9 9.0 %all-to-all-start = ((bf16[32,16,1152]{2,1,0:T(8,128)(2,1)}), bf16[32,16,1152]{2,1,0:T(8,128)(2,1)S(1)}, u32[]{:S(2)}, u32[]{:S(2)}) async-start(bf16[32,16,1152]{2,1,0:T(8,128)(2,1)} %bitcast.3), calls=%async_computation | async-start | bytes 2359296 | tf_op jit(solution)/shard_map/all_to_all | solution.py:24
  13.9 16.5 %all-to-all-done = bf16[32,16,1152]{2,1,0:T(8,128)(2,1)S(1)} async-done(((bf16[32,16,1152]{2,1,0:T(8,128)(2,1)}), bf16[32,16,1152]{2,1,0:T(8,128)(2,1)S(1)}, u32[]{:S(2)}, u32[]{:S(2)}) %all-to-all-start) | async-done | bytes 1179680 | tf_op jit(solution)/shard_map/all_to_all | solution.py:24
  30.4 1.7 broadcast_in_dim.41
  32.2 6.2 %all-to-all-start.1 = ((bf16[32,32,1152]{2,1,0:T(8,128)(2,1)}), bf16[32,32,1152]{2,1,0:T(8,128)(2,1)S(1)}, u32[]{:S(2)}, u32[]{:S(2)}) async-start(bf16[32,32,1152]{2,1,0:T(8,128)(2,1)} %broadcast_in_dim.41), calls=%async_computation.1 | async-start | bytes 4718592 | tf_op jit(solution)/shard_map/all_to_all | solution.py:24
  39.1 27.9 %all-to-all-done.1 = bf16[32,32,1152]{2,1,0:T(8,128)(2,1)S(1)} async-done(((bf16[32,32,1152]{2,1,0:T(8,128)(2,1)}), bf16[32,32,1152]{2,1,0:T(8,128)(2,1)S(1)}, u32[]{:S(2)}, u32[]{:S(2)}) %all-to-all-start.1) | async-done | bytes 2359328 | tf_op jit(solution)/shard_map/all_to_all | solution.py:24
  67.4 0.4 fusion.6
  67.7 1.2 multiply_reduce_fusion
  69.1 1.0 copy-done.7
  70.1 0.6 fusion.4
  70.7 0.2 fusion.16
  71.0 0.7 all_to_all.27
  71.8 7.6 %all-to-all-start.2 = ((f32[8,2,2304]{2,1,0:T(2,128)}), f32[8,2,2304]{2,1,0:T(2,128)S(1)}, u32[]{:S(2)}, u32[]{:S(2)}) async-start(f32[8,2,2304]{2,1,0:T(2,128)} %all_to_all.27), calls=%async_computation.2 | async-start | bytes 294912 | tf_op jit(solution)/shard_map/all_to_all | solution.py:24
  79.4 9.2 %all-to-all-done.2 = f32[8,2,2304]{2,1,0:T(2,128)S(1)} async-done(((f32[8,2,2304]{2,1,0:T(2,128)}), f32[8,2,2304]{2,1,0:T(2,128)S(1)}, u32[]{:S(2)}, u32[]{:S(2)}) %all-to-all-start.2) | async-done | bytes 147488 | tf_op jit(solution)/shard_map/all_to_all | solution.py:24
  88.7 0.7 broadcast_in_dim.46
  89.4 3.4 %all-to-all-start.3 = ((f32[8,2,1152]{2,1,0:T(2,128)}), f32[8,2,1152]{2,1,0:T(2,128)S(1)}, u32[]{:S(2)}, u32[]{:S(2)}) async-start(f32[8,2,1152]{2,1,0:T(2,128)} %broadcast_in_dim.46), calls=%async_computation.3 | async-start | bytes 147456 | tf_op jit(solution)/shard_map/all_to_all | solution.py:24
  92.8 8.6 %all-to-all-done.3 = f32[8,2,1152]{2,1,0:T(2,128)S(1)} async-done(((f32[8,2,1152]{2,1,0:T(2,128)}), f32[8,2,1152]{2,1,0:T(2,128)S(1)}, u32[]{:S(2)}, u32[]{:S(2)}) %all-to-all-start.3) | async-done | bytes 73760 | tf_op jit(solution)/shard_map/all_to_all | solution.py:24
  101.5 1.1 broadcast_in_dim.47
  102.6 7.6 %all-to-all-start.4 = ((f32[32,8,1152]{2,1,0:T(8,128)}), f32[32,8,1152]{2,1,0:T(8,128)}, u32[]{:S(2)}, u32[]{:S(2)}) async-start(f32[32,8,1152]{2,1,0:T(8,128)} %broadcast_in_dim.47), calls=%async_computation.4 | async-start | bytes 2359296 | tf_op jit(solution)/shard_map/all_to_all | solution.py:24
  110.1 0.5 broadcast.272
  110.7 0.7 reduce.15
  111.6 0.7 constant_dynamic-slice_fusion.6
  112.4 2.7 %gather_fusion.1 = bf16[512,768]{1,0:T(8,128)(2,1)} fusion(bf16[512,768]{1,0:T(8,128)(2,1)S(1)} %slice.210, s32[1024]{0:T(1024)S(1)} %pad_clamp_fusion), kind=kCustom, calls=%fused_computation.1 | custom fusion | bytes 1574912 | tf_op jit(solution)/shard_map/gather | solution.py:19
  115.1 1.4 fusion.7
  116.6 1.1 slice.221
  117.7 0.2 multiply_reduce_fusion.1
  117.9 0.5 copy-done.8
  118.4 1.0 multiply_subtract_fusion
  119.4 1.3 copy-done.5
  120.7 1.1 slice.218
  121.9 4.4 %all-to-all-done.4.mine_ref = f32[32,8,1152]{2,1,0:T(8,128)} async-done(((f32[32,8,1152]{2,1,0:T(8,128)}), f32[32,8,1152]{2,1,0:T(8,128)}, u32[]{:S(2)}, u32[]{:S(2)}) %all-to-all-start.4) | async-done | bytes 1179680 | tf_op jit(solution)/shard_map/all_to_all | solution.py:24
  126.3 1.5 slice_add_fusion
  127.9 0.8 collective-permute-start.5
  128.7 3.4 %collective-permute-start.7 = (f32[32,1024]{1,0:T(8,128)S(1)}, f32[32,1024]{1,0:T(8,128)S(1)}, u32[]{:S(2)}, u32[]{:S(2)}) collective-permute-start(f32[32,1024]{1,0:T(8,128)S(1)} %get-tuple-element.17), channel_id=1, source_target_pairs={{0,6},{1,7},{2,0},{3,1},{4,2},{5,3},{6,4},{7,5},{8,14},{9,15},{10,... | collective-permute-start | bytes 393224 | tf_op jit(solution)/shard_map/ppermute | solution.py:293
  132.1 1.4 slice_add_fusion.1
  133.5 0.8 dynamic-slice_bitcast_fusion.1
  134.3 3.1 %collective-permute-start.2 = (f32[64,1024]{1,0:T(8,128)S(1)}, f32[64,1024]{1,0:T(8,128)S(1)}, u32[]{:S(2)}, u32[]{:S(2)}) collective-permute-start(f32[64,1024]{1,0:T(8,128)S(1)} %get-tuple-element.22), channel_id=1, source_target_pairs={{0,4},{1,5},{2,6},{3,7},{4,0},{5,1},{6,2},{7,3},{8,12},{9,13},{10,... | collective-permute-start | bytes 786440 | tf_op jit(solution)/shard_map/ppermute | solution.py:288
  137.4 0.9 collective-permute-done.5
  138.4 3.1 %collective-permute-start.6 = (f32[64,1024]{1,0:T(8,128)S(1)}, f32[64,1024]{1,0:T(8,128)S(1)}, u32[]{:S(2)}, u32[]{:S(2)}) collective-permute-start(f32[64,1024]{1,0:T(8,128)S(1)} %pad_maximum_fusion), channel_id=1, source_target_pairs={{0,2},{1,3},{2,4},{3,5},{4,6},{5,7},{6,0},{7,1},{8,10},{9,11},{10,... | collective-permute-start | bytes 786440 | tf_op jit(solution)/shard_map/ppermute | solution.py:293
  141.6 1.5 collective-permute-start.8
  143.1 1.7 dynamic-slice_bitcast_fusion.u0_ref
  144.8 32.1 %shard_map.55 = (f32[1024,1024]{1,0:T(8,128)}, f32[1024,128]{1,0:T(8,128)}) custom-call(s32[1]{0:T(128)} %bitcast.27.core_ref, f32[32,8,1152]{2,1,0:T(8,128)} %all-to-all-done.4.mine_ref, f32[32,8,1152]{2,1,0:T(8,128)} %collective-permute-done.9.other_ref), custom_call_target="tpu_custom_call" | custom-call | tf_op jit(solution)/shard_map/pallas_call | solution.py:192
  177.0 0.6 copy-done.11
  178.0 7.0 %shard_map.56 = f32[64,1024]{1,0:T(8,128)} custom-call(s32[1]{0:T(128)} %bitcast.first_ref, f32[64,1024]{1,0:T(8,128)} %get-tuple-element.24.d0_ref, f32[64,1024]{1,0:T(8,128)} %copy-done.13, f32[64,1024]{1,0:T(8,128)} %copy-done.12, f32[64,1024]{1,0:T(8,128)} %copy-done.11, f32[64,1024]{1,0:T(8,128)} %dynamic-slice_bitcast_fusion.u0_ref, ...), custom_call_target="tpu_custom_call" | custom-call | tf_op jit(solution)/shard_map/pallas_call | solution.py:202
  (87 shorter events, 1.9 us)
Async XLA Ops:
  0.0 1.7 copy-start
  1.7 2.0 %copy-start.9 = (bf16[512,256]{1,0:T(8,128)(2,1)S(1)}, bf16[512,256]{1,0:T(8,128)(2,1)}, u32[]{:S(2)}) copy-start(bf16[512,256]{1,0:T(8,128)(2,1)} %param.6) | copy-start | bytes 786436
  4.9 25.5 %all-to-all-start = ((bf16[32,16,1152]{2,1,0:T(8,128)(2,1)}), bf16[32,16,1152]{2,1,0:T(8,128)(2,1)S(1)}, u32[]{:S(2)}, u32[]{:S(2)}) async-start(bf16[32,16,1152]{2,1,0:T(8,128)(2,1)} %bitcast.3), calls=%async_computation | async-start | bytes 2359296 | tf_op jit(solution)/shard_map/all_to_all | solution.py:24
  30.4 1.8 copy-start.2
  32.2 34.8 %all-to-all-start.1 = ((bf16[32,32,1152]{2,1,0:T(8,128)(2,1)}), bf16[32,32,1152]{2,1,0:T(8,128)(2,1)S(1)}, u32[]{:S(2)}, u32[]{:S(2)}) async-start(bf16[32,32,1152]{2,1,0:T(8,128)(2,1)} %broadcast_in_dim.41), calls=%async_computation.1 | async-start | bytes 4718592 | tf_op jit(solution)/shard_map/all_to_all | solution.py:24
  68.9 1.2 copy-start.7
  71.8 16.8 %all-to-all-start.2 = ((f32[8,2,2304]{2,1,0:T(2,128)}), f32[8,2,2304]{2,1,0:T(2,128)S(1)}, u32[]{:S(2)}, u32[]{:S(2)}) async-start(f32[8,2,2304]{2,1,0:T(2,128)} %all_to_all.27), calls=%async_computation.2 | async-start | bytes 294912 | tf_op jit(solution)/shard_map/all_to_all | solution.py:24
  88.7 22.0 %copy-start.16 = (s32[1,512]{1,0:T(1,128)S(1)}, s32[1,512]{1,0:T(1,128)}, u32[]{:S(2)}) copy-start(s32[1,512]{1,0:T(1,128)} %param.8) | copy-start | bytes 6148
  89.4 12.0 %all-to-all-start.3 = ((f32[8,2,1152]{2,1,0:T(2,128)}), f32[8,2,1152]{2,1,0:T(2,128)S(1)}, u32[]{:S(2)}, u32[]{:S(2)}) async-start(f32[8,2,1152]{2,1,0:T(2,128)} %broadcast_in_dim.46), calls=%async_computation.3 | async-start | bytes 147456 | tf_op jit(solution)/shard_map/all_to_all | solution.py:24
  101.5 10.9 %copy-start.3 = (bf16[32,16,1152]{2,1,0:T(8,128)(2,1)S(1)}, bf16[32,16,1152]{2,1,0:T(8,128)(2,1)}, u32[]{:S(2)}) copy-start(bf16[32,16,1152]{2,1,0:T(8,128)(2,1)} %copy-done.2) | copy-start | bytes 3538948
  102.6 23.7 %all-to-all-start.4 = ((f32[32,8,1152]{2,1,0:T(8,128)}), f32[32,8,1152]{2,1,0:T(8,128)}, u32[]{:S(2)}, u32[]{:S(2)}) async-start(f32[32,8,1152]{2,1,0:T(8,128)} %broadcast_in_dim.47), calls=%async_computation.4 | async-start | bytes 2359296 | tf_op jit(solution)/shard_map/all_to_all | solution.py:24
  112.4 2.7 %copy-start.10 = (bf16[4,1,64,256]{3,2,1,0:T(8,128)(2,1)S(1)}, bf16[4,1,64,256]{3,2,1,0:T(8,128)(2,1)}, u32[]{:S(2)}) copy-start(bf16[4,1,64,256]{3,2,1,0:T(8,128)(2,1)} %get-tuple-element.27) | copy-start | bytes 393220
  115.1 2.5 %copy-start.4 = (bf16[512,768]{1,0:T(8,128)(2,1)S(1)}, bf16[512,768]{1,0:T(8,128)(2,1)}, u32[]{:S(2)}) copy-start(bf16[512,768]{1,0:T(8,128)(2,1)} %gather_fusion.1) | copy-start | bytes 2359300
  116.6 1.8 copy-start.8
  117.7 8.7 %collective-permute-start.4 = (f32[256,1024]{1,0:T(8,128)}, f32[256,1024]{1,0:T(8,128)}, u32[]{:S(2)}, u32[]{:S(2)}) collective-permute-start(f32[256,1024]{1,0:T(8,128)} %slice.221), channel_id=1, source_target_pairs={{0,1},{1,0},{2,3},{3,2},{4,5},{5,4},{6,7},{7,6},{8,9},{9,8},{10,11... | collective-permute-start | bytes 3145736 | tf_op jit(solution)/shard_map/ppermute | solution.py:281
  119.4 1.3 copy-start.5
  121.8 10.3 %collective-permute-start = (f32[256,1024]{1,0:T(8,128)}, f32[256,1024]{1,0:T(8,128)}, u32[]{:S(2)}, u32[]{:S(2)}) collective-permute-start(f32[256,1024]{1,0:T(8,128)} %slice.218), channel_id=1, source_target_pairs={{0,1},{1,0},{2,3},{3,2},{4,5},{5,4},{6,7},{7,6},{8,9},{9,8},{10,11... | collective-permute-start | bytes 3145736 | tf_op jit(solution)/shard_map/ppermute | solution.py:281
  126.3 5.8 %copy-start.6 = (f32[512,1024]{1,0:T(8,128)S(1)}, f32[512,1024]{1,0:T(8,128)}, u32[]{:S(2)}) copy-start(f32[512,1024]{1,0:T(8,128)} %copy-done.5) | copy-start | bytes 6291460
  126.3 15.3 %collective-permute-start.9 = (f32[32,8,1152]{2,1,0:T(8,128)}, f32[32,8,1152]{2,1,0:T(8,128)}, u32[]{:S(2)}, u32[]{:S(2)}) collective-permute-start(f32[32,8,1152]{2,1,0:T(8,128)} %all-to-all-done.4.mine_ref), channel_id=1, source_target_pairs={{0,1},{1,0},{2,3},{3,2},{4,5},{5,4},{6,7},{7,6},{8,9},{9,8},{10,11... | collective-permute-start | bytes 3538952 | tf_op jit(solution)/shard_map/ppermute | solution.py:322
  127.8 10.5 %copy-start.1 = (f32[256,1024]{1,0:T(8,128)}, f32[256,1024]{1,0:T(8,128)S(1)}, u32[]{:S(2)}) copy-start(f32[256,1024]{1,0:T(8,128)S(1)} %slice_add_fusion) | copy-start | bytes 3145732
  127.9 10.4 %collective-permute-start.5 = (f32[32,1024]{1,0:T(8,128)S(1)}, f32[32,1024]{1,0:T(8,128)S(1)}, u32[]{:S(2)}, u32[]{:S(2)}) collective-permute-start(f32[32,1024]{1,0:T(8,128)S(1)} %get-tuple-element.16), channel_id=1, source_target_pairs={{0,2},{1,3},{2,4},{3,5},{4,6},{5,7},{6,0},{7,1},{8,10},{9,11},{10,... | collective-permute-start | bytes 393224 | tf_op jit(solution)/shard_map/ppermute | solution.py:293
  128.7 9.6 %collective-permute-start.7 = (f32[32,1024]{1,0:T(8,128)S(1)}, f32[32,1024]{1,0:T(8,128)S(1)}, u32[]{:S(2)}, u32[]{:S(2)}) collective-permute-start(f32[32,1024]{1,0:T(8,128)S(1)} %get-tuple-element.17), channel_id=1, source_target_pairs={{0,6},{1,7},{2,0},{3,1},{4,2},{5,3},{6,4},{7,5},{8,14},{9,15},{10,... | collective-permute-start | bytes 393224 | tf_op jit(solution)/shard_map/ppermute | solution.py:293
  134.3 42.6 %collective-permute-start.3 = (f32[64,1024]{1,0:T(8,128)S(1)}, f32[64,1024]{1,0:T(8,128)S(1)}, u32[]{:S(2)}, u32[]{:S(2)}) collective-permute-start(f32[64,1024]{1,0:T(8,128)S(1)} %get-tuple-element.21), channel_id=1, source_target_pairs={{0,6},{1,7},{2,0},{3,1},{4,2},{5,3},{6,4},{7,5},{8,14},{9,15},{10,... | collective-permute-start | bytes 786440 | tf_op jit(solution)/shard_map/ppermute | solution.py:288
  134.3 42.6 %collective-permute-start.2 = (f32[64,1024]{1,0:T(8,128)S(1)}, f32[64,1024]{1,0:T(8,128)S(1)}, u32[]{:S(2)}, u32[]{:S(2)}) collective-permute-start(f32[64,1024]{1,0:T(8,128)S(1)} %get-tuple-element.22), channel_id=1, source_target_pairs={{0,4},{1,5},{2,6},{3,7},{4,0},{5,1},{6,2},{7,3},{8,12},{9,13},{10,... | collective-permute-start | bytes 786440 | tf_op jit(solution)/shard_map/ppermute | solution.py:288
  138.4 38.6 %collective-permute-start.1 = (f32[64,1024]{1,0:T(8,128)S(1)}, f32[64,1024]{1,0:T(8,128)S(1)}, u32[]{:S(2)}, u32[]{:S(2)}) collective-permute-start(f32[64,1024]{1,0:T(8,128)S(1)} %get-tuple-element.23), channel_id=1, source_target_pairs={{0,2},{1,3},{2,4},{3,5},{4,6},{5,7},{6,0},{7,1},{8,10},{9,11},{10,... | collective-permute-start | bytes 786440 | tf_op jit(solution)/shard_map/ppermute | solution.py:288
  138.4 38.5 %collective-permute-start.6 = (f32[64,1024]{1,0:T(8,128)S(1)}, f32[64,1024]{1,0:T(8,128)S(1)}, u32[]{:S(2)}, u32[]{:S(2)}) collective-permute-start(f32[64,1024]{1,0:T(8,128)S(1)} %pad_maximum_fusion), channel_id=1, source_target_pairs={{0,2},{1,3},{2,4},{3,5},{4,6},{5,7},{6,0},{7,1},{8,10},{9,11},{10,... | collective-permute-start | bytes 786440 | tf_op jit(solution)/shard_map/ppermute | solution.py:293
  141.6 35.3 %collective-permute-start.8 = (f32[64,1024]{1,0:T(8,128)S(1)}, f32[64,1024]{1,0:T(8,128)S(1)}, u32[]{:S(2)}, u32[]{:S(2)}) collective-permute-start(f32[64,1024]{1,0:T(8,128)S(1)} %pad_maximum_fusion.1), channel_id=1, source_target_pairs={{0,6},{1,7},{2,0},{3,1},{4,2},{5,3},{6,4},{7,5},{8,14},{9,15},{10,... | collective-permute-start | bytes 786440 | tf_op jit(solution)/shard_map/ppermute | solution.py:293
  176.9 0.7 copy-start.11
  176.9 0.8 copy-start.12
  176.9 0.9 copy-start.13
  176.9 1.0 copy-start.14
  177.0 1.0 copy-start.15

commit v9 on v7

--- a/solution.py
+++ b/solution.py
@@ -299,7 +299,8 @@
         down = step(opposite[middle:], -1)
         nxt = jnp.concatenate([nxt[:middle] + up, nxt[middle:]], axis=0)
         prev = jnp.concatenate([prev[:middle], prev[middle:] + down], axis=0)
-        return [piece_at(0), step(nxt, 1), step(prev, -1)]
+        kept_piece = piece_at(0)
+        return [kept_piece, step(nxt, 1), step(prev, -1)]
 
     half = pairs * own
     update = inner(split_rows(slab), top_slab)
@@ -307,7 +308,8 @@
     updates = (update[half:] + update_got).reshape(pairs, own, TOP)
     updates = relayed_over_pairs(updates)
 
-    ordered = rows_at(arrived, split_rows(place_order[0]))
+    own_places = split_rows(place_order[0])
+    ordered = rows_at(arrived, own_places)
     dist = sq_norms(ordered)[:, None] + top_norms[None, :] - 2.0 * inner(ordered, top_feats)
     dist_got = other_core(dist[:half])
     dists = (dist[half:] + dist_got).reshape(pairs, own, TOP)

time: 188 us -> 188 us (level)
  no operation moved by 1% of the time
where the time goes in v9:
time: 188 us; the launch traced here: 185 us
  waiting for transfers between devices  67.6 us (36%)
  starting transfers between devices  45.6 us (24%)
  Pallas kernels  39.2 us (21%)
  local copies, waits for them, and re-layouts  19.8 us (11%)
  other arithmetic  7.2 us (4%)
  matrix products  4.41 us (2%)
    all_to_all x5, waiting for transfers between devices, swap(): return lax.all_to_all(value, axis, split_axis=0, concat_axis=0, tiled=True)  66.7 us
    all_to_all x5, starting transfers between devices, swap(): return lax.all_to_all(value, axis, split_axis=0, concat_axis=0, tiled=True)  33.7 us
    pallas_call x1, Pallas kernels, factor(): pl.pallas_call(factor_kernel, out_shape=(jax.ShapeDtypeStruct((TOP, TOP),...  32.1 us
    ppermute x4, starting transfers between devices, step(): lax.ppermute(piece, 'col', [(c, (c // 2 + by) % pairs * 2 + c % 2) for c...  8.81 us
    pallas_call x1, Pallas kernels, solve(): pl.pallas_call(solve_kernel, out_shape=jax.ShapeDtypeStruct((parts[0].sha...  7.03 us
    gather x2, local copies, waits for them, and re-layouts, rows_at(): lax.gather(array, where[:, None], dims, (1, array.shape[1]), unique_indic...  4.73 us
    unnamed x39, local copies, waits for them, and re-layouts  4.39 us
  transfers between devices with their start and end apart: 15, of which 6 were waited for; matrix products, arithmetic and copies ran while one was open for 8% of the time, Pallas kernels for 17%

profile of v9, /device:TPU:2, one launch (start us, length us, event | category | flops | bytes accessed | tf_op | source)
XLA Modules:
  0.0 185.0 jit_solution(2900660294460684805)
XLA Ops:
  0.0 0.8 pad_clamp_fusion.1
  0.8 0.7 fusion.40
  1.5 0.2 copy.16
  1.7 2.0 %gather_fusion = bf16[512,768]{1,0:T(8,128)(2,1)S(1)} fusion(bf16[512,768]{1,0:T(8,128)(2,1)S(1)} %copy-done, s32[1024]{0:T(1024)S(1)} %pad_clamp_fusion.1), kind=kCustom, calls=%fused_computation | custom fusion | bytes 1574912 | tf_op jit(solution)/shard_map/gather | solution.py:19
  3.7 1.1 fusion.3
  4.9 9.0 %all-to-all-start = ((bf16[32,16,1152]{2,1,0:T(8,128)(2,1)}), bf16[32,16,1152]{2,1,0:T(8,128)(2,1)S(1)}, u32[]{:S(2)}, u32[]{:S(2)}) async-start(bf16[32,16,1152]{2,1,0:T(8,128)(2,1)} %bitcast.3), calls=%async_computation | async-start | bytes 2359296 | tf_op jit(solution)/shard_map/all_to_all | solution.py:24
  13.9 16.5 %all-to-all-done = bf16[32,16,1152]{2,1,0:T(8,128)(2,1)S(1)} async-done(((bf16[32,16,1152]{2,1,0:T(8,128)(2,1)}), bf16[32,16,1152]{2,1,0:T(8,128)(2,1)S(1)}, u32[]{:S(2)}, u32[]{:S(2)}) %all-to-all-start) | async-done | bytes 1179680 | tf_op jit(solution)/shard_map/all_to_all | solution.py:24
  30.4 1.7 broadcast_in_dim.41
  32.2 6.2 %all-to-all-start.1 = ((bf16[32,32,1152]{2,1,0:T(8,128)(2,1)}), bf16[32,32,1152]{2,1,0:T(8,128)(2,1)S(1)}, u32[]{:S(2)}, u32[]{:S(2)}) async-start(bf16[32,32,1152]{2,1,0:T(8,128)(2,1)} %broadcast_in_dim.41), calls=%async_computation.1 | async-start | bytes 4718592 | tf_op jit(solution)/shard_map/all_to_all | solution.py:24
  39.1 27.9 %all-to-all-done.1 = bf16[32,32,1152]{2,1,0:T(8,128)(2,1)S(1)} async-done(((bf16[32,32,1152]{2,1,0:T(8,128)(2,1)}), bf16[32,32,1152]{2,1,0:T(8,128)(2,1)S(1)}, u32[]{:S(2)}, u32[]{:S(2)}) %all-to-all-start.1) | async-done | bytes 2359328 | tf_op jit(solution)/shard_map/all_to_all | solution.py:24
  67.4 0.4 fusion.6
  67.7 1.2 multiply_reduce_fusion
  69.1 1.0 copy-done.7
  70.1 0.6 fusion.4
  70.7 0.2 fusion.16
  71.0 0.7 all_to_all.27
  71.8 7.6 %all-to-all-start.2 = ((f32[8,2,2304]{2,1,0:T(2,128)}), f32[8,2,2304]{2,1,0:T(2,128)S(1)}, u32[]{:S(2)}, u32[]{:S(2)}) async-start(f32[8,2,2304]{2,1,0:T(2,128)} %all_to_all.27), calls=%async_computation.2 | async-start | bytes 294912 | tf_op jit(solution)/shard_map/all_to_all | solution.py:24
  79.4 9.2 %all-to-all-done.2 = f32[8,2,2304]{2,1,0:T(2,128)S(1)} async-done(((f32[8,2,2304]{2,1,0:T(2,128)}), f32[8,2,2304]{2,1,0:T(2,128)S(1)}, u32[]{:S(2)}, u32[]{:S(2)}) %all-to-all-start.2) | async-done | bytes 147488 | tf_op jit(solution)/shard_map/all_to_all | solution.py:24
  88.7 0.7 broadcast_in_dim.46
  89.4 3.4 %all-to-all-start.3 = ((f32[8,2,1152]{2,1,0:T(2,128)}), f32[8,2,1152]{2,1,0:T(2,128)S(1)}, u32[]{:S(2)}, u32[]{:S(2)}) async-start(f32[8,2,1152]{2,1,0:T(2,128)} %broadcast_in_dim.46), calls=%async_computation.3 | async-start | bytes 147456 | tf_op jit(solution)/shard_map/all_to_all | solution.py:24
  92.8 8.6 %all-to-all-done.3 = f32[8,2,1152]{2,1,0:T(2,128)S(1)} async-done(((f32[8,2,1152]{2,1,0:T(2,128)}), f32[8,2,1152]{2,1,0:T(2,128)S(1)}, u32[]{:S(2)}, u32[]{:S(2)}) %all-to-all-start.3) | async-done | bytes 73760 | tf_op jit(solution)/shard_map/all_to_all | solution.py:24
  101.5 1.1 broadcast_in_dim.47
  102.6 7.6 %all-to-all-start.4 = ((f32[32,8,1152]{2,1,0:T(8,128)}), f32[32,8,1152]{2,1,0:T(8,128)}, u32[]{:S(2)}, u32[]{:S(2)}) async-start(f32[32,8,1152]{2,1,0:T(8,128)} %broadcast_in_dim.47), calls=%async_computation.4 | async-start | bytes 2359296 | tf_op jit(solution)/shard_map/all_to_all | solution.py:24
  110.1 0.5 broadcast.272
  110.7 0.7 reduce.15
  111.6 0.7 constant_dynamic-slice_fusion.6
  112.4 2.7 %gather_fusion.1 = bf16[512,768]{1,0:T(8,128)(2,1)} fusion(bf16[512,768]{1,0:T(8,128)(2,1)S(1)} %slice.210, s32[1024]{0:T(1024)S(1)} %pad_clamp_fusion), kind=kCustom, calls=%fused_computation.1 | custom fusion | bytes 1574912 | tf_op jit(solution)/shard_map/gather | solution.py:19
  115.1 1.4 fusion.7
  116.6 1.1 slice.221
  117.7 0.2 multiply_reduce_fusion.1
  117.9 0.5 copy-done.8
  118.4 1.0 multiply_subtract_fusion
  119.4 1.3 copy-done.5
  120.7 1.1 slice.218
  121.9 4.4 %all-to-all-done.4.mine_ref = f32[32,8,1152]{2,1,0:T(8,128)} async-done(((f32[32,8,1152]{2,1,0:T(8,128)}), f32[32,8,1152]{2,1,0:T(8,128)}, u32[]{:S(2)}, u32[]{:S(2)}) %all-to-all-start.4) | async-done | bytes 1179680 | tf_op jit(solution)/shard_map/all_to_all | solution.py:24
  126.3 1.5 slice_add_fusion
  127.9 0.8 collective-permute-start.5
  128.7 3.4 %collective-permute-start.7 = (f32[32,1024]{1,0:T(8,128)S(1)}, f32[32,1024]{1,0:T(8,128)S(1)}, u32[]{:S(2)}, u32[]{:S(2)}) collective-permute-start(f32[32,1024]{1,0:T(8,128)S(1)} %get-tuple-element.17), channel_id=1, source_target_pairs={{0,6},{1,7},{2,0},{3,1},{4,2},{5,3},{6,4},{7,5},{8,14},{9,15},{10,... | collective-permute-start | bytes 393224 | tf_op jit(solution)/shard_map/ppermute | solution.py:291
  132.1 1.4 slice_add_fusion.1
  133.5 0.8 dynamic-slice_bitcast_fusion.1
  134.3 3.1 %collective-permute-start.2 = (f32[64,1024]{1,0:T(8,128)S(1)}, f32[64,1024]{1,0:T(8,128)S(1)}, u32[]{:S(2)}, u32[]{:S(2)}) collective-permute-start(f32[64,1024]{1,0:T(8,128)S(1)} %get-tuple-element.22), channel_id=1, source_target_pairs={{0,4},{1,5},{2,6},{3,7},{4,0},{5,1},{6,2},{7,3},{8,12},{9,13},{10,... | collective-permute-start | bytes 786440 | tf_op jit(solution)/shard_map/ppermute | solution.py:286
  137.4 0.9 collective-permute-done.5
  138.4 3.1 %collective-permute-start.6 = (f32[64,1024]{1,0:T(8,128)S(1)}, f32[64,1024]{1,0:T(8,128)S(1)}, u32[]{:S(2)}, u32[]{:S(2)}) collective-permute-start(f32[64,1024]{1,0:T(8,128)S(1)} %pad_maximum_fusion), channel_id=1, source_target_pairs={{0,2},{1,3},{2,4},{3,5},{4,6},{5,7},{6,0},{7,1},{8,10},{9,11},{10,... | collective-permute-start | bytes 786440 | tf_op jit(solution)/shard_map/ppermute | solution.py:291
  141.6 1.5 collective-permute-start.8
  143.1 1.7 dynamic-slice_bitcast_fusion.u0_ref
  144.8 32.1 %shard_map.55 = (f32[1024,1024]{1,0:T(8,128)}, f32[1024,128]{1,0:T(8,128)}) custom-call(s32[1]{0:T(128)} %bitcast.27.core_ref, f32[32,8,1152]{2,1,0:T(8,128)} %all-to-all-done.4.mine_ref, f32[32,8,1152]{2,1,0:T(8,128)} %collective-permute-done.9.other_ref), custom_call_target="tpu_custom_call" | custom-call | tf_op jit(solution)/shard_map/pallas_call | solution.py:192
  177.0 0.6 copy-done.11
  178.0 7.0 %shard_map.56 = f32[64,1024]{1,0:T(8,128)} custom-call(s32[1]{0:T(128)} %bitcast.first_ref, f32[64,1024]{1,0:T(8,128)} %get-tuple-element.24.d0_ref, f32[64,1024]{1,0:T(8,128)} %copy-done.13, f32[64,1024]{1,0:T(8,128)} %copy-done.12, f32[64,1024]{1,0:T(8,128)} %copy-done.11, f32[64,1024]{1,0:T(8,128)} %dynamic-slice_bitcast_fusion.u0_ref, ...), custom_call_target="tpu_custom_call" | custom-call | tf_op jit(solution)/shard_map/pallas_call | solution.py:202
  (87 shorter events, 1.9 us)
Async XLA Ops:
  0.0 1.7 copy-start
  1.7 2.0 %copy-start.9 = (bf16[512,256]{1,0:T(8,128)(2,1)S(1)}, bf16[512,256]{1,0:T(8,128)(2,1)}, u32[]{:S(2)}) copy-start(bf16[512,256]{1,0:T(8,128)(2,1)} %param.6) | copy-start | bytes 786436
  4.9 25.5 %all-to-all-start = ((bf16[32,16,1152]{2,1,0:T(8,128)(2,1)}), bf16[32,16,1152]{2,1,0:T(8,128)(2,1)S(1)}, u32[]{:S(2)}, u32[]{:S(2)}) async-start(bf16[32,16,1152]{2,1,0:T(8,128)(2,1)} %bitcast.3), calls=%async_computation | async-start | bytes 2359296 | tf_op jit(solution)/shard_map/all_to_all | solution.py:24
  30.4 1.8 copy-start.2
  32.2 34.8 %all-to-all-start.1 = ((bf16[32,32,1152]{2,1,0:T(8,128)(2,1)}), bf16[32,32,1152]{2,1,0:T(8,128)(2,1)S(1)}, u32[]{:S(2)}, u32[]{:S(2)}) async-start(bf16[32,32,1152]{2,1,0:T(8,128)(2,1)} %broadcast_in_dim.41), calls=%async_computation.1 | async-start | bytes 4718592 | tf_op jit(solution)/shard_map/all_to_all | solution.py:24
  68.9 1.2 copy-start.7
  71.8 16.8 %all-to-all-start.2 = ((f32[8,2,2304]{2,1,0:T(2,128)}), f32[8,2,2304]{2,1,0:T(2,128)S(1)}, u32[]{:S(2)}, u32[]{:S(2)}) async-start(f32[8,2,2304]{2,1,0:T(2,128)} %all_to_all.27), calls=%async_computation.2 | async-start | bytes 294912 | tf_op jit(solution)/shard_map/all_to_all | solution.py:24
  88.7 22.0 %copy-start.16 = (s32[1,512]{1,0:T(1,128)S(1)}, s32[1,512]{1,0:T(1,128)}, u32[]{:S(2)}) copy-start(s32[1,512]{1,0:T(1,128)} %param.8) | copy-start | bytes 6148
  89.4 12.0 %all-to-all-start.3 = ((f32[8,2,1152]{2,1,0:T(2,128)}), f32[8,2,1152]{2,1,0:T(2,128)S(1)}, u32[]{:S(2)}, u32[]{:S(2)}) async-start(f32[8,2,1152]{2,1,0:T(2,128)} %broadcast_in_dim.46), calls=%async_computation.3 | async-start | bytes 147456 | tf_op jit(solution)/shard_map/all_to_all | solution.py:24
  101.5 10.9 %copy-start.3 = (bf16[32,16,1152]{2,1,0:T(8,128)(2,1)S(1)}, bf16[32,16,1152]{2,1,0:T(8,128)(2,1)}, u32[]{:S(2)}) copy-start(bf16[32,16,1152]{2,1,0:T(8,128)(2,1)} %copy-done.2) | copy-start | bytes 3538948
  102.6 23.7 %all-to-all-start.4 = ((f32[32,8,1152]{2,1,0:T(8,128)}), f32[32,8,1152]{2,1,0:T(8,128)}, u32[]{:S(2)}, u32[]{:S(2)}) async-start(f32[32,8,1152]{2,1,0:T(8,128)} %broadcast_in_dim.47), calls=%async_computation.4 | async-start | bytes 2359296 | tf_op jit(solution)/shard_map/all_to_all | solution.py:24
  112.4 2.7 %copy-start.10 = (bf16[4,1,64,256]{3,2,1,0:T(8,128)(2,1)S(1)}, bf16[4,1,64,256]{3,2,1,0:T(8,128)(2,1)}, u32[]{:S(2)}) copy-start(bf16[4,1,64,256]{3,2,1,0:T(8,128)(2,1)} %get-tuple-element.27) | copy-start | bytes 393220
  115.1 2.5 %copy-start.4 = (bf16[512,768]{1,0:T(8,128)(2,1)S(1)}, bf16[512,768]{1,0:T(8,128)(2,1)}, u32[]{:S(2)}) copy-start(bf16[512,768]{1,0:T(8,128)(2,1)} %gather_fusion.1) | copy-start | bytes 2359300
  116.6 1.8 copy-start.8
  117.7 8.7 %collective-permute-start.4 = (f32[256,1024]{1,0:T(8,128)}, f32[256,1024]{1,0:T(8,128)}, u32[]{:S(2)}, u32[]{:S(2)}) collective-permute-start(f32[256,1024]{1,0:T(8,128)} %slice.221), channel_id=1, source_target_pairs={{0,1},{1,0},{2,3},{3,2},{4,5},{5,4},{6,7},{7,6},{8,9},{9,8},{10,11... | collective-permute-start | bytes 3145736 | tf_op jit(solution)/shard_map/ppermute | solution.py:279
  119.4 1.3 copy-start.5
  121.8 10.3 %collective-permute-start = (f32[256,1024]{1,0:T(8,128)}, f32[256,1024]{1,0:T(8,128)}, u32[]{:S(2)}, u32[]{:S(2)}) collective-permute-start(f32[256,1024]{1,0:T(8,128)} %slice.218), channel_id=1, source_target_pairs={{0,1},{1,0},{2,3},{3,2},{4,5},{5,4},{6,7},{7,6},{8,9},{9,8},{10,11... | collective-permute-start | bytes 3145736 | tf_op jit(solution)/shard_map/ppermute | solution.py:279
  126.3 5.8 %copy-start.6 = (f32[512,1024]{1,0:T(8,128)S(1)}, f32[512,1024]{1,0:T(8,128)}, u32[]{:S(2)}) copy-start(f32[512,1024]{1,0:T(8,128)} %copy-done.5) | copy-start | bytes 6291460
  126.3 15.3 %collective-permute-start.9 = (f32[32,8,1152]{2,1,0:T(8,128)}, f32[32,8,1152]{2,1,0:T(8,128)}, u32[]{:S(2)}, u32[]{:S(2)}) collective-permute-start(f32[32,8,1152]{2,1,0:T(8,128)} %all-to-all-done.4.mine_ref), channel_id=1, source_target_pairs={{0,1},{1,0},{2,3},{3,2},{4,5},{5,4},{6,7},{7,6},{8,9},{9,8},{10,11... | collective-permute-start | bytes 3538952 | tf_op jit(solution)/shard_map/ppermute | solution.py:322
  127.8 10.5 %copy-start.1 = (f32[256,1024]{1,0:T(8,128)}, f32[256,1024]{1,0:T(8,128)S(1)}, u32[]{:S(2)}) copy-start(f32[256,1024]{1,0:T(8,128)S(1)} %slice_add_fusion) | copy-start | bytes 3145732
  127.9 10.4 %collective-permute-start.5 = (f32[32,1024]{1,0:T(8,128)S(1)}, f32[32,1024]{1,0:T(8,128)S(1)}, u32[]{:S(2)}, u32[]{:S(2)}) collective-permute-start(f32[32,1024]{1,0:T(8,128)S(1)} %get-tuple-element.16), channel_id=1, source_target_pairs={{0,2},{1,3},{2,4},{3,5},{4,6},{5,7},{6,0},{7,1},{8,10},{9,11},{10,... | collective-permute-start | bytes 393224 | tf_op jit(solution)/shard_map/ppermute | solution.py:291
  128.7 9.6 %collective-permute-start.7 = (f32[32,1024]{1,0:T(8,128)S(1)}, f32[32,1024]{1,0:T(8,128)S(1)}, u32[]{:S(2)}, u32[]{:S(2)}) collective-permute-start(f32[32,1024]{1,0:T(8,128)S(1)} %get-tuple-element.17), channel_id=1, source_target_pairs={{0,6},{1,7},{2,0},{3,1},{4,2},{5,3},{6,4},{7,5},{8,14},{9,15},{10,... | collective-permute-start | bytes 393224 | tf_op jit(solution)/shard_map/ppermute | solution.py:291
  134.3 42.6 %collective-permute-start.3 = (f32[64,1024]{1,0:T(8,128)S(1)}, f32[64,1024]{1,0:T(8,128)S(1)}, u32[]{:S(2)}, u32[]{:S(2)}) collective-permute-start(f32[64,1024]{1,0:T(8,128)S(1)} %get-tuple-element.21), channel_id=1, source_target_pairs={{0,6},{1,7},{2,0},{3,1},{4,2},{5,3},{6,4},{7,5},{8,14},{9,15},{10,... | collective-permute-start | bytes 786440 | tf_op jit(solution)/shard_map/ppermute | solution.py:286
  134.3 42.6 %collective-permute-start.2 = (f32[64,1024]{1,0:T(8,128)S(1)}, f32[64,1024]{1,0:T(8,128)S(1)}, u32[]{:S(2)}, u32[]{:S(2)}) collective-permute-start(f32[64,1024]{1,0:T(8,128)S(1)} %get-tuple-element.22), channel_id=1, source_target_pairs={{0,4},{1,5},{2,6},{3,7},{4,0},{5,1},{6,2},{7,3},{8,12},{9,13},{10,... | collective-permute-start | bytes 786440 | tf_op jit(solution)/shard_map/ppermute | solution.py:286
  138.4 38.6 %collective-permute-start.1 = (f32[64,1024]{1,0:T(8,128)S(1)}, f32[64,1024]{1,0:T(8,128)S(1)}, u32[]{:S(2)}, u32[]{:S(2)}) collective-permute-start(f32[64,1024]{1,0:T(8,128)S(1)} %get-tuple-element.23), channel_id=1, source_target_pairs={{0,2},{1,3},{2,4},{3,5},{4,6},{5,7},{6,0},{7,1},{8,10},{9,11},{10,... | collective-permute-start | bytes 786440 | tf_op jit(solution)/shard_map/ppermute | solution.py:286
  138.4 38.5 %collective-permute-start.6 = (f32[64,1024]{1,0:T(8,128)S(1)}, f32[64,1024]{1,0:T(8,128)S(1)}, u32[]{:S(2)}, u32[]{:S(2)}) collective-permute-start(f32[64,1024]{1,0:T(8,128)S(1)} %pad_maximum_fusion), channel_id=1, source_target_pairs={{0,2},{1,3},{2,4},{3,5},{4,6},{5,7},{6,0},{7,1},{8,10},{9,11},{10,... | collective-permute-start | bytes 786440 | tf_op jit(solution)/shard_map/ppermute | solution.py:291
  141.6 35.3 %collective-permute-start.8 = (f32[64,1024]{1,0:T(8,128)S(1)}, f32[64,1024]{1,0:T(8,128)S(1)}, u32[]{:S(2)}, u32[]{:S(2)}) collective-permute-start(f32[64,1024]{1,0:T(8,128)S(1)} %pad_maximum_fusion.1), channel_id=1, source_target_pairs={{0,6},{1,7},{2,0},{3,1},{4,2},{5,3},{6,4},{7,5},{8,14},{9,15},{10,... | collective-permute-start | bytes 786440 | tf_op jit(solution)/shard_map/ppermute | solution.py:291
  176.9 0.7 copy-start.11
  176.9 0.8 copy-start.12
  176.9 0.9 copy-start.13
  176.9 1.0 copy-start.14
  177.0 1.0 copy-start.15
